TPU v7x, 32 devices: a whole 2x2x4 slice. The times are simulated.
32 devices in a mesh: expert: 8 (over z, x), tensor: 4 (over y, core).
Axes of the slice: x: 2, y: 2, z: 4, core: 2. Of those that a mesh axis runs over, the one named last changes fastest.
Arguments:
- block_in: bfloat16 [2048, 2048], P('expert'), may hold values from -6 to 6
- attention_gain: bfloat16 [2048], P('expert'), may hold values from 0.5 to 1.5
- query_down: bfloat16 [2048, 1536], P('expert'), may hold values from -0.125 to 0.125
- query_gain: bfloat16 [1536], P('expert'), may hold values from 0.5 to 1.5
- query_up: bfloat16 [1536, 3072], P('expert', 'tensor'), may hold values from -0.15625 to 0.15625
- latent_down: bfloat16 [2048, 576], P('expert'), may hold values from -0.125 to 0.125
- latent_gain: bfloat16 [512], P('expert'), may hold values from 0.5 to 1.5
- latent_up: bfloat16 [512, 4096], P('expert', 'tensor'), may hold values from -0.25 to 0.25
- out_proj: bfloat16 [2048, 2048], P('tensor', 'expert'), may hold values from -0.5 to 0.5
- ffn_gain: bfloat16 [2048], P('expert'), may hold values from 0.5 to 1.5
- router: bfloat16 [2048, 64], P('expert'), may hold values from -0.125 to 0.125
- shared_gate: bfloat16 [2048, 2816], P('expert', 'tensor'), may hold values from -0.125 to 0.125
- shared_up: bfloat16 [2048, 2816], P('expert', 'tensor'), may hold values from -0.125 to 0.125
- shared_down: bfloat16 [2816, 2048], P('tensor', 'expert'), may hold values from -0.109375 to 0.109375
- expert_gate: bfloat16 [64, 2048, 1408], P('expert', None, 'tensor'), may hold values from -0.125 to 0.125
- expert_up: bfloat16 [64, 2048, 1408], P('expert', None, 'tensor'), may hold values from -0.125 to 0.125
- expert_down: bfloat16 [64, 1408, 2048], P('expert', 'tensor'), may hold values from -0.15625 to 0.15625
- doc_lengths: int32 [8, 3], P('expert'), may hold values from 1 to 128, 256 in all within a row
- routes: int32 [2048, 6], P('expert'), may hold values from 0 to 63, all different within a row; in each aligned block of 256 rows (0 to 255, 256 to 511, ...) at most 32 rows name the same one
- out_grad: bfloat16 [2048, 2048], P('expert'), may hold values from -6 to 6
Outputs:
- block_out: bfloat16 [2048, 2048], P('expert')
- input_grad: bfloat16 [2048, 2048], P('expert')
- grad_attention_gain: float32 [2048], P('expert')
- grad_query_down: float32 [2048, 1536], P('expert')
- grad_query_gain: float32 [1536], P('expert')
- grad_query_up: float32 [1536, 3072], P('expert', 'tensor')
- grad_latent_down: float32 [2048, 576], P('expert')
- grad_latent_gain: float32 [512], P('expert')
- grad_latent_up: float32 [512, 4096], P('expert', 'tensor')
- grad_out_proj: float32 [2048, 2048], P('tensor', 'expert')
- grad_ffn_gain: float32 [2048], P('expert')
- grad_router: float32 [2048, 64], P('expert')
- grad_shared_gate: float32 [2048, 2816], P('expert', 'tensor')
- grad_shared_up: float32 [2048, 2816], P('expert', 'tensor')
- grad_shared_down: float32 [2816, 2048], P('tensor', 'expert')
- grad_expert_gate: float32 [64, 2048, 1408], P('expert', None, 'tensor')
- grad_expert_up: float32 [64, 2048, 1408], P('expert', None, 'tensor')
- grad_expert_down: float32 [64, 1408, 2048], P('expert', 'tensor')
Inputs may be any that keep to these rules, and one draw needn't show every extreme that they name: `doc_lengths`: each block's lengths sum to 256; in every block the longest document has exactly 128 tokens. `routes`: each row names 6 different experts. Among the 256 rows of one block, no expert is named by more than 32 rows, a bound that some block reaches.
All inputs are finite; a program needn't handle non-finite values.
Results may differ from a plain program's by a relative error of at most 0.029.
Values may be sent and summed in bfloat16 or wider, within the bound.
A program may use at most 384 MiB of HBM per device.

v0:
```python
import math

import jax
import jax.numpy as jnp
from jax import lax
from jax.sharding import PartitionSpec as P

D = 2048
NOPE = 128
ROPE = 64
VD = 128
KR = 512
EXPERTS = 64
TOPK = 6
CAP = 32


EPSILON = 1e-06
ROPE_BASE = 50000.0
ROUTE_SCALE = 2.446


def matmul(left, right):
    return jnp.dot(left, right, preferred_element_type=jnp.float32)


def contract(form, left, right):
    return jnp.einsum(form, left, right, preferred_element_type=jnp.float32)


def rms_forward(values, gain):
    inverse = lax.rsqrt(jnp.mean(values * values, axis=-1, keepdims=True) + EPSILON)
    return (values * inverse * gain.astype(jnp.float32), inverse)


def rms_backward(values, inverse, gain, cotangent):
    scaled = cotangent * gain.astype(jnp.float32)
    normed = values * inverse
    return inverse * (scaled - normed * jnp.mean(scaled * normed, axis=-1, keepdims=True))


def gain_gradient(values, inverse, cotangent):
    return jnp.sum(cotangent * (values * inverse), axis=0)


def rotate(values, cosine, sinusoid):
    half_width = values.shape[-1] // 2
    leading = values[..., :half_width]
    trailing = values[..., half_width:]
    return jnp.concatenate(
        [leading * cosine - trailing * sinusoid, trailing * cosine + leading * sinusoid], axis=-1
    )


def rotate_back(values, cosine, sinusoid):
    half_width = values.shape[-1] // 2
    leading = values[..., :half_width]
    trailing = values[..., half_width:]
    return jnp.concatenate(
        [leading * cosine + trailing * sinusoid, trailing * cosine - leading * sinusoid], axis=-1
    )


def layout(lengths, row_count):
    doc_count = lengths.shape[0]
    doc_ends = jnp.cumsum(lengths)
    starts = doc_ends - lengths
    row_index = jnp.arange(row_count, dtype=jnp.int32)
    doc_ids = jnp.sum((row_index[:, None] >= doc_ends[None, :]).astype(jnp.int32), axis=1)
    owners = doc_ids[:, None] == jnp.arange(doc_count, dtype=jnp.int32)[None, :]
    first_row = jnp.sum(jnp.where(owners, starts[None, :], 0), axis=1)
    positions = (row_index - first_row).astype(jnp.float32)
    allowed = (doc_ids[:, None] == doc_ids[None, :]) & (row_index[None, :] <= row_index[:, None])
    frequency = jnp.exp(
        -math.log(ROPE_BASE) * 2.0 * jnp.arange(ROPE // 2, dtype=jnp.float32) / ROPE
    )
    angles = positions[:, None] * frequency[None, :]
    return (allowed, jnp.cos(angles), jnp.sin(angles))


def latent_stem(residual, stem_weights, cosine, sinusoid):
    attention_gain, query_down, query_gain, latent_down, latent_gain = stem_weights
    normed, inverse_first = rms_forward(residual, attention_gain)
    first_normed = normed.astype(jnp.bfloat16)
    query_lat = matmul(first_normed, query_down)
    query_n, inverse_query = rms_forward(query_lat, query_gain)
    latent_all = matmul(first_normed, latent_down)
    latent = latent_all[:, :KR]
    latent_n, inverse_latent = rms_forward(latent, latent_gain)
    key_rope = rotate(latent_all[:, KR:], cosine, sinusoid)
    return (
        first_normed,
        inverse_first,
        query_lat,
        inverse_query,
        query_n.astype(jnp.bfloat16),
        latent,
        inverse_latent,
        latent_n.astype(jnp.bfloat16),
        key_rope,
    )


def heads_forward(query_n, latent_n, key_rope, query_up, latent_up, allowed, cosine, sinusoid):
    row_count = query_n.shape[0]
    head_width = NOPE + ROPE
    head_count = query_up.shape[1] // head_width
    queries = matmul(query_n, query_up).reshape(row_count, head_count, head_width)
    queries = jnp.concatenate(
        [
            queries[..., :NOPE],
            rotate(queries[..., NOPE:], cosine[:, None, :], sinusoid[:, None, :]),
        ],
        axis=-1,
    ).astype(jnp.bfloat16)
    keyval = matmul(latent_n, latent_up).reshape(row_count, head_count, NOPE + VD)
    key_rows = jnp.concatenate(
        [keyval[..., :NOPE], jnp.broadcast_to(key_rope[:, None, :], (row_count, head_count, ROPE))],
        axis=-1,
    ).astype(jnp.bfloat16)
    value_rows = keyval[..., NOPE:].astype(jnp.bfloat16)
    scores = contract("qhc,khc->hqk", queries, key_rows) * head_width ** (-0.5)
    scores = jnp.where(allowed[None], scores, -1e30)
    row_peak = jnp.max(scores, axis=-1, keepdims=True)
    powers = jnp.exp(scores - row_peak)
    totals = jnp.sum(powers, axis=-1, keepdims=True)
    logsum = row_peak + jnp.log(totals)
    attn_probs = (powers / totals).astype(jnp.bfloat16)
    attended = (
        contract("hqk,khc->qhc", attn_probs, value_rows)
        .reshape(row_count, head_count * VD)
        .astype(jnp.bfloat16)
    )
    return (attended, logsum, queries, key_rows, value_rows)


def heads_backward(
    attended_grad,
    logsum,
    queries,
    key_rows,
    value_rows,
    query_n,
    latent_n,
    query_up,
    latent_up,
    allowed,
    cosine,
    sinusoid,
):
    row_count = queries.shape[0]
    head_count = queries.shape[1]
    head_width = NOPE + ROPE
    attended_rows = attended_grad.reshape(row_count, head_count, VD)
    scores = contract("qhc,khc->hqk", queries, key_rows) * head_width ** (-0.5)
    attn_probs = jnp.where(allowed[None], jnp.exp(scores - logsum), 0.0)
    dvalues = contract("hqk,qhc->khc", attn_probs.astype(jnp.bfloat16), attended_rows)
    dprobs = contract("qhc,khc->hqk", attended_rows, value_rows)
    row_delta = jnp.sum(attn_probs * dprobs, axis=-1, keepdims=True)
    dscores = (attn_probs * (dprobs - row_delta) * head_width ** (-0.5)).astype(jnp.bfloat16)
    dquery = contract("hqk,khc->qhc", dscores, key_rows)
    dkey_rows = contract("hqk,qhc->khc", dscores, queries)
    dquery = jnp.concatenate(
        [
            dquery[..., :NOPE],
            rotate_back(dquery[..., NOPE:], cosine[:, None, :], sinusoid[:, None, :]),
        ],
        axis=-1,
    )
    dquery = dquery.reshape(row_count, head_count * head_width).astype(jnp.bfloat16)
    dkey_rope = rotate_back(jnp.sum(dkey_rows[..., NOPE:], axis=1), cosine, sinusoid)
    dkeyval = (
        jnp.concatenate([dkey_rows[..., :NOPE], dvalues], axis=-1)
        .reshape(row_count, head_count * (NOPE + VD))
        .astype(jnp.bfloat16)
    )
    grad_query_up = matmul(query_n.T, dquery)
    grad_latent_up = matmul(latent_n.T, dkeyval)
    dquery_n = matmul(dquery, query_up.T)
    dlatent_n = matmul(dkeyval, latent_up.T)
    return (dquery_n, dlatent_n, dkey_rope, grad_query_up, grad_latent_up)


def latent_stem_back(residual, stashed, stem_weights, dquery_n, dlatent_n, dkey_rope):
    attention_gain, query_down, query_gain, latent_down, latent_gain = stem_weights
    first_normed = stashed[0]
    dquery_lat = rms_backward(stashed[2], stashed[3], query_gain, dquery_n).astype(jnp.bfloat16)
    grad_query_gain = gain_gradient(stashed[2], stashed[3], dquery_n)
    dlatent_all = jnp.concatenate(
        [rms_backward(stashed[5], stashed[6], latent_gain, dlatent_n), dkey_rope], axis=-1
    ).astype(jnp.bfloat16)
    grad_latent_gain = gain_gradient(stashed[5], stashed[6], dlatent_n)
    grad_query_down = matmul(first_normed.T, dquery_lat)
    grad_latent_down = matmul(first_normed.T, dlatent_all)
    dfirst = matmul(dquery_lat, query_down.T) + matmul(dlatent_all, latent_down.T)
    dresidual = rms_backward(residual, stashed[1], attention_gain, dfirst)
    grad_attention_gain = gain_gradient(residual, stashed[1], dfirst)
    return (
        dresidual,
        (grad_attention_gain, grad_query_down, grad_query_gain, grad_latent_down, grad_latent_gain),
    )


def swiglu_forward(row_inputs, gate_weight, up_weight):
    gate_pre = matmul(row_inputs, gate_weight)
    up_pre = matmul(row_inputs, up_weight)
    hidden = (gate_pre * jax.nn.sigmoid(gate_pre) * up_pre).astype(jnp.bfloat16)
    return (gate_pre, up_pre, hidden)


def swiglu_backward(row_inputs, cotangent, gate_pre, up_pre, hidden, down_weight):
    sigmoid_gate = jax.nn.sigmoid(gate_pre)
    dhidden = matmul(cotangent, down_weight.T)
    gate_grad = (dhidden * up_pre * sigmoid_gate * (1.0 + gate_pre * (1.0 - sigmoid_gate))).astype(
        jnp.bfloat16
    )
    up_grad = (dhidden * gate_pre * sigmoid_gate).astype(jnp.bfloat16)
    return (
        gate_grad,
        up_grad,
        matmul(row_inputs.T, gate_grad),
        matmul(row_inputs.T, up_grad),
        matmul(hidden.T, cotangent),
    )


def router_forward(second_normed, router_weight, route_rows):
    sigmoid_all = jax.nn.sigmoid(matmul(second_normed, router_weight))
    route_hot = route_rows[:, :, None] == jnp.arange(EXPERTS, dtype=jnp.int32)[None, None, :]
    chosen = jnp.sum(jnp.where(route_hot, sigmoid_all[:, None, :], 0.0), axis=-1)
    totals = jnp.sum(chosen, axis=-1, keepdims=True)
    return (route_hot, chosen, totals, ROUTE_SCALE * chosen / totals)


def router_backward(route_hot, chosen, totals, dweights):
    dchosen = (
        ROUTE_SCALE
        / totals
        * (dweights - jnp.sum(dweights * chosen, axis=-1, keepdims=True) / totals)
    )
    dpicked = dchosen * chosen * (1.0 - chosen)
    return jnp.sum(jnp.where(route_hot, dpicked[:, :, None], 0.0), axis=1).astype(jnp.bfloat16)


def slot_positions(route_rows, capacity):
    flat_routes = route_rows.reshape(-1)
    route_hot = (flat_routes[:, None] == jnp.arange(EXPERTS, dtype=jnp.int32)[None, :]).astype(
        jnp.int32
    )
    earlier = jnp.cumsum(route_hot, axis=0) - route_hot
    slot_rank = jnp.sum(earlier * route_hot, axis=1)
    return flat_routes * capacity + slot_rank


def body(
    block_in,
    attention_gain,
    query_down,
    query_gain,
    query_up,
    latent_down,
    latent_gain,
    latent_up,
    out_proj,
    ffn_gain,
    router,
    shared_gate,
    shared_up,
    shared_down,
    expert_gate,
    expert_up,
    expert_down,
    doc_lengths,
    routes,
    out_grad,
):
    groups = lax.axis_size("expert")
    row_count = block_in.shape[0]
    local_count = expert_gate.shape[0]
    gathered = (
        lax.all_gather(attention_gain, "expert", axis=0, tiled=True),
        lax.all_gather(ffn_gain, "expert", axis=0, tiled=True),
        lax.all_gather(query_gain, "expert", axis=0, tiled=True),
        lax.all_gather(latent_gain, "expert", axis=0, tiled=True),
        lax.all_gather(query_down, "expert", axis=0, tiled=True),
        lax.all_gather(latent_down, "expert", axis=0, tiled=True),
        lax.all_gather(router, "expert", axis=0, tiled=True),
        lax.all_gather(query_up, "expert", axis=0, tiled=True),
        lax.all_gather(latent_up, "expert", axis=0, tiled=True),
        lax.all_gather(out_proj, "expert", axis=1, tiled=True),
        lax.all_gather(shared_gate, "expert", axis=0, tiled=True),
        lax.all_gather(shared_up, "expert", axis=0, tiled=True),
        lax.all_gather(shared_down, "expert", axis=1, tiled=True),
    )
    (
        attention_full,
        ffn_full,
        query_gain_full,
        latent_gain_full,
        query_down_full,
        latent_down_full,
        router_full,
    ) = gathered[:7]
    (
        query_up_full,
        latent_up_full,
        out_proj_full,
        shared_gate_full,
        shared_up_full,
        shared_down_full,
    ) = gathered[7:]
    stem_weights = (
        attention_full,
        query_down_full,
        query_gain_full,
        latent_down_full,
        latent_gain_full,
    )
    residual = block_in.astype(jnp.float32)
    allowed, cosine, sinusoid = layout(doc_lengths[0], row_count)
    stashed = latent_stem(residual, stem_weights, cosine, sinusoid)
    attended, logsum, queries, key_rows, value_rows = heads_forward(
        stashed[4], stashed[7], stashed[8], query_up_full, latent_up_full, allowed, cosine, sinusoid
    )
    middle = residual + lax.psum(
        matmul(attended, out_proj_full).astype(jnp.bfloat16), "tensor"
    ).astype(jnp.float32)
    second_f, inverse_ffn = rms_forward(middle, ffn_full)
    second_normed = second_f.astype(jnp.bfloat16)
    route_hot, chosen, totals, route_weights = router_forward(second_normed, router_full, routes)
    slot_index = slot_positions(routes, CAP)
    tensor_index = lax.axis_index("tensor")
    leading_group = (tensor_index == 0).astype(jnp.float32)
    copies = jnp.broadcast_to(second_normed[:, None, :], (row_count, TOPK, D)).reshape(
        row_count * TOPK, D
    )
    outgoing = (
        jnp.zeros((EXPERTS * CAP, D), jnp.bfloat16)
        .at[slot_index]
        .set(copies)
        .reshape(groups, local_count, CAP, D)
    )
    arrived = lax.all_to_all(outgoing, "expert", split_axis=0, concat_axis=0, tiled=True)
    expert_rows = []
    expert_stash = []
    produced = []
    for expert_slot in range(local_count):
        row_inputs = arrived[:, expert_slot].reshape(groups * CAP, D)
        gate_pre, up_pre, hidden = swiglu_forward(
            row_inputs, expert_gate[expert_slot], expert_up[expert_slot]
        )
        expert_rows.append(row_inputs)
        expert_stash.append((gate_pre, up_pre, hidden))
        produced.append(
            matmul(hidden, expert_down[expert_slot]).astype(jnp.bfloat16).reshape(groups, CAP, D)
        )
    stacked_rows = jnp.stack(produced, axis=1)
    returned = lax.all_to_all(stacked_rows, "expert", split_axis=0, concat_axis=0, tiled=True)
    routed = (
        returned.reshape(EXPERTS * CAP, D)[slot_index]
        .astype(jnp.float32)
        .reshape(row_count, TOPK, D)
    )
    shared_gate_pre, shared_up_pre, shared_hidden = swiglu_forward(
        second_normed, shared_gate_full, shared_up_full
    )
    shared_out = matmul(shared_hidden, shared_down_full)
    gradient = out_grad.astype(jnp.float32)
    mixed_part = shared_out + jnp.sum(route_weights[:, :, None] * routed, axis=1)
    dweight_part = jnp.sum(gradient[:, None, :] * routed, axis=-1)
    mixed, dweights = (
        lax.psum(mixed_part.astype(jnp.bfloat16), "tensor").astype(jnp.float32),
        lax.psum(dweight_part.astype(jnp.bfloat16), "tensor").astype(jnp.float32),
    )
    block_out = (middle + mixed).astype(jnp.bfloat16)
    scaled = (
        (route_weights[:, :, None] * gradient[:, None, :])
        .astype(jnp.bfloat16)
        .reshape(row_count * TOPK, D)
    )
    outgoing_grad = (
        jnp.zeros((EXPERTS * CAP, D), jnp.bfloat16)
        .at[slot_index]
        .set(scaled)
        .reshape(groups, local_count, CAP, D)
    )
    arrived_grad = lax.all_to_all(outgoing_grad, "expert", split_axis=0, concat_axis=0, tiled=True)
    back_rows = []
    grads_gate = []
    grads_up = []
    grads_down = []
    for expert_slot in range(local_count):
        cotangent = arrived_grad[:, expert_slot].reshape(groups * CAP, D)
        gate_pre, up_pre, hidden = expert_stash[expert_slot]
        gate_grad, up_grad, grad_gate, grad_up, grad_down = swiglu_backward(
            expert_rows[expert_slot], cotangent, gate_pre, up_pre, hidden, expert_down[expert_slot]
        )
        input_rows = matmul(gate_grad, expert_gate[expert_slot].T) + matmul(
            up_grad, expert_up[expert_slot].T
        )
        back_rows.append(input_rows.astype(jnp.bfloat16).reshape(groups, CAP, D))
        grads_gate.append(grad_gate)
        grads_up.append(grad_up)
        grads_down.append(grad_down)
    stacked_back = jnp.stack(back_rows, axis=1)
    returned_grad = lax.all_to_all(stacked_back, "expert", split_axis=0, concat_axis=0, tiled=True)
    drouted = jnp.sum(
        returned_grad.reshape(EXPERTS * CAP, D)[slot_index]
        .astype(jnp.float32)
        .reshape(row_count, TOPK, D),
        axis=1,
    )
    dlogits = router_backward(route_hot, chosen, totals, dweights)
    shared_gate_grad, shared_up_grad, grad_shared_gate, grad_shared_up, grad_shared_down = (
        swiglu_backward(
            second_normed, out_grad, shared_gate_pre, shared_up_pre, shared_hidden, shared_down_full
        )
    )
    dsecond_part = (
        matmul(shared_gate_grad, shared_gate_full.T)
        + matmul(shared_up_grad, shared_up_full.T)
        + drouted
        + matmul(dlogits, router_full.T) * leading_group
    )
    grad_router = matmul(second_normed.T, dlogits) * leading_group
    grad_ffn_gain = gain_gradient(middle, inverse_ffn, dsecond_part)
    dsecond = lax.psum(dsecond_part.astype(jnp.bfloat16), "tensor").astype(jnp.float32)
    middle_grad = gradient + rms_backward(middle, inverse_ffn, ffn_full, dsecond)
    attention_grad = middle_grad.astype(jnp.bfloat16)
    grad_out_proj = matmul(attended.T, attention_grad)
    attended_grad = matmul(attention_grad, out_proj_full.T).astype(jnp.bfloat16)
    dquery_n, dlatent_n, dkey_rope, grad_query_up, grad_latent_up = heads_backward(
        attended_grad,
        logsum,
        queries,
        key_rows,
        value_rows,
        stashed[4],
        stashed[7],
        query_up_full,
        latent_up_full,
        allowed,
        cosine,
        sinusoid,
    )
    dresidual, stem_grads = latent_stem_back(
        residual, stashed, stem_weights, dquery_n, dlatent_n, dkey_rope
    )
    summed = (
        lax.psum(dresidual.astype(jnp.bfloat16), "tensor").astype(jnp.float32),
        lax.psum(stem_grads[0].astype(jnp.bfloat16), "tensor").astype(jnp.float32),
        lax.psum(stem_grads[1].astype(jnp.bfloat16), "tensor").astype(jnp.float32),
        lax.psum(stem_grads[2].astype(jnp.bfloat16), "tensor").astype(jnp.float32),
        lax.psum(stem_grads[3].astype(jnp.bfloat16), "tensor").astype(jnp.float32),
        lax.psum(stem_grads[4].astype(jnp.bfloat16), "tensor").astype(jnp.float32),
        lax.psum(grad_ffn_gain.astype(jnp.bfloat16), "tensor").astype(jnp.float32),
        lax.psum(grad_router.astype(jnp.bfloat16), "tensor").astype(jnp.float32),
    )
    dresidual_sum = summed[0]
    reduced = (
        lax.psum_scatter(
            summed[1].astype(jnp.bfloat16), "expert", scatter_dimension=0, tiled=True
        ).astype(jnp.float32),
        lax.psum_scatter(
            summed[6].astype(jnp.bfloat16), "expert", scatter_dimension=0, tiled=True
        ).astype(jnp.float32),
        lax.psum_scatter(
            summed[3].astype(jnp.bfloat16), "expert", scatter_dimension=0, tiled=True
        ).astype(jnp.float32),
        lax.psum_scatter(
            summed[5].astype(jnp.bfloat16), "expert", scatter_dimension=0, tiled=True
        ).astype(jnp.float32),
        lax.psum_scatter(
            summed[2].astype(jnp.bfloat16), "expert", scatter_dimension=0, tiled=True
        ).astype(jnp.float32),
        lax.psum_scatter(
            summed[4].astype(jnp.bfloat16), "expert", scatter_dimension=0, tiled=True
        ).astype(jnp.float32),
        lax.psum_scatter(
            summed[7].astype(jnp.bfloat16), "expert", scatter_dimension=0, tiled=True
        ).astype(jnp.float32),
        lax.psum_scatter(
            grad_query_up.astype(jnp.bfloat16), "expert", scatter_dimension=0, tiled=True
        ).astype(jnp.float32),
        lax.psum_scatter(
            grad_latent_up.astype(jnp.bfloat16), "expert", scatter_dimension=0, tiled=True
        ).astype(jnp.float32),
        lax.psum_scatter(
            grad_out_proj.astype(jnp.bfloat16), "expert", scatter_dimension=1, tiled=True
        ).astype(jnp.float32),
        lax.psum_scatter(
            grad_shared_gate.astype(jnp.bfloat16), "expert", scatter_dimension=0, tiled=True
        ).astype(jnp.float32),
        lax.psum_scatter(
            grad_shared_up.astype(jnp.bfloat16), "expert", scatter_dimension=0, tiled=True
        ).astype(jnp.float32),
        lax.psum_scatter(
            grad_shared_down.astype(jnp.bfloat16), "expert", scatter_dimension=1, tiled=True
        ).astype(jnp.float32),
    )
    input_grad = (middle_grad + dresidual_sum).astype(jnp.bfloat16)
    return (
        block_out,
        input_grad,
        reduced[0],
        reduced[4],
        reduced[2],
        reduced[7],
        reduced[5],
        reduced[3],
        reduced[8],
        reduced[9],
        reduced[1],
        reduced[6],
        reduced[10],
        reduced[11],
        reduced[12],
        jnp.stack(grads_gate, axis=0),
        jnp.stack(grads_up, axis=0),
        jnp.stack(grads_down, axis=0),
    )


def solution(mesh):
    placed = (
        P("expert", None),
        P("expert"),
        P("expert", None),
        P("expert"),
        P("expert", "tensor"),
        P("expert", None),
        P("expert"),
        P("expert", "tensor"),
        P("tensor", "expert"),
        P("expert"),
        P("expert", None),
        P("expert", "tensor"),
        P("expert", "tensor"),
        P("tensor", "expert"),
        P("expert", None, "tensor"),
        P("expert", None, "tensor"),
        P("expert", "tensor", None),
        P("expert", None),
        P("expert", None),
        P("expert", None),
    )
    return jax.shard_map(
        body,
        mesh=mesh,
        in_specs=placed,
        out_specs=(
            P("expert", None),
            P("expert", None),
            P("expert"),
            P("expert", None),
            P("expert"),
            P("expert", "tensor"),
            P("expert", None),
            P("expert"),
            P("expert", "tensor"),
            P("tensor", "expert"),
            P("expert"),
            P("expert", None),
            P("expert", "tensor"),
            P("expert", "tensor"),
            P("tensor", "expert"),
            P("expert", None, "tensor"),
            P("expert", None, "tensor"),
            P("expert", "tensor", None),
        ),
        check_vma=False,
    )
```

profile of v0, /device:TPU:0, one launch (start us, length us, event | category | flops | bytes accessed | tf_op | source)
XLA Modules:
  0.0 2243.6 jit_solution(7313152346299688446)
XLA Ops:
  16.7 23.5 %all-reduce.7 = (bf16[512]{0:T(512)(128)(2,1)S(1)}, bf16[1536]{0:T(1024)(128)(2,1)S(1)}) all-reduce(bf16[512]{0:T(512)(128)(2,1)S(1)} %dynamic-update-slice, bf16[1536]{0:T(1024)(128)(2,1)S(1)} %dynamic-update-slice.1), channel_id=1, replica_groups=mesh['expert'=8,'tensor'=4] {'expert'}, use_global_device_ids=true, to_apply=%add | all-reduce | flops 2048 | bytes 8192
  40.3 16.8 all-gather
  58.2 8.4 all-gather.11.cloned.1.call-done
  69.3 38.0 %all-gather.13.cloned.1.call-done = bf16[512,1024]{1,0:T(8,128)(2,1)} async-done(((bf16[64,1024]{1,0:T(8,128)(2,1)}), bf16[512,1024]{1,0:T(8,128)(2,1)}) %all-gather.13.cloned.1.call-update) | async-done | bytes 1048592 | tf_op jit(solution)/shard_map/all_gather | solution.py:289
  110.2 96.6 %all-gather.15.cloned.1.call-done = bf16[2048,1536]{1,0:T(8,128)(2,1)} async-done(((bf16[256,1536]{1,0:T(8,128)(2,1)}), bf16[2048,1536]{1,0:T(8,128)(2,1)}) %all-gather.15.cloned.1.call-update) | async-done | bytes 6291472 | tf_op jit(solution)/shard_map/all_gather | solution.py:285
  206.9 4.7 multiply_reduce_fusion.7
  211.6 47.3 %all-gather.17.cloned.1.call-done = bf16[1536,768]{1,0:T(8,128)(2,1)} async-done(((bf16[192,768]{1,0:T(8,128)(2,1)}), bf16[1536,768]{1,0:T(8,128)(2,1)}) %all-gather.17.cloned.1.call-update) | async-done | bytes 2359312 | tf_op jit(solution)/shard_map/all_gather | solution.py:288
  263.7 46.0 %all-gather.19.cloned.1.call-done = bf16[512,2048]{1,0:T(8,128)(2,1)} async-done(((bf16[512,256]{1,0:T(8,128)(2,1)}), bf16[512,2048]{1,0:T(8,128)(2,1)}) %all-gather.19.cloned.1.call-update) | async-done | bytes 2097168 | tf_op jit(solution)/shard_map/all_gather | solution.py:290
  309.7 3.3 convolution_convert_fusion.7
  313.2 17.9 all-gather.1
  331.5 18.1 reduce-window.11
  354.0 4.8 broadcast_in_dim.62
  358.9 11.0 reshape.380
  369.9 15.2 scatter_custom_fusion
  385.1 5.3 all-to-all-start
  390.4 8.3 mul.701
  398.8 15.7 mul.702
  414.4 176.6 %all_gather.51 = bf16[2048,64]{0,1:T(8,128)(2,1)S(1)} all-gather(bf16[256,64]{0,1:T(8,128)(2,1)S(1)} %copy-done.150), channel_id=1, replica_groups=mesh['expert'=8,'tensor'=4] {'expert'}, dimensions={0}, use_global_device_ids=true | all-gather | bytes 294912 | tf_op jit(solution)/shard_map/all_gather | solution.py:287
  592.6 16.3 scatter_custom_fusion.1
  608.9 5.4 all-to-all-start.2
  614.2 4.0 fusion.252
  618.4 3.7 fusion.68
  661.5 131.2 %all-to-all-done.2 = bf16[8,8,32,2048]{3,2,1,0:T(8,128)(2,1)} async-done(((bf16[8,8,32,2048]{3,2,1,0:T(8,128)(2,1)}), bf16[8,8,32,2048]{3,2,1,0:T(8,128)(2,1)}, u32[]{:S(2)}, u32[]{:S(2)}) %all-to-all-start.2) | async-done | bytes 8388640 | tf_op jit(solution)/shard_map/all_to_all | solution.py:387
  792.8 4.3 fusion.251
  797.2 4.6 multiply_convert_fusion.12
  824.0 3.0 multiply_convert_fusion.22
  846.6 5.0 all-to-all-start.3
  878.0 190.4 %all-to-all-done.3 = bf16[8,8,32,2048]{3,2,1,0:T(8,128)(2,1)} async-done(((bf16[8,8,32,2048]{3,2,1,0:T(8,128)(2,1)}), bf16[8,8,32,2048]{3,2,1,0:T(8,128)(2,1)}, u32[]{:S(2)}, u32[]{:S(2)}) %all-to-all-start.3) | async-done | bytes 8388640 | tf_op jit(solution)/shard_map/all_to_all | solution.py:406
  1068.4 4.9 all-to-all-start.1
  1076.5 3.6 fusion.256
  1080.1 177.6 %all-gather.21.cloned.1.call-done = bf16[2048,704]{0,1:T(8,128)(2,1)} async-done(((bf16[256,704]{0,1:T(8,128)(2,1)}), bf16[2048,704]{0,1:T(8,128)(2,1)}) %all-gather.21.cloned.1.call-update) | async-done | bytes 2883600 | tf_op jit(solution)/shard_map/all_gather | solution.py:291
  1257.7 3.6 fusion.255
  1261.3 63.8 %all-gather.25.cloned.1.call-done = bf16[704,2048]{1,0:T(8,128)(2,1)} async-done(((bf16[704,256]{1,0:T(8,128)(2,1)}), bf16[704,2048]{1,0:T(8,128)(2,1)}) %all-gather.25.cloned.1.call-update) | async-done | bytes 2883600 | tf_op jit(solution)/shard_map/all_gather | solution.py:293
  1325.1 3.5 multiply_convert_fusion.5
  1330.9 17.6 gather_fusion.1
  1348.5 17.1 gather_fusion
  1365.6 11.7 reshape.358
  1377.3 12.2 multiply_reduce_fusion
  1389.6 6.8 psum.86
  1396.5 11.7 reshape.359
  1408.2 9.8 reduce_sum.239
  1418.1 4.1 fusion.35
  1432.9 26.9 %all-reduce.16.cloned.1.call-done = bf16[256,2048]{1,0:T(8,128)(2,1)} async-done(((bf16[256,2048]{1,0:T(8,128)(2,1)}), bf16[256,2048]{1,0:T(8,128)(2,1)}) %all-reduce.16.cloned.1.call-update) | async-done | bytes 1048592 | tf_op jit(solution)/shard_map/psum | solution.py:427
  1459.9 3.4 multiply_reduce_fusion.2
  1468.0 4.0 convolution_bitcast_fusion.24
  1480.7 3.1 convolution_bitcast_fusion.25
  1484.0 4.1 multiply_reduce_fusion.5
  1488.7 4.6 convolution_convert_fusion
  1503.1 34.1 %reduce-scatter.18.cloned.1.call-done = bf16[256,704]{0,1:T(8,128)(2,1)} async-done(((bf16[2048,704]{0,1:T(8,128)(2,1)}), bf16[256,704]{0,1:T(8,128)(2,1)}) %reduce-scatter.18.cloned.1.call-update) | async-done | bytes 360464 | tf_op jit(solution)/shard_map/reduce_scatter | solution.py:494
  1539.1 74.3 %reduce-scatter.16.cloned.1.call-done = bf16[256,704]{0,1:T(8,128)(2,1)} async-done(((bf16[2048,704]{0,1:T(8,128)(2,1)}), bf16[256,704]{0,1:T(8,128)(2,1)}) %reduce-scatter.16.cloned.1.call-update) | async-done | bytes 360464 | tf_op jit(solution)/shard_map/reduce_scatter | solution.py:491
  1615.4 74.4 %reduce-scatter.20.cloned.1.call-done = bf16[704,256]{1,0:T(8,128)(2,1)} async-done(((bf16[704,2048]{1,0:T(8,128)(2,1)}), bf16[704,256]{1,0:T(8,128)(2,1)}) %reduce-scatter.20.cloned.1.call-update) | async-done | bytes 360464 | tf_op jit(solution)/shard_map/reduce_scatter | solution.py:497
  1691.7 3.5 fusion.33
  1713.8 8.2 copy-done.103
  1724.7 3.5 fusion.15
  1752.0 10.5 reduce-scatter.24.cloned.1.call-done
  1762.5 120.7 %reduce-scatter.22.cloned.1.call-done = bf16[256,1536]{1,0:T(8,128)(2,1)} async-done(((bf16[2048,1536]{1,0:T(8,128)(2,1)}), bf16[256,1536]{1,0:T(8,128)(2,1)}) %reduce-scatter.22.cloned.1.call-update) | async-done | bytes 786448 | tf_op jit(solution)/shard_map/reduce_scatter | solution.py:473
  1883.2 3.4 fusion.22
  1895.2 35.5 %all-reduce.6 = (bf16[2048]{0:T(1024)(128)(2,1)S(1)}, bf16[1536]{0:T(1024)(128)(2,1)S(1)}, bf16[512]{0:T(512)(128)(2,1)S(1)}, bf16[2048]{0:T(1024)(128)(2,1)S(1)}) all-reduce(bf16[2048]{0:T(1024)(128)(2,1)S(1)} %get-tuple-element.22, bf16[1536]{0:T(1024)(128)(2,1)S(1)} %copy-done.164, ...), channel_id=2, replica_groups=mesh['expert'=8,'tensor'=4] {'expert'}, use_global_device_ids=true, to_apply=%region_34.35.clone | all-reduce | flops 6144 | bytes 24576
  1931.0 17.7 reduce-scatter.26.cloned.1.call-done
  1948.7 11.0 all-reduce.8
  1962.6 52.7 %reduce-scatter.12.cloned.1.call-done = bf16[64,1024]{1,0:T(8,128)(2,1)} async-done(((bf16[512,1024]{1,0:T(8,128)(2,1)}), bf16[64,1024]{1,0:T(8,128)(2,1)}) %reduce-scatter.12.cloned.1.call-update) | async-done | bytes 131088 | tf_op jit(solution)/shard_map/reduce_scatter | solution.py:485
  2016.9 69.4 %reduce-scatter.14.cloned.1.call-done = bf16[512,256]{1,0:T(8,128)(2,1)} async-done(((bf16[512,2048]{1,0:T(8,128)(2,1)}), bf16[512,256]{1,0:T(8,128)(2,1)}) %reduce-scatter.14.cloned.1.call-update) | async-done | bytes 262160 | tf_op jit(solution)/shard_map/reduce_scatter | solution.py:488
  2088.0 70.4 %reduce-scatter.10.cloned.1.call-done = bf16[192,768]{1,0:T(8,128)(2,1)} async-done(((bf16[1536,768]{1,0:T(8,128)(2,1)}), bf16[192,768]{1,0:T(8,128)(2,1)}) %reduce-scatter.10.cloned.1.call-update) | async-done | bytes 294928 | tf_op jit(solution)/shard_map/reduce_scatter | solution.py:482
  2160.2 69.5 %all-reduce.18.cloned.1.call-done = (bf16[256,2048]{1,0:T(8,128)(2,1)}, bf16[256,2048]{1,0:T(8,128)(2,1)}, bf16[256,1536]{1,0:T(8,128)(2,1)}, bf16[256,576]{0,1:T(8,128)(2,1)}) async-done(((bf16[256,2048]{1,0:T(8,128)(2,1)}, bf16[256,2048]{1,0:T(8,128)(2,1)}, bf16[256,1536]{1,0:T(8,128)(2,1)}, bf16[256,576]{0,1:T(8,128)(2,1)}), (bf16[256,2048]{1,0:T(8,128)(2,1)}, bf16[256,2048]{1,0:T(8,128)(2,1)}, ...) | async-done | bytes 3178512 | tf_op jit(solution)/shard_map/psum | solution.py:372
  (644 shorter events, 244.8 us)
Async XLA Ops:
  7.2 59.4 %copy-start = (bf16[256,2048]{1,0:T(8,128)(2,1)S(1)}, bf16[256,2048]{1,0:T(8,128)(2,1)}, u32[]{:S(2)}) copy-start(bf16[256,2048]{1,0:T(8,128)(2,1)} %param.20) | copy-start | bytes 3145732
  7.2 49.8 %copy-start.137 = (s32[256,6]{0,1:T(8,128)S(1)}, s32[256,6]{0,1:T(8,128)}, u32[]{:S(2)}) copy-start(s32[256,6]{0,1:T(8,128)} %param.38) | copy-start | bytes 18436
  7.3 59.3 %all-gather.11.cloned.1.call-start = ((), (), s32[]{:S(2)}) async-start(), calls=%async_computation.13 | async-start | bytes 2654208 | tf_op jit(solution)/shard_map/all_gather | solution.py:286
  8.0 99.2 %all-gather.13.cloned.1.call-start = ((), (), s32[]{:S(2)}) async-start(), calls=%async_computation.14 | async-start | bytes 1179648 | tf_op jit(solution)/shard_map/all_gather | solution.py:289
  8.7 198.1 %all-gather.15.cloned.1.call-start = ((), (), s32[]{:S(2)}) async-start(), calls=%async_computation.15 | async-start | bytes 7077888 | tf_op jit(solution)/shard_map/all_gather | solution.py:285
  9.5 249.4 %all-gather.17.cloned.1.call-start = ((), (), s32[]{:S(2)}) async-start(), calls=%async_computation.16 | async-start | bytes 2654208 | tf_op jit(solution)/shard_map/all_gather | solution.py:288
  10.0 299.7 %all-gather.19.cloned.1.call-start = ((), (), s32[]{:S(2)}) async-start(), calls=%async_computation.17 | async-start | bytes 2359296 | tf_op jit(solution)/shard_map/all_gather | solution.py:290
  10.6 340.0 %all-reduce.14.cloned.1.call-start = ((), (), s32[]{:S(2)}) async-start(), calls=%async_computation.18 | async-start | bytes 2097152 | tf_op jit(solution)/shard_map/psum | solution.py:325
  10.7 99.3 %copy-start.168 = (f32[32]{0:T(128)}, f32[32]{0:T(128)S(1)}, u32[]{:S(2)}) copy-start(f32[32]{0:T(128)S(1)} %multiply_exponential_fusion) | copy-start | bytes 388
  12.4 250.2 %copy-start.104 = (pred[256,256]{0,1:T(8,128)(4,1)}, pred[256,256]{0,1:T(8,128)(4,1)S(1)}, u32[]{:S(2)}) copy-start(pred[256,256]{0,1:T(8,128)(4,1)S(1)} %fusion.205) | copy-start | bytes 196612
  12.5 97.5 %copy-start.156 = (f32[256]{0:T(256)}, f32[256]{0:T(256)S(1)}, u32[]{:S(2)}) copy-start(f32[256]{0:T(256)S(1)} %subtract_convert_fusion.2) | copy-start | bytes 3076
  14.2 247.6 %copy-start.123 = (f32[256,32]{0,1:T(8,128)}, f32[256,32]{0,1:T(8,128)S(1)}, u32[]{:S(2)}) copy-start(f32[256,32]{0,1:T(8,128)S(1)} %get-tuple-element.96) | copy-start | bytes 98308
  14.2 247.6 %copy-start.125 = (f32[256,32]{0,1:T(8,128)}, f32[256,32]{0,1:T(8,128)S(1)}, u32[]{:S(2)}) copy-start(f32[256,32]{0,1:T(8,128)S(1)} %get-tuple-element.97) | copy-start | bytes 98308
  14.2 192.6 %copy-start.138 = (f32[256]{0:T(256)}, f32[256]{0:T(256)S(1)}, u32[]{:S(2)}) copy-start(f32[256]{0:T(256)S(1)} %add_rsqrt_fusion.3) | copy-start | bytes 3076
  40.3 67.0 %copy-start.148 = (f32[512]{0:T(512)}, f32[512]{0:T(512)S(1)}, u32[]{:S(2)}) copy-start(f32[512]{0:T(512)S(1)} %convert_element_type.378) | copy-start | bytes 6148
  57.1 149.8 %copy-start.106 = (f32[8,1,256]{2,1,0:T(1,128)}, f32[8,1,256]{2,1,0:T(1,128)S(1)}, u32[]{:S(2)}) copy-start(f32[8,1,256]{2,1,0:T(1,128)S(1)} %convert_element_type.490) | copy-start | bytes 24580
  57.1 201.8 %copy-start.131 = (f32[1536]{0:T(1024)}, f32[1536]{0:T(1024)S(1)}, u32[]{:S(2)}) copy-start(f32[1536]{0:T(1024)S(1)} %convert_element_type.381) | copy-start | bytes 18436
  69.2 41.1 %copy-start.34 = (f32[256,576]{0,1:T(8,128)}, f32[256,576]{0,1:T(8,128)S(1)}, u32[]{:S(2)}) copy-start(f32[256,576]{0,1:T(8,128)S(1)} %fusion.249) | copy-start | bytes 1769476
  69.3 40.0 %copy-start.154 = (f32[256]{0:T(256)}, f32[256]{0:T(256)S(1)}, u32[]{:S(2)}) copy-start(f32[256]{0:T(256)S(1)} %add_rsqrt_fusion.2) | copy-start | bytes 3076
  109.2 153.3 %copy-start.63 = (bf16[256,1024]{0,1:T(8,128)(2,1)}, bf16[256,1024]{0,1:T(8,128)(2,1)S(1)}, u32[]{:S(2)}) copy-start(bf16[256,1024]{0,1:T(8,128)(2,1)S(1)} %copy.190) | copy-start | bytes 1572868
  211.6 50.3 %copy-start.6 = (f32[256,1536]{1,0:T(8,128)}, f32[256,1536]{1,0:T(8,128)S(1)}, u32[]{:S(2)}) copy-start(f32[256,1536]{1,0:T(8,128)S(1)} %get-tuple-element.103) | copy-start | bytes 4718596
  211.6 50.3 %copy-start.151 = (f32[256]{0:T(256)}, f32[256]{0:T(256)S(1)}, u32[]{:S(2)}) copy-start(f32[256]{0:T(256)S(1)} %add_rsqrt_fusion.1) | copy-start | bytes 3076
  263.3 49.7 %copy-start.160 = (f32[4,256]{1,0:T(4,128)}, f32[4,256]{1,0:T(4,128)S(1)}, u32[]{:S(2)}) copy-start(f32[4,256]{1,0:T(4,128)S(1)} %fusion.194) | copy-start | bytes 12292
  263.7 67.6 %copy-start.100 = (bf16[4,128,256]{2,1,0:T(8,128)(2,1)}, bf16[4,128,256]{2,1,0:T(8,128)(2,1)S(1)}, u32[]{:S(2)}) copy-start(bf16[4,128,256]{2,1,0:T(8,128)(2,1)S(1)} %convolution_convert_fusion.20) | copy-start | bytes 786436
  263.7 49.5 %copy-start.175 = (bf16[256]{0:T(256)(128)(2,1)S(1)}, bf16[256]{0:T(256)(128)(2,1)}, u32[]{:S(2)}) copy-start(bf16[256]{0:T(256)(128)(2,1)} %param.29) | copy-start | bytes 1540
  263.7 67.7 %copy-start.65 = (s32[64,12,128]{2,1,0:T(8,128)S(1)}, s32[64,12,128]{2,1,0:T(8,128)}, u32[]{:S(2)}) copy-start(s32[64,12,128]{2,1,0:T(8,128)} %fusion.200) | copy-start | bytes 1179652
  331.1 21.2 copy-start.133
  385.1 223.7 %all-to-all-start = ((bf16[8,8,32,2048]{3,2,1,0:T(8,128)(2,1)}), bf16[8,8,32,2048]{3,2,1,0:T(8,128)(2,1)}, u32[]{:S(2)}, u32[]{:S(2)}) async-start(bf16[8,8,32,2048]{3,2,1,0:T(8,128)(2,1)} %bitcast.489), calls=%async_computation | async-start | bytes 16777216 | tf_op jit(solution)/shard_map/all_to_all | solution.py:343
  608.9 183.9 %all-to-all-start.2 = ((bf16[8,8,32,2048]{3,2,1,0:T(8,128)(2,1)}), bf16[8,8,32,2048]{3,2,1,0:T(8,128)(2,1)}, u32[]{:S(2)}, u32[]{:S(2)}) async-start(bf16[8,8,32,2048]{3,2,1,0:T(8,128)(2,1)} %bitcast.488), calls=%async_computation.2 | async-start | bytes 16777216 | tf_op jit(solution)/shard_map/all_to_all | solution.py:387
  618.3 24.5 %copy-start.23 = (bf16[8,1,32,2048]{3,2,1,0:T(8,128)(2,1)}, bf16[8,1,32,2048]{3,2,1,0:T(8,128)(2,1)S(1)}, u32[]{:S(2)}) copy-start(bf16[8,1,32,2048]{3,2,1,0:T(8,128)(2,1)S(1)} %get-tuple-element.57) | copy-start | bytes 3145732
  618.3 29.8 %copy-start.25 = (bf16[8,1,32,2048]{3,2,1,0:T(8,128)(2,1)}, bf16[8,1,32,2048]{3,2,1,0:T(8,128)(2,1)S(1)}, u32[]{:S(2)}) copy-start(bf16[8,1,32,2048]{3,2,1,0:T(8,128)(2,1)S(1)} %get-tuple-element.58) | copy-start | bytes 3145732
  618.3 35.1 %copy-start.27 = (bf16[8,1,32,2048]{3,2,1,0:T(8,128)(2,1)}, bf16[8,1,32,2048]{3,2,1,0:T(8,128)(2,1)S(1)}, u32[]{:S(2)}) copy-start(bf16[8,1,32,2048]{3,2,1,0:T(8,128)(2,1)S(1)} %get-tuple-element.59) | copy-start | bytes 3145732
  618.4 40.5 %copy-start.30 = (bf16[8,1,32,2048]{3,2,1,0:T(8,128)(2,1)}, bf16[8,1,32,2048]{3,2,1,0:T(8,128)(2,1)S(1)}, u32[]{:S(2)}) copy-start(bf16[8,1,32,2048]{3,2,1,0:T(8,128)(2,1)S(1)} %get-tuple-element.60) | copy-start | bytes 3145732
  797.1 22.5 %copy-start.47 = (bf16[8,1,32,2048]{3,2,1,0:T(8,128)(2,1)}, bf16[8,1,32,2048]{3,2,1,0:T(8,128)(2,1)S(1)}, u32[]{:S(2)}) copy-start(bf16[8,1,32,2048]{3,2,1,0:T(8,128)(2,1)S(1)} %get-tuple-element.50) | copy-start | bytes 3145732
  797.2 26.4 %copy-start.49 = (bf16[8,1,32,2048]{3,2,1,0:T(8,128)(2,1)}, bf16[8,1,32,2048]{3,2,1,0:T(8,128)(2,1)S(1)}, u32[]{:S(2)}) copy-start(bf16[8,1,32,2048]{3,2,1,0:T(8,128)(2,1)S(1)} %get-tuple-element.51) | copy-start | bytes 3145732
  797.2 30.6 %copy-start.51 = (bf16[8,1,32,2048]{3,2,1,0:T(8,128)(2,1)}, bf16[8,1,32,2048]{3,2,1,0:T(8,128)(2,1)S(1)}, u32[]{:S(2)}) copy-start(bf16[8,1,32,2048]{3,2,1,0:T(8,128)(2,1)S(1)} %get-tuple-element.52) | copy-start | bytes 3145732
  801.9 31.9 %copy-start.76 = (bf16[256,352]{0,1:T(8,128)(2,1)}, bf16[256,352]{0,1:T(8,128)(2,1)S(1)}, u32[]{:S(2)}) copy-start(bf16[256,352]{0,1:T(8,128)(2,1)S(1)} %get-tuple-element.71) | copy-start | bytes 540676
  801.9 69.8 %copy-start.108 = (bf16[256,352]{0,1:T(8,128)(2,1)}, bf16[256,352]{0,1:T(8,128)(2,1)S(1)}, u32[]{:S(2)}) copy-start(bf16[256,352]{0,1:T(8,128)(2,1)S(1)} %get-tuple-element.73) | copy-start | bytes 540676
  807.1 27.3 %copy-start.78 = (bf16[256,352]{0,1:T(8,128)(2,1)}, bf16[256,352]{0,1:T(8,128)(2,1)S(1)}, u32[]{:S(2)}) copy-start(bf16[256,352]{0,1:T(8,128)(2,1)S(1)} %get-tuple-element.68) | copy-start | bytes 540676
  811.0 24.2 %copy-start.80 = (bf16[256,352]{0,1:T(8,128)(2,1)}, bf16[256,352]{0,1:T(8,128)(2,1)S(1)}, u32[]{:S(2)}) copy-start(bf16[256,352]{0,1:T(8,128)(2,1)S(1)} %get-tuple-element.74) | copy-start | bytes 540676
  846.6 221.7 %all-to-all-start.3 = ((bf16[8,8,32,2048]{3,2,1,0:T(8,128)(2,1)}), bf16[8,8,32,2048]{3,2,1,0:T(8,128)(2,1)}, u32[]{:S(2)}, u32[]{:S(2)}) async-start(bf16[8,8,32,2048]{3,2,1,0:T(8,128)(2,1)} %constant_dynamic-update-slice_fusion.8), calls=%async_computation.3 | async-start | bytes 16777216 | tf_op jit(solution)/shard_map/all_to_all | solution.py:406
  851.6 224.9 %all-gather.23.cloned.1.call-start = ((), (), s32[]{:S(2)}) async-start(), calls=%async_computation.20 | async-start | bytes 3244032 | tf_op jit(solution)/shard_map/all_gather | solution.py:292
  1068.4 280.1 %all-to-all-start.1 = ((bf16[8,8,32,2048]{3,2,1,0:T(8,128)(2,1)}), bf16[8,8,32,2048]{3,2,1,0:T(8,128)(2,1)}, u32[]{:S(2)}, u32[]{:S(2)}) async-start(bf16[8,8,32,2048]{3,2,1,0:T(8,128)(2,1)} %constant_dynamic-update-slice_fusion), calls=%async_computation.1 | async-start | bytes 16777216 | tf_op jit(solution)/shard_map/all_to_all | solution.py:358
  1073.3 184.3 %all-gather.21.cloned.1.call-start = ((), (), s32[]{:S(2)}) async-start(), calls=%async_computation.19 | async-start | bytes 3244032 | tf_op jit(solution)/shard_map/all_gather | solution.py:291
  1074.1 251.0 %all-gather.25.cloned.1.call-start = ((), (), s32[]{:S(2)}) async-start(), calls=%async_computation.21 | async-start | bytes 3244032 | tf_op jit(solution)/shard_map/all_gather | solution.py:293
  1074.8 385.0 %all-reduce.16.cloned.1.call-start = ((), (), s32[]{:S(2)}) async-start(), calls=%async_computation.22 | async-start | bytes 2097152 | tf_op jit(solution)/shard_map/psum | solution.py:427
  1328.6 101.2 %copy-start.57 = (bf16[256,704]{0,1:T(8,128)(2,1)}, bf16[256,704]{0,1:T(8,128)(2,1)S(1)}, u32[]{:S(2)}) copy-start(bf16[256,704]{0,1:T(8,128)(2,1)S(1)} %get-tuple-element.63) | copy-start | bytes 1081348
  1396.5 25.7 %copy-start.121 = (bf16[256,64]{0,1:T(8,128)(2,1)}, bf16[256,64]{0,1:T(8,128)(2,1)S(1)}, u32[]{:S(2)}) copy-start(bf16[256,64]{0,1:T(8,128)(2,1)S(1)} %select_reduce_fusion.3) | copy-start | bytes 98308
  1424.4 112.9 %reduce-scatter.18.cloned.1.call-start = ((), (), s32[]{:S(2)}) async-start(), calls=%async_computation.27 | async-start | bytes 3244032 | tf_op jit(solution)/shard_map/reduce_scatter | solution.py:494
  1426.9 186.5 %reduce-scatter.16.cloned.1.call-start = ((), (), s32[]{:S(2)}) async-start(), calls=%async_computation.26 | async-start | bytes 3244032 | tf_op jit(solution)/shard_map/reduce_scatter | solution.py:491
  1429.7 260.1 %reduce-scatter.20.cloned.1.call-start = ((), (), s32[]{:S(2)}) async-start(), calls=%async_computation.28 | async-start | bytes 3244032 | tf_op jit(solution)/shard_map/reduce_scatter | solution.py:497
  1432.2 27.6 %copy-start.1 = (bf16[256,2048]{1,0:T(8,128)(2,1)S(1)}, bf16[256,2048]{1,0:T(8,128)(2,1)}, u32[]{:S(2)}) copy-start(bf16[256,2048]{1,0:T(8,128)(2,1)} %param.20) | copy-start | bytes 3145732
  1432.2 27.6 %copy-start.4 = (bf16[256,2048]{1,0:T(8,128)(2,1)S(1)}, bf16[256,2048]{1,0:T(8,128)(2,1)}, u32[]{:S(2)}) copy-start(bf16[256,2048]{1,0:T(8,128)(2,1)} %all-reduce.14.cloned.1.call-done) | copy-start | bytes 3145732
  1432.2 27.6 %copy-start.134 = (f32[8,1,256]{2,1,0:T(1,128)S(1)}, f32[8,1,256]{2,1,0:T(1,128)}, u32[]{:S(2)}) copy-start(f32[8,1,256]{2,1,0:T(1,128)} %copy-done.133) | copy-start | bytes 24580
  1432.3 27.6 %copy-start.167 = (f32[256]{0:T(256)S(1)}, f32[256]{0:T(256)}, u32[]{:S(2)}) copy-start(f32[256]{0:T(256)} %copy-done.166) | copy-start | bytes 3076
  1432.3 330.2 %reduce-scatter.24.cloned.1.call-start = ((), (), s32[]{:S(2)}) async-start(), calls=%async_computation.30 | async-start | bytes 2654208 | tf_op jit(solution)/shard_map/reduce_scatter | solution.py:476
  1432.9 41.3 %copy-start.162 = (f32[4,256]{1,0:T(4,128)}, f32[4,256]{1,0:T(4,128)S(1)}, u32[]{:S(2)}) copy-start(f32[4,256]{1,0:T(4,128)S(1)} %log_add_fusion) | copy-start | bytes 12292
  1480.6 402.6 %reduce-scatter.22.cloned.1.call-start = ((), (), s32[]{:S(2)}) async-start(), calls=%async_computation.29 | async-start | bytes 7077888 | tf_op jit(solution)/shard_map/reduce_scatter | solution.py:473
  1493.3 455.4 %reduce-scatter.26.cloned.1.call-start = ((), (), s32[]{:S(2)}) async-start(), calls=%async_computation.31 | async-start | bytes 294912 | tf_op jit(solution)/shard_map/reduce_scatter | solution.py:479
  1495.1 520.1 %reduce-scatter.12.cloned.1.call-start = ((), (), s32[]{:S(2)}) async-start(), calls=%async_computation.24 | async-start | bytes 1179648 | tf_op jit(solution)/shard_map/reduce_scatter | solution.py:485
  1498.0 588.2 %reduce-scatter.14.cloned.1.call-start = ((), (), s32[]{:S(2)}) async-start(), calls=%async_computation.25 | async-start | bytes 2359296 | tf_op jit(solution)/shard_map/reduce_scatter | solution.py:488
  1501.2 657.2 %reduce-scatter.10.cloned.1.call-start = ((), (), s32[]{:S(2)}) async-start(), calls=%async_computation.23 | async-start | bytes 2654208 | tf_op jit(solution)/shard_map/reduce_scatter | solution.py:482
  1724.4 505.4 %all-reduce.18.cloned.1.call-start = ((), (), s32[]{:S(2)}) async-start(), calls=%async_computation.32 | async-start | bytes 6356992 | tf_op jit(solution)/shard_map/psum | solution.py:372
  1750.5 132.7 %copy-start.75 = (bf16[256,352]{0,1:T(8,128)(2,1)S(1)}, bf16[256,352]{0,1:T(8,128)(2,1)}, u32[]{:S(2)}) copy-start(bf16[256,352]{0,1:T(8,128)(2,1)} %copy-done.74) | copy-start | bytes 540676
  (159 other events, 669.9 us)
Sparse Core Ops, SparseCore 0:
  10.1 56.4 all-gather.10
  68.7 38.4 all-gather.12
  109.4 97.3 all-gather.14
  208.9 49.9 all-gather.16
  260.8 48.8 all-gather.18
  313.2 34.8 all-reduce.13
  854.5 182.0 all-gather.22
  1076.2 181.4 all-gather.20
  1259.7 65.3 all-gather.24
  1424.5 35.3 all-reduce.15
  1464.0 73.1 reduce-scatter.17
  1541.2 72.2 reduce-scatter.15
  1617.6 72.1 reduce-scatter.19
  1693.1 69.3 reduce-scatter.23
  1765.9 117.2 reduce-scatter.21
  1886.9 61.7 reduce-scatter.25
  1952.0 63.2 reduce-scatter.11
  2018.6 67.5 reduce-scatter.13
  2089.8 68.5 reduce-scatter.9
  2161.4 68.2 all-reduce.17
where the time goes:
time: 2250 us; the launch traced here: 2240 us
  waiting for transfers between devices  1430 us (64%)
  blocking collectives  288 us (13%)
  matrix products  230 us (10%)
  local copies, waits for them, and re-layouts  163 us (7%)
  other arithmetic  95 us (4%)
    dot_general x99, matrix products, matmul(): return jnp.dot(left, right, preferred_element_type=jnp.float32)  220 us
    all_to_all x1, waiting for transfers between devices, body(): lax.all_to_all(stacked_back, 'expert', split_axis=0, concat_axis=0, tiled...  190 us
    all_gather x1, waiting for transfers between devices, body(): lax.all_gather(shared_gate, 'expert', axis=0, tiled=True)  178 us
    all_gather x1, blocking collectives, body(): lax.all_gather(router, 'expert', axis=0, tiled=True)  177 us
    all_to_all x1, waiting for transfers between devices, body(): lax.all_to_all(outgoing_grad, 'expert', split_axis=0, concat_axis=0, tile...  131 us
    reduce_scatter x1, waiting for transfers between devices, body(): lax.psum_scatter(summed[2].astype(jnp.bfloat16), 'expert', scatter_dimens...  121 us
    all_gather x1, waiting for transfers between devices, body(): lax.all_gather(query_down, 'expert', axis=0, tiled=True)  96.6 us
    reduce_scatter x1, waiting for transfers between devices, body(): lax.psum_scatter(grad_shared_down.astype(jnp.bfloat16), 'expert', scatter...  74.4 us
  transfers between devices with their start and end apart: 24, of which 20 were waited for; matrix products, arithmetic and copies ran while one was open for 14% of the time, Pallas kernels for 0%

commit v1 on v0

v1 whole, which is shorter than its diff:
```python
import functools
import math

import jax
import jax.numpy as jnp
from jax import lax
from jax.experimental import pallas as pl
from jax.experimental.pallas import tpu as pltpu
from jax.sharding import PartitionSpec as P

NOPE = 128
ROPE = 64
VD = 128
CAP = 32
LANES = 128
VMEM_BYTES = 60 * 2**20

EPSILON = 1e-06
ROPE_BASE = 50000.0
ROUTE_SCALE = 2.446


def matmul(left, right):
    return jnp.dot(left, right, preferred_element_type=jnp.float32)


def contract(form, left, right):
    return jnp.einsum(form, left, right, preferred_element_type=jnp.float32)


def matmul_nt(left, right):
    return lax.dot_general(left, right, (((1,), (1,)), ((), ())), preferred_element_type=jnp.float32)


def matmul_tn(left, right):
    return lax.dot_general(left, right, (((0,), (0,)), ((), ())), preferred_element_type=jnp.float32)


def rms_forward(values, gain):
    inverse = lax.rsqrt(jnp.mean(values * values, axis=-1, keepdims=True) + EPSILON)
    return (values * inverse * gain, inverse)


def rms_backward(values, inverse, gain, cotangent):
    scaled = cotangent * gain
    normed = values * inverse
    return inverse * (scaled - normed * jnp.mean(scaled * normed, axis=-1, keepdims=True))


def gain_gradient(values, inverse, cotangent):
    return jnp.sum(cotangent * (values * inverse), axis=0)


def rotate(values, cosine, sinusoid):
    half_width = values.shape[-1] // 2
    leading = values[..., :half_width]
    trailing = values[..., half_width:]
    return jnp.concatenate(
        [leading * cosine - trailing * sinusoid, trailing * cosine + leading * sinusoid], axis=-1
    )


def rotate_back(values, cosine, sinusoid):
    return rotate(values, cosine, -sinusoid)


def layout(lengths, row_count):
    doc_count = lengths.shape[0]
    doc_ends = jnp.cumsum(lengths)
    starts = doc_ends - lengths
    row_index = jnp.arange(row_count, dtype=jnp.int32)
    doc_ids = jnp.sum((row_index[:, None] >= doc_ends[None, :]).astype(jnp.int32), axis=1)
    owners = doc_ids[:, None] == jnp.arange(doc_count, dtype=jnp.int32)[None, :]
    first_row = jnp.sum(jnp.where(owners, starts[None, :], 0), axis=1)
    positions = (row_index - first_row).astype(jnp.float32)
    allowed = (doc_ids[:, None] == doc_ids[None, :]) & (row_index[None, :] <= row_index[:, None])
    frequency = jnp.exp(
        -math.log(ROPE_BASE) * 2.0 * jnp.arange(ROPE // 2, dtype=jnp.float32) / ROPE
    )
    angles = positions[:, None] * frequency[None, :]
    return (allowed, jnp.cos(angles), jnp.sin(angles))


def heads_forward(query_n, latent_n, key_rope, query_up, latent_up, allowed, cosine, sinusoid):
    row_count = query_n.shape[0]
    head_width = NOPE + ROPE
    head_count = query_up.shape[1] // head_width
    queries = matmul(query_n, query_up).reshape(row_count, head_count, head_width)
    queries = jnp.concatenate(
        [
            queries[..., :NOPE],
            rotate(queries[..., NOPE:], cosine[:, None, :], sinusoid[:, None, :]),
        ],
        axis=-1,
    ).astype(jnp.bfloat16)
    keyval = matmul(latent_n, latent_up).reshape(row_count, head_count, NOPE + VD)
    key_rows = jnp.concatenate(
        [keyval[..., :NOPE], jnp.broadcast_to(key_rope[:, None, :], (row_count, head_count, ROPE))],
        axis=-1,
    ).astype(jnp.bfloat16)
    value_rows = keyval[..., NOPE:].astype(jnp.bfloat16)
    scores = contract("qhc,khc->hqk", queries, key_rows) * head_width ** (-0.5)
    scores = jnp.where(allowed[None], scores, -1e30)
    row_peak = jnp.max(scores, axis=-1, keepdims=True)
    powers = jnp.exp(scores - row_peak)
    totals = jnp.sum(powers, axis=-1, keepdims=True)
    logsum = row_peak + jnp.log(totals)
    attn_probs = (powers / totals).astype(jnp.bfloat16)
    attended = (
        contract("hqk,khc->qhc", attn_probs, value_rows)
        .reshape(row_count, head_count * VD)
        .astype(jnp.bfloat16)
    )
    return (attended, logsum, queries, key_rows, value_rows)


def heads_backward(
    attended_grad,
    logsum,
    queries,
    key_rows,
    value_rows,
    query_n,
    latent_n,
    query_up,
    latent_up,
    allowed,
    cosine,
    sinusoid,
):
    row_count = queries.shape[0]
    head_count = queries.shape[1]
    head_width = NOPE + ROPE
    attended_rows = attended_grad.reshape(row_count, head_count, VD)
    scores = contract("qhc,khc->hqk", queries, key_rows) * head_width ** (-0.5)
    attn_probs = jnp.where(allowed[None], jnp.exp(scores - logsum), 0.0)
    dvalues = contract("hqk,qhc->khc", attn_probs.astype(jnp.bfloat16), attended_rows)
    dprobs = contract("qhc,khc->hqk", attended_rows, value_rows)
    row_delta = jnp.sum(attn_probs * dprobs, axis=-1, keepdims=True)
    dscores = (attn_probs * (dprobs - row_delta) * head_width ** (-0.5)).astype(jnp.bfloat16)
    dquery = contract("hqk,khc->qhc", dscores, key_rows)
    dkey_rows = contract("hqk,qhc->khc", dscores, queries)
    dquery = jnp.concatenate(
        [
            dquery[..., :NOPE],
            rotate_back(dquery[..., NOPE:], cosine[:, None, :], sinusoid[:, None, :]),
        ],
        axis=-1,
    )
    dquery = dquery.reshape(row_count, head_count * head_width).astype(jnp.bfloat16)
    dkey_rope = rotate_back(jnp.sum(dkey_rows[..., NOPE:], axis=1), cosine, sinusoid)
    dkeyval = (
        jnp.concatenate([dkey_rows[..., :NOPE], dvalues], axis=-1)
        .reshape(row_count, head_count * (NOPE + VD))
        .astype(jnp.bfloat16)
    )
    grad_query_up = matmul(query_n.T, dquery)
    grad_latent_up = matmul(latent_n.T, dkeyval)
    dquery_n = matmul(dquery, query_up.T)
    dlatent_n = matmul(dkeyval, latent_up.T)
    return (dquery_n, dlatent_n, dkey_rope, grad_query_up, grad_latent_up)


def swiglu(gate_pre, up_pre):
    sigmoid_gate = jax.nn.sigmoid(gate_pre)
    return (sigmoid_gate, (gate_pre * sigmoid_gate * up_pre).astype(jnp.bfloat16))


def swiglu_back(dhidden, gate_pre, up_pre, sigmoid_gate):
    gate_grad = dhidden * up_pre * sigmoid_gate * (1.0 + gate_pre * (1.0 - sigmoid_gate))
    up_grad = dhidden * gate_pre * sigmoid_gate
    return (gate_grad.astype(jnp.bfloat16), up_grad.astype(jnp.bfloat16))


def expert_kernel(
    x_ref, g_ref, w_ref, gate_ref, up_ref, down_ref, y_ref, dr_ref, dw_ref, gg_ref, gu_ref, gd_ref
):
    blocks, _, cap, width = x_ref.shape
    rows = blocks * cap
    row_inputs = x_ref[...].reshape(rows, width)
    gradient = g_ref[...].reshape(rows, width).astype(jnp.float32)
    weight = w_ref[...].reshape(rows, 1)
    gate, up, down = gate_ref[0], up_ref[0], down_ref[0]
    gate_pre = matmul_nt(row_inputs, gate)
    up_pre = matmul_nt(row_inputs, up)
    sigmoid_gate, hidden = swiglu(gate_pre, up_pre)
    produced = matmul(hidden, down)
    dw_ref[...] = jnp.sum(gradient * produced, axis=1, keepdims=True).reshape(dw_ref.shape)
    y_ref[...] = (weight * produced).astype(jnp.bfloat16).reshape(y_ref.shape)
    cotangent = (weight * gradient).astype(jnp.bfloat16)
    dhidden = matmul_nt(cotangent, down)
    gate_grad, up_grad = swiglu_back(dhidden, gate_pre, up_pre, sigmoid_gate)
    back = matmul(gate_grad, gate) + matmul(up_grad, up)
    dr_ref[...] = back.astype(jnp.bfloat16).reshape(dr_ref.shape)
    first = pl.program_id(1) == 0

    def accumulate(ref, left, right):
        part = matmul_tn(left, right)

        @pl.when(first)
        def _():
            ref[0] = part

        @pl.when(jnp.logical_not(first))
        def _():
            ref[0] += part

    accumulate(gg_ref, gate_grad, row_inputs)
    accumulate(gu_ref, up_grad, row_inputs)
    accumulate(gd_ref, hidden, cotangent)


def expert_stage(row_inputs, gradients, weights, gate_t, up_t, down):
    blocks, local, cap, width = row_inputs.shape
    units = gate_t.shape[1]
    step = min(blocks, 256 // cap)
    rows_spec = pl.BlockSpec((step, 1, cap, width), lambda j, r: (r, j, 0, 0))
    slot_spec = pl.BlockSpec((step, 1, cap, 1), lambda j, r: (r, j, 0, 0))
    unit_spec = pl.BlockSpec((1, units, width), lambda j, r: (j, 0, 0))
    rows_shape = jax.ShapeDtypeStruct(row_inputs.shape, jnp.bfloat16)
    unit_shape = jax.ShapeDtypeStruct((local, units, width), jnp.float32)
    flops = 18 * blocks * local * cap * width * units
    moved = 8 * blocks * local * cap * width + 18 * local * units * width
    return pl.pallas_call(
        expert_kernel,
        grid=(local, blocks // step),
        in_specs=[rows_spec, rows_spec, slot_spec, unit_spec, unit_spec, unit_spec],
        out_specs=[rows_spec, rows_spec, slot_spec, unit_spec, unit_spec, unit_spec],
        out_shape=[
            rows_shape,
            rows_shape,
            jax.ShapeDtypeStruct((blocks, local, cap, 1), jnp.float32),
            unit_shape,
            unit_shape,
            unit_shape,
        ],
        compiler_params=pltpu.CompilerParams(vmem_limit_bytes=VMEM_BYTES),
        cost_estimate=pl.CostEstimate(flops=flops, bytes_accessed=moved, transcendentals=0),
        name="experts",
    )(row_inputs, gradients, weights, gate_t, up_t, down)


def combine_kernel(
    p_ref, y_ref, dr_ref, dw_ref, x_ref, g_ref, shared_ref, out_ref, ds_ref, grad_ref
):
    picks = p_ref[0]
    row_inputs, cotangent = x_ref[0], g_ref[0]
    gate, up, down = shared_ref[0], shared_ref[1], shared_ref[2]
    gate_pre = matmul_nt(row_inputs, gate)
    up_pre = matmul_nt(row_inputs, up)
    sigmoid_gate, hidden = swiglu(gate_pre, up_pre)
    out_ref[0] = (matmul_tn(picks, y_ref[0]) + matmul(hidden, down)).astype(jnp.bfloat16)
    dhidden = matmul_nt(cotangent, down)
    gate_grad, up_grad = swiglu_back(dhidden, gate_pre, up_pre, sigmoid_gate)
    back = matmul_tn(picks, dr_ref[0]) + matmul(gate_grad, gate) + matmul(up_grad, up)
    width = back.shape[1]
    ds_ref[0, :, :width] = back.astype(jnp.bfloat16)
    ds_ref[0, :, width:] = matmul_tn(picks, dw_ref[0]).astype(jnp.bfloat16)
    first = pl.program_id(0) == 0
    for index, (left, right) in enumerate(
        ((gate_grad, row_inputs), (up_grad, row_inputs), (hidden, cotangent))
    ):
        part = matmul_tn(left, right)

        @pl.when(first)
        def _(index=index, part=part):
            grad_ref[index] = part

        @pl.when(jnp.logical_not(first))
        def _(index=index, part=part):
            grad_ref[index] += part


def combine_stage(picks, produced, back, spread, tokens, gradients, shared):
    blocks, slots, rows = picks.shape
    width = tokens.shape[-1]
    slot_spec = pl.BlockSpec((1, slots, width), lambda b: (b, 0, 0))
    rows_spec = pl.BlockSpec((1, rows, width), lambda b: (b, 0, 0))
    whole = pl.BlockSpec(shared.shape, lambda b: (0, 0, 0))
    lanes = spread.shape[-1]
    units = shared.shape[1]
    flops = 4 * blocks * slots * rows * width + 18 * blocks * rows * width * units
    moved = 4 * blocks * slots * width + 8 * blocks * rows * width
    return pl.pallas_call(
        combine_kernel,
        grid=(blocks,),
        in_specs=[
            pl.BlockSpec((1, slots, rows), lambda b: (b, 0, 0)),
            slot_spec,
            slot_spec,
            pl.BlockSpec((1, slots, lanes), lambda b: (b, 0, 0)),
            rows_spec,
            rows_spec,
            whole,
        ],
        out_specs=[
            rows_spec,
            pl.BlockSpec((1, rows, width + lanes), lambda b: (b, 0, 0)),
            whole,
        ],
        out_shape=[
            jax.ShapeDtypeStruct((blocks, rows, width), jnp.bfloat16),
            jax.ShapeDtypeStruct((blocks, rows, width + lanes), jnp.bfloat16),
            jax.ShapeDtypeStruct(shared.shape, jnp.float32),
        ],
        compiler_params=pltpu.CompilerParams(vmem_limit_bytes=VMEM_BYTES),
        cost_estimate=pl.CostEstimate(flops=flops, bytes_accessed=moved, transcendentals=0),
        name="combine",
    )(picks, produced, back, spread, tokens, gradients, shared)


MESH = pl.DeviceIdType.MESH
PAIR = 2
ANY = pl.BlockSpec(memory_space=pl.ANY)
IN_VMEM = pl.BlockSpec(memory_space=pltpu.VMEM)
DMA = pltpu.SemaphoreType.DMA


def place():
    me, part = lax.axis_index("expert"), lax.axis_index("tensor")
    return (me // PAIR, me % PAIR, part // PAIR, part % PAIR)


def device(z, x, y, c):
    return {"expert": z * PAIR + x, "tensor": y * PAIR + c}


def greet(peers):
    barrier = pltpu.get_barrier_semaphore()
    for peer in peers:
        pl.semaphore_signal(barrier, inc=1, device_id=peer, device_id_type=MESH)
    pl.semaphore_wait(barrier, len(peers))


def push(source, target, send, arrive, peer):
    copy = pltpu.make_async_remote_copy(
        src_ref=source,
        dst_ref=target,
        send_sem=send,
        recv_sem=arrive,
        device_id=peer,
        device_id_type=MESH,
    )
    copy.start()
    return copy


def bring(source, target, done):
    copy = pltpu.make_async_copy(source, target, done)
    copy.start()
    return copy


def arrived(target, done):
    pltpu.make_async_copy(target, target, done).wait()


def slot(ref, axis, index, size):
    start = pl.multiple_of(index * size, size)
    if axis == 0:
        return ref.at[pl.ds(start, size), :]
    return ref.at[:, pl.ds(start, size)]


class Calls:
    def __init__(self):
        self.count = 0

    def params(self):
        self.count += 1
        return pltpu.CompilerParams(
            collective_id=self.count, has_side_effects=True, vmem_limit_bytes=VMEM_BYTES
        )


def gather_expert_kernel(deep, axes, cuts, *refs):
    count = len(axes)
    sources, targets = list(refs[:count]), refs[count : 2 * count]
    held, (send, arrive, own) = refs[2 * count : 3 * count], refs[3 * count :]
    z, x, y, c = place()
    part = y * PAIR + c
    for i, cut in enumerate(cuts):
        if cut is not None:
            sources[i] = slot(sources[i], cut[0], part, cut[1])
    sizes = [h.shape[axis] for h, axis in zip(held, axes)]

    def at(i, from_z, from_x):
        return slot(targets[i], axes[i], from_z * PAIR + from_x, sizes[i])

    others = [device((z + k) % deep, x, y, c) for k in range(1, deep)]
    twin = device(z, 1 - x, y, c)
    greet(others + [twin])
    copies = []
    loads = [bring(sources[i], held[i], own.at[i]) for i in range(count)]
    for i in range(count):
        for k in range(1, deep):
            copies.append(
                push(sources[i], at(i, z, x), send.at[i, k], arrive.at[i, k], others[k - 1])
            )
        copies.append(push(sources[i], at(i, z, x), send.at[i, 0], arrive.at[i, 0], twin))
    stores = []
    for i in range(count):
        loads[i].wait()
        stores.append(bring(held[i], at(i, z, x), own.at[i]))
    for i in range(count):
        for k in range(1, deep):
            piece = at(i, (z + deep - k) % deep, x)
            arrived(piece, arrive.at[i, k])
            copies.append(
                push(piece, piece, send.at[i, deep + k], arrive.at[i, deep + k], twin)
            )
    for i in range(count):
        arrived(at(i, z, 1 - x), arrive.at[i, 0])
        for k in range(1, deep):
            arrived(at(i, (z + deep - k) % deep, 1 - x), arrive.at[i, deep + k])
    for copy in copies:
        copy.wait_send()
    for store in stores:
        store.wait()


def gather_expert(calls, groups, arrays, axes, cuts):
    deep = groups // PAIR
    held, shapes = [], []
    for array, axis, cut in zip(arrays, axes, cuts):
        shape = list(array.shape)
        if cut is not None:
            shape[cut[0]] = cut[1]
        held.append(pltpu.VMEM(tuple(shape), array.dtype))
        shape[axis] *= groups
        shapes.append(jax.ShapeDtypeStruct(tuple(shape), array.dtype))
    count = len(arrays)
    return pl.pallas_call(
        functools.partial(gather_expert_kernel, deep, tuple(axes), tuple(cuts)),
        in_specs=[ANY] * count,
        out_specs=[ANY] * count,
        out_shape=shapes,
        scratch_shapes=held
        + [DMA((count, 2 * deep)), DMA((count, 2 * deep)), DMA((count,))],
        compiler_params=calls.params(),
        name="gather_expert",
    )(*arrays)


def gather_tensor_kernel(axes, *refs):
    count = len(axes)
    sources, targets = refs[:count], refs[count : 2 * count]
    held, (send, arrive, own) = refs[2 * count : 3 * count], refs[3 * count :]
    z, x, y, c = place()
    sizes = [h.shape[axis] for h, axis in zip(held, axes)]

    def at(i, from_y, from_c):
        return slot(targets[i], axes[i], from_y * PAIR + from_c, sizes[i])

    across, beside = device(z, x, 1 - y, c), device(z, x, y, 1 - c)
    greet([across, beside])
    copies = []
    loads = [bring(sources[i], held[i], own.at[i]) for i in range(count)]
    for i in range(count):
        mine = at(i, y, c)
        copies.append(push(sources[i], mine, send.at[i, 0], arrive.at[i, 0], across))
        copies.append(push(sources[i], mine, send.at[i, 1], arrive.at[i, 1], beside))
    stores = []
    for i in range(count):
        loads[i].wait()
        stores.append(bring(held[i], at(i, y, c), own.at[i]))
    for i in range(count):
        piece = at(i, 1 - y, c)
        arrived(piece, arrive.at[i, 0])
        copies.append(push(piece, piece, send.at[i, 2], arrive.at[i, 2], beside))
    for i in range(count):
        arrived(at(i, y, 1 - c), arrive.at[i, 1])
        arrived(at(i, 1 - y, 1 - c), arrive.at[i, 2])
    for copy in copies:
        copy.wait_send()
    for store in stores:
        store.wait()


def gather_tensor(calls, parts, arrays, axes):
    shapes = []
    for array, axis in zip(arrays, axes):
        shape = list(array.shape)
        shape[axis] *= parts
        shapes.append(jax.ShapeDtypeStruct(tuple(shape), array.dtype))
    count = len(arrays)
    return pl.pallas_call(
        functools.partial(gather_tensor_kernel, tuple(axes)),
        in_specs=[ANY] * count,
        out_specs=[ANY] * count,
        out_shape=shapes,
        scratch_shapes=[pltpu.VMEM(a.shape, a.dtype) for a in arrays]
        + [DMA((count, 3)), DMA((count, 3)), DMA((count,))],
        compiler_params=calls.params(),
        name="gather_tensor",
    )(*arrays)


def add_rows(count, store):
    lax.fori_loop(0, count, lambda i, carry: (store(i), carry)[1], 0)


def sum_tensor_kernel(p_ref, o_ref, own_buf, from_beside, out_buf, from_across, send, arrive, own):
    z, x, y, c = place()
    rows = o_ref.shape[0]
    across, beside = device(z, x, 1 - y, c), device(z, x, y, 1 - c)
    greet([across, beside])
    first = push(p_ref.at[:, 1 - c], from_beside, send.at[0], arrive.at[0], beside)
    load = bring(p_ref.at[:, c], own_buf, own.at[0])
    load.wait()
    arrived(from_beside, arrive.at[0])
    step = 16

    def add(at, target, give):
        span = pl.ds(pl.multiple_of(at * step, step), step)
        total = own_buf[give, span, :].astype(jnp.float32) + from_beside[
            give, span, :
        ].astype(jnp.float32)
        target[span, :] = total.astype(target.dtype)

    add_rows(rows // step, lambda i: add(i, out_buf, 1 - y))
    second = push(out_buf, from_across, send.at[1], arrive.at[1], across)
    add_rows(rows // step, lambda i: add(i, o_ref, y))
    arrived(from_across, arrive.at[1])

    def finish(at):
        span = pl.ds(pl.multiple_of(at * step, step), step)
        o_ref[span, :] = o_ref[span, :] + from_across[span, :].astype(jnp.float32)

    add_rows(rows // step, finish)
    first.wait_send()
    second.wait_send()


def sum_tensor(calls, parts, partial):
    rows, width = partial.shape[0] // parts, partial.shape[1]
    half = parts // PAIR
    buf = pltpu.VMEM((half, rows, width), jnp.bfloat16)
    one = pltpu.VMEM((rows, width), jnp.bfloat16)
    return pl.pallas_call(
        sum_tensor_kernel,
        in_specs=[ANY],
        out_specs=IN_VMEM,
        out_shape=jax.ShapeDtypeStruct((rows, width), jnp.float32),
        scratch_shapes=[buf, buf, one, one, DMA((2,)), DMA((2,)), DMA((1,))],
        compiler_params=calls.params(),
        name="sum_tensor",
    )(partial.astype(jnp.bfloat16).reshape(half, PAIR, rows, width))


def gather_all_kernel(deep, streams, count, *refs):
    sources, targets = refs[:count], refs[count : 2 * count]
    held, (send, arrive, own) = refs[2 * count : 3 * count], refs[3 * count :]
    z, x, y, c = place()

    def at(s, from_z, from_x, from_y, from_c):
        i, left, wide, _ = streams[s]
        rows = held[i].shape[0]
        index = ((from_z * PAIR + from_x) * PAIR + from_y) * PAIR + from_c
        start = pl.multiple_of(index * rows, rows)
        return targets[i].at[pl.ds(start, rows), pl.ds(left, wide)]

    others = [device((z + k) % deep, x, y, c) for k in range(1, deep)]
    twin, across, beside = (
        device(z, 1 - x, y, c),
        device(z, x, 1 - y, c),
        device(z, x, y, 1 - c),
    )
    greet(others + [twin, across, beside])
    copies = []
    loads = [bring(sources[i], held[i], own.at[i]) for i in range(count)]

    def forward(s, number, peer, source, target):
        copies.append(push(source, target, send.at[s, number], arrive.at[s, number], peer))

    first = [twin if order == 0 else across for _, _, _, order in streams]
    second = [across if order == 0 else twin for _, _, _, order in streams]

    def piece(s, k, flip_first, flip_second, flip_core):
        order = streams[s][3]
        flip_x, flip_y = (
            (flip_first, flip_second) if order == 0 else (flip_second, flip_first)
        )
        return at(
            s,
            (z + deep - k) % deep,
            1 - x if flip_x else x,
            1 - y if flip_y else y,
            1 - c if flip_core else c,
        )

    for s in range(len(streams)):
        i, left, wide, _ = streams[s]
        source = sources[i].at[:, pl.ds(left, wide)]
        mine = piece(s, 0, False, False, False)
        for k in range(1, deep):
            forward(s, k, others[k - 1], source, mine)
        forward(s, deep, first[s], source, mine)
        forward(s, 2 * deep, second[s], source, mine)
        forward(s, 4 * deep, beside, source, mine)
    for k in range(1, deep):
        for s in range(len(streams)):
            got = piece(s, k, False, False, False)
            arrived(got, arrive.at[s, k])
            forward(s, deep + k, first[s], got, got)
            forward(s, 2 * deep + k, second[s], got, got)
            forward(s, 4 * deep + k, beside, got, got)
    for k in range(deep):
        for s in range(len(streams)):
            got = piece(s, k, True, False, False)
            arrived(got, arrive.at[s, deep + k])
            forward(s, 3 * deep + k, second[s], got, got)
            forward(s, 5 * deep + k, beside, got, got)
    for k in range(deep):
        for s in range(len(streams)):
            got = piece(s, k, False, True, False)
            arrived(got, arrive.at[s, 2 * deep + k])
            forward(s, 6 * deep + k, beside, got, got)
            got = piece(s, k, True, True, False)
            arrived(got, arrive.at[s, 3 * deep + k])
            forward(s, 7 * deep + k, beside, got, got)
    stores = []
    for i in range(count):
        loads[i].wait()
        rows = held[i].shape[0]
        index = ((z * PAIR + x) * PAIR + y) * PAIR + c
        stores.append(bring(held[i], slot(targets[i], 0, index, rows), own.at[i]))
    for k in range(deep):
        for s in range(len(streams)):
            arrived(piece(s, k, False, False, True), arrive.at[s, 4 * deep + k])
            arrived(piece(s, k, True, False, True), arrive.at[s, 5 * deep + k])
            arrived(piece(s, k, False, True, True), arrive.at[s, 6 * deep + k])
            arrived(piece(s, k, True, True, True), arrive.at[s, 7 * deep + k])
    for copy in copies:
        copy.wait_send()
    for store in stores:
        store.wait()


def gather_all(calls, groups, parts, arrays):
    deep = groups // PAIR
    streams = []
    for i, array in enumerate(arrays):
        wide = array.shape[1] // PAIR
        if wide % LANES == 0:
            streams += [(i, 0, wide, 0), (i, wide, wide, 1)]
        else:
            streams.append((i, 0, array.shape[1], 0))
    count = len(arrays)
    shapes = [
        jax.ShapeDtypeStruct((a.shape[0] * groups * parts, a.shape[1]), a.dtype) for a in arrays
    ]
    sems = DMA((len(streams), 8 * deep))
    return pl.pallas_call(
        functools.partial(gather_all_kernel, deep, tuple(streams), count),
        in_specs=[ANY] * count,
        out_specs=[ANY] * count,
        out_shape=shapes,
        scratch_shapes=[pltpu.VMEM(a.shape, a.dtype) for a in arrays]
        + [sems, sems, DMA((count,))],
        compiler_params=calls.params(),
        name="gather_all",
    )(*arrays)


def sum_all_kernel(deep, chunks, count, *refs):
    partials, outs = refs[:count], refs[count : 2 * count]
    total = len(chunks)
    rest = refs[2 * count :]
    own_buf, from_core = rest[:total], rest[total : 2 * total]
    from_first, from_second = rest[2 * total : 3 * total], rest[3 * total : 4 * total]
    from_deep = rest[4 * total : 5 * total]
    send, arrive, own = rest[5 * total :]
    z, x, y, c = place()
    others = [device((z + k) % deep, x, y, c) for k in range(1, deep)]
    twin, across, beside = (
        device(z, 1 - x, y, c),
        device(z, x, 1 - y, c),
        device(z, x, y, 1 - c),
    )
    greet(others + [twin, across, beside])
    copies, loads = [], []
    for n, (i, left, wide, order) in enumerate(chunks):
        span = pl.ds(left, wide)
        copies.append(
            push(
                partials[i].at[:, 1 - c, :, span],
                from_core[n],
                send.at[n, 0],
                arrive.at[n, 0],
                beside,
            )
        )
        loads.append(bring(partials[i].at[:, c, :, span], own_buf[n], own.at[n]))

    def index(order, depth, on_first, on_second):
        on_x, on_y = (on_first, on_second) if order == 0 else (on_second, on_first)
        return (depth * PAIR + on_x) * PAIR + on_y

    def stage_core(n):
        _, _, _, order = chunks[n]
        buf, other = own_buf[n], from_core[n]
        loads[n].wait()
        arrived(other, arrive.at[n, 0])

        def add(k):
            buf[k] = (buf[k].astype(jnp.float32) + other[k].astype(jnp.float32)).astype(
                jnp.bfloat16
            )

        add_rows(deep * PAIR * PAIR, add)
        mine = x if order == 0 else y
        for depth in range(deep):
            for s in range(PAIR):
                number = 1 + depth * PAIR + s
                copies.append(
                    push(
                        buf.at[index(order, depth, 1 - mine, s)],
                        from_first[n].at[depth * PAIR + s],
                        send.at[n, number],
                        arrive.at[n, number],
                        twin if order == 0 else across,
                    )
                )

    def stage_first(n):
        _, _, _, order = chunks[n]
        buf, other = own_buf[n], from_first[n]
        mine, following = (x, y) if order == 0 else (y, x)
        for number in range(1, 1 + PAIR * deep):
            arrived(other.at[number - 1], arrive.at[n, number])

        def add(k):
            at = index(order, k // PAIR, mine, k % PAIR)
            buf[at] = (buf[at].astype(jnp.float32) + other[k].astype(jnp.float32)).astype(
                jnp.bfloat16
            )

        add_rows(deep * PAIR, add)
        for depth in range(deep):
            number = 1 + PAIR * deep + depth
            copies.append(
                push(
                    buf.at[index(order, depth, mine, 1 - following)],
                    from_second[n].at[depth],
                    send.at[n, number],
                    arrive.at[n, number],
                    across if order == 0 else twin,
                )
            )

    def stage_second(n):
        _, _, _, order = chunks[n]
        buf, other = own_buf[n], from_second[n]
        mine, following = (x, y) if order == 0 else (y, x)
        base = 1 + PAIR * deep
        for depth in range(deep):
            arrived(other.at[depth], arrive.at[n, base + depth])

        def add(k):
            at = index(order, k, mine, following)
            buf[at] = (buf[at].astype(jnp.float32) + other[k].astype(jnp.float32)).astype(
                jnp.bfloat16
            )

        add_rows(deep, add)
        for k in range(1, deep):
            number = base + deep + k - 1
            copies.append(
                push(
                    buf.at[index(order, (z + k) % deep, mine, following)],
                    from_deep[n].at[k - 1],
                    send.at[n, number],
                    arrive.at[n, number],
                    others[k - 1],
                )
            )

    def stage_deep(n):
        i, left, wide, order = chunks[n]
        base = 1 + PAIR * deep + deep
        for k in range(1, deep):
            arrived(from_deep[n].at[k - 1], arrive.at[n, base + k - 1])
        mine, following = (x, y) if order == 0 else (y, x)
        result = own_buf[n][index(order, z, mine, following)].astype(jnp.float32)
        for k in range(deep - 1):
            result = result + from_deep[n][k].astype(jnp.float32)
        outs[i][:, pl.ds(left, wide)] = result

    for step in range(total + 3):
        for lag, stage in enumerate((stage_core, stage_first, stage_second, stage_deep)):
            if 0 <= step - lag < total:
                stage(step - lag)
    for copy in copies:
        copy.wait_send()


def sum_all(calls, groups, parts, arrays):
    deep = groups // PAIR
    rows = arrays[0].shape[0] // (groups * parts)
    budget, calls_of, used = 46 * 2**20, [[]], 0
    number = 0
    for i, array in enumerate(arrays):
        left = 0
        while left < array.shape[1]:
            wide = min(512, array.shape[1] - left)
            if 0 < array.shape[1] - left - wide < 512 // 2:
                wide = array.shape[1] - left
            cost = 2 * rows * wide * (4 * deep * 2 + 2 * deep + deep + deep) + 4 * rows * wide
            if used + cost > budget:
                calls_of.append([])
                used = 0
            used += cost
            calls_of[-1].append((i, left, wide, number % 2))
            number += 1
            left += wide
    views = [a.reshape(groups * parts // PAIR, PAIR, rows, a.shape[1]) for a in arrays]
    pieces = [[] for _ in arrays]
    for chunks in calls_of:
        used_arrays = sorted({c[0] for c in chunks})
        bounds = {
            i: (min(c[1] for c in chunks if c[0] == i), sum(c[2] for c in chunks if c[0] == i))
            for i in used_arrays
        }
        local = [(used_arrays.index(i), left, wide, order) for i, left, wide, order in chunks]
        count = len(used_arrays)
        many = deep * PAIR * PAIR

        def bufs(n):
            return [pltpu.VMEM((n, rows, wide), jnp.bfloat16) for _, _, wide, _ in chunks]

        sems = DMA((len(chunks), 1 + PAIR * deep + deep + deep))
        outs = pl.pallas_call(
            functools.partial(
                sum_all_kernel,
                deep,
                tuple(local),
                count,
            ),
            in_specs=[ANY] * count,
            out_specs=[IN_VMEM] * count,
            out_shape=[
                jax.ShapeDtypeStruct((rows, arrays[i].shape[1]), jnp.float32)
                for i in used_arrays
            ],
            scratch_shapes=bufs(many)
            + bufs(many)
            + bufs(PAIR * deep)
            + bufs(deep)
            + bufs(deep - 1)
            + [sems, sems, DMA((len(chunks),))],
            compiler_params=calls.params(),
            name="sum_all",
        )(*[views[i] for i in used_arrays])
        for i, out in zip(used_arrays, outs):
            pieces[i].append(out[:, bounds[i][0] : bounds[i][0] + bounds[i][1]])
    return [p[0] if len(p) == 1 else jnp.concatenate(p, axis=1) for p in pieces]


def sum_expert_kernel(deep, axes, *refs):
    count = len(axes)
    grads, outs = refs[:count], refs[count : 2 * count]
    rest = refs[2 * count :]
    own_buf, from_twin = rest[:count], rest[count : 2 * count]
    from_deep, (send, arrive, own) = rest[2 * count : 3 * count], rest[3 * count :]
    z, x, y, c = place()
    others = [device((z + k) % deep, x, y, c) for k in range(1, deep)]
    twin = device(z, 1 - x, y, c)
    greet(others + [twin])
    sizes = [o.shape[axis] for o, axis in zip(outs, axes)]
    copies, loads = [], []
    for i in range(count):
        loads.append([])
        for k in list(range(1, deep)) + [0]:
            far = (z + k) % deep
            copies.append(
                push(
                    slot(grads[i], axes[i], far * PAIR + 1 - x, sizes[i]),
                    from_twin[i].at[k],
                    send.at[i, k],
                    arrive.at[i, k],
                    twin,
                )
            )
            loads[i].append(
                bring(
                    slot(grads[i], axes[i], far * PAIR + x, sizes[i]),
                    own_buf[i].at[k],
                    own.at[i, k],
                )
            )
    step = 16
    for i in range(count):
        for load in loads[i]:
            load.wait()
        rows = own_buf[i].shape[1]
        for k in list(range(1, deep)) + [0]:
            arrived(from_twin[i].at[k], arrive.at[i, k])
            if k:

                def add(at, i=i, k=k):
                    span = pl.ds(pl.multiple_of(at * step, step), step)
                    own_buf[i][k, span, :] = (
                        own_buf[i][k, span, :].astype(jnp.float32)
                        + from_twin[i][k, span, :].astype(jnp.float32)
                    ).astype(jnp.bfloat16)

                add_rows(rows // step, add)
                copies.append(
                    push(
                        own_buf[i].at[k],
                        from_deep[i].at[k - 1],
                        send.at[i, deep + k],
                        arrive.at[i, deep + k],
                        others[k - 1],
                    )
                )
    for i in range(count):
        for k in range(1, deep):
            arrived(from_deep[i].at[k - 1], arrive.at[i, deep + k])

        def finish(at, i=i):
            span = pl.ds(pl.multiple_of(at * step, step), step)
            result = own_buf[i][0, span, :].astype(jnp.float32)
            result = result + from_twin[i][0, span, :].astype(jnp.float32)
            for k in range(deep - 1):
                result = result + from_deep[i][k, span, :].astype(jnp.float32)
            outs[i][span, :] = result

        add_rows(own_buf[i].shape[1] // step, finish)
    for copy in copies:
        copy.wait_send()


def sum_expert(calls, groups, arrays, axes):
    deep = groups // PAIR
    shapes = []
    for array, axis in zip(arrays, axes):
        shape = list(array.shape)
        shape[axis] //= groups
        shapes.append(tuple(shape))
    count = len(arrays)

    def bufs(n):
        return [pltpu.VMEM((n, *shape), jnp.bfloat16) for shape in shapes]

    sems = DMA((count, 2 * deep))
    return pl.pallas_call(
        functools.partial(sum_expert_kernel, deep, tuple(axes)),
        in_specs=[ANY] * count,
        out_specs=[IN_VMEM] * count,
        out_shape=[jax.ShapeDtypeStruct(shape, jnp.float32) for shape in shapes],
        scratch_shapes=bufs(deep) + bufs(deep) + bufs(deep - 1) + [sems, sems, DMA((count, deep))],
        compiler_params=calls.params(),
        name="sum_expert",
    )(*arrays)


ALL = ("expert", "tensor")


def gather(values, axes, dimension):
    return lax.all_gather(values, axes, axis=dimension, tiled=True)


def scatter_sum(values, axes, dimension):
    return lax.psum_scatter(
        values.astype(jnp.bfloat16), axes, scatter_dimension=dimension, tiled=True
    ).astype(jnp.float32)


def aligned(size, axis):
    return size % LANES == 0 if axis else size % 16 == 0


def gather_experts(calls, groups, part, items):
    taken = [axis == 0 or aligned(array.shape[axis], axis) for array, axis, _ in items]
    given = [item for item, take in zip(items, taken) if take]
    results = iter(gather_expert(calls, groups, *zip(*given)))

    def native(array, axis, cut):
        if cut is not None:
            array = lax.dynamic_slice_in_dim(array, part * cut[1], cut[1], axis=cut[0])
        return gather(array, "expert", axis)

    return [next(results) if take else native(*item) for item, take in zip(items, taken)]


def sum_experts(calls, groups, items):
    items = [(array.astype(jnp.bfloat16), axis) for array, axis in items]
    taken = [aligned(array.shape[axis] // groups, axis) for array, axis in items]
    given = [item for item, take in zip(items, taken) if take]
    results = iter(sum_expert(calls, groups, *zip(*given)))
    return [
        next(results) if take else scatter_sum(item[0], "expert", item[1])
        for item, take in zip(items, taken)
    ]


def part_of(values, index, count, dimension):
    size = values.shape[dimension] // count
    return lax.dynamic_slice_in_dim(values, index * size, size, axis=dimension)


def body(
    calls,
    block_in,
    attention_gain,
    query_down,
    query_gain,
    query_up,
    latent_down,
    latent_gain,
    latent_up,
    out_proj,
    ffn_gain,
    router,
    shared_gate,
    shared_up,
    shared_down,
    expert_gate,
    expert_up,
    expert_down,
    doc_lengths,
    routes,
    out_grad,
):
    groups = lax.axis_size("expert")
    parts = lax.axis_size("tensor")
    me = lax.axis_index("expert")
    part = lax.axis_index("tensor")
    row_count, width = block_in.shape
    top = routes.shape[1]
    local = expert_gate.shape[0]
    experts = local * groups
    latent_rank = latent_gain.shape[0] * groups
    query_rank = query_gain.shape[0] * groups

    all_gains = (attention_gain, ffn_gain, query_gain, latent_gain)
    gain_sizes = [g.shape[0] for g in all_gains]
    gain_room = -(-sum(gain_sizes) // (16 * LANES)) * 16 * LANES
    gains = jnp.concatenate([g.astype(jnp.float32) for g in all_gains])
    gains = jnp.pad(gains, (0, gain_room - sum(gain_sizes))).reshape(-1, LANES)
    routes_pad = jnp.pad(routes.T, ((0, -top % 8), (0, 0)))
    query_cut = query_down.shape[1] // parts
    latent_cut = latent_down.shape[1] // parts
    (
        gains,
        query_down_part,
        latent_down_part,
        query_up_full,
        latent_up_full,
        out_proj_full,
        router_t,
        routes_t,
    ) = gather_experts(
        calls,
        groups,
        part,
        [
            (gains, 0, None),
            (query_down, 0, (1, query_cut)),
            (latent_down.T, 1, (0, latent_cut)),
            (query_up, 0, None),
            (latent_up, 0, None),
            (out_proj, 1, None),
            (router.T, 1, None),
            (routes_pad, 1, None),
        ],
    )
    routes_t = routes_t[:top]
    gains = gains.reshape(groups, gain_room)
    ends = [sum(gain_sizes[: i + 1]) for i in range(len(gain_sizes))]
    attention_full, ffn_full, query_gain_full, latent_gain_full = (
        gains[:, end - size : end].reshape(-1) for size, end in zip(gain_sizes, ends)
    )
    gradient_all = gather(part_of(out_grad, part, parts, 0), ALL, 0)
    shared = jnp.stack([shared_gate.T, shared_up.T, shared_down])
    shared_units = shared.shape[1] // groups
    shared = shared.reshape(3, groups, shared_units, -1).transpose(1, 0, 2, 3)
    shared = lax.all_to_all(shared, "expert", split_axis=0, concat_axis=0, tiled=True)
    shared = shared.transpose(1, 2, 0, 3).reshape(3, shared_units, width)

    residual = block_in.astype(jnp.float32)
    allowed, cosine, sinusoid = layout(doc_lengths[0], row_count)
    first_f, inverse_first = rms_forward(residual, attention_full)
    first_normed = first_f.astype(jnp.bfloat16)
    query_lat = matmul(first_normed, query_down_part).astype(jnp.bfloat16)
    latent_all = matmul_nt(latent_down_part, first_normed).astype(jnp.bfloat16)
    query_lat, latent_all = gather_tensor(calls, parts, (query_lat, latent_all), (1, 0))
    query_lat = query_lat.astype(jnp.float32)
    latent_all = latent_all.T.astype(jnp.float32)
    query_n, inverse_query = rms_forward(query_lat, query_gain_full)
    query_n = query_n.astype(jnp.bfloat16)
    latent = latent_all[:, :latent_rank]
    latent_n, inverse_latent = rms_forward(latent, latent_gain_full)
    latent_n = latent_n.astype(jnp.bfloat16)
    key_rope = rotate(latent_all[:, latent_rank:], cosine, sinusoid)

    attended, logsum, queries, key_rows, value_rows = heads_forward(
        query_n, latent_n, key_rope, query_up_full, latent_up_full, allowed, cosine, sinusoid
    )
    mixed_heads = sum_tensor(calls, parts, matmul(attended, out_proj_full))

    residual_rows = part_of(residual, part, parts, 0)
    gradient_rows = part_of(out_grad, part, parts, 0).astype(jnp.float32)
    middle = residual_rows + mixed_heads
    second_f, inverse_ffn = rms_forward(middle, ffn_full)
    second_normed = second_f.astype(jnp.bfloat16)
    routes_rows = part_of(routes, part, parts, 0)
    expert_ids = jnp.arange(experts, dtype=jnp.int32)
    routed_here = jnp.any(routes_rows[:, :, None] == expert_ids[None, None, :], axis=1)
    chosen = jnp.where(routed_here, jax.nn.sigmoid(matmul_nt(second_normed, router_t)), 0.0)
    totals = jnp.sum(chosen, axis=-1, keepdims=True)
    route_weights = ROUTE_SCALE * chosen / totals

    lane_pad = -experts % LANES
    tokens, weights_all = gather_all(
        calls, groups, parts, (second_normed, jnp.pad(route_weights, ((0, 0), (0, lane_pad))))
    )
    tokens = tokens.reshape(groups, row_count, width)
    gradients = gradient_all.reshape(groups, row_count, width)

    own_ids = me * local + jnp.arange(local, dtype=jnp.int32)
    named = jnp.any(
        routes_t.reshape(top, groups, 1, row_count) == own_ids[None, None, :, None], axis=0
    )
    row_index = jnp.arange(row_count, dtype=jnp.int32)
    earlier = (row_index[:, None] < row_index[None, :]).astype(jnp.bfloat16)
    rank = contract("bjs,st->bjt", named.astype(jnp.bfloat16), earlier)
    slots = jnp.arange(CAP, dtype=jnp.int32).astype(jnp.float32)
    picked = named[:, :, None, :] & (rank[:, :, None, :] == slots[None, None, :, None])
    own_weights = lax.dynamic_slice_in_dim(weights_all, me * local, local, axis=1)
    own_weights = own_weights.reshape(groups, row_count, local).transpose(0, 2, 1)
    slot_weights = jnp.sum(
        jnp.where(picked, own_weights[:, :, None, :], 0.0), axis=-1, keepdims=True
    )
    picks = picked.astype(jnp.bfloat16).reshape(groups, local * CAP, row_count)
    expert_rows = contract("bst,btd->bsd", picks, tokens).astype(jnp.bfloat16)
    expert_grads = contract("bst,btd->bsd", picks, gradients).astype(jnp.bfloat16)
    slot_shape = (groups, local, CAP, width)
    produced, back, slot_dweights, grad_gate, grad_up, grad_down = expert_stage(
        expert_rows.reshape(slot_shape),
        expert_grads.reshape(slot_shape),
        slot_weights,
        expert_gate.transpose(0, 2, 1),
        expert_up.transpose(0, 2, 1),
        expert_down,
    )
    lane_ids = jnp.arange(experts + lane_pad, dtype=jnp.int32)
    spread = jnp.where(
        own_ids[None, :, None, None] == lane_ids[None, None, None, :], slot_dweights, 0.0
    ).astype(jnp.bfloat16)
    mixed_part, dsecond_part, grad_shared = combine_stage(
        picks,
        produced.reshape(groups, local * CAP, width),
        back.reshape(groups, local * CAP, width),
        spread.reshape(groups, local * CAP, experts + lane_pad),
        tokens,
        gradients,
        shared,
    )
    dsecond, mixed = sum_all(
        calls,
        groups,
        parts,
        (
            dsecond_part.reshape(-1, width + experts + lane_pad),
            mixed_part.reshape(-1, width),
        ),
    )
    dweights = dsecond[:, width : width + experts]
    dsecond = dsecond[:, :width]

    dchosen = (
        ROUTE_SCALE
        / totals
        * (dweights - jnp.sum(dweights * chosen, axis=-1, keepdims=True) / totals)
    )
    dlogits = jnp.where(routed_here, dchosen * chosen * (1.0 - chosen), 0.0).astype(jnp.bfloat16)
    dsecond = dsecond + matmul(dlogits, router_t)
    grad_router = matmul_tn(dlogits, second_normed)
    grad_ffn_gain = gain_gradient(middle, inverse_ffn, dsecond)
    middle_grad = gradient_rows + rms_backward(middle, inverse_ffn, ffn_full, dsecond)

    attention_grad, block_out = gather_tensor(
        calls,
        parts,
        (middle_grad.astype(jnp.bfloat16), (middle + mixed).astype(jnp.bfloat16)),
        (0, 0),
    )
    grad_out_proj = matmul_tn(attended, attention_grad)
    attended_grad = matmul_nt(attention_grad, out_proj_full).astype(jnp.bfloat16)
    dquery_n, dlatent_n, dkey_rope, grad_query_up, grad_latent_up = heads_backward(
        attended_grad,
        logsum,
        queries,
        key_rows,
        value_rows,
        query_n,
        latent_n,
        query_up_full,
        latent_up_full,
        allowed,
        cosine,
        sinusoid,
    )
    heads_grad = jnp.concatenate(
        [v.astype(jnp.bfloat16) for v in (dquery_n, dlatent_n, dkey_rope)], axis=1
    )
    heads_wide = heads_grad.shape[1]
    heads_grad = jnp.pad(heads_grad, ((0, 0), (0, -heads_wide % LANES)))
    heads_grad = sum_tensor(calls, parts, heads_grad)
    dquery_n = heads_grad[:, :query_rank]
    dlatent_n = heads_grad[:, query_rank : query_rank + latent_rank]
    dkey_rope = heads_grad[:, query_rank + latent_rank : heads_wide]
    query_lat_rows = part_of(query_lat, part, parts, 0)
    latent_rows = part_of(latent, part, parts, 0)
    inverse_query_rows = part_of(inverse_query, part, parts, 0)
    inverse_latent_rows = part_of(inverse_latent, part, parts, 0)
    dquery_lat = rms_backward(query_lat_rows, inverse_query_rows, query_gain_full, dquery_n)
    grad_query_gain = gain_gradient(query_lat_rows, inverse_query_rows, dquery_n)
    dlatent = rms_backward(latent_rows, inverse_latent_rows, latent_gain_full, dlatent_n)
    grad_latent_gain = gain_gradient(latent_rows, inverse_latent_rows, dlatent_n)
    dlatent_all = jnp.concatenate([dlatent, dkey_rope], axis=-1)
    dquery_lat = lax.all_to_all(
        dquery_lat.astype(jnp.bfloat16), "tensor", split_axis=1, concat_axis=0, tiled=True
    )
    dlatent_all = lax.all_to_all(
        dlatent_all.astype(jnp.bfloat16), "tensor", split_axis=1, concat_axis=0, tiled=True
    )
    grad_query_down = matmul_tn(first_normed, dquery_lat)
    grad_latent_down = matmul_tn(dlatent_all, first_normed)
    dfirst = matmul_nt(dquery_lat, query_down_part) + matmul(dlatent_all, latent_down_part)
    dfirst = sum_tensor(calls, parts, dfirst)
    inverse_rows = part_of(inverse_first, part, parts, 0)
    dresidual = rms_backward(residual_rows, inverse_rows, attention_full, dfirst)
    grad_attention_gain = gain_gradient(residual_rows, inverse_rows, dfirst)

    grad_shared = grad_shared.astype(jnp.bfloat16).reshape(3, shared_units, groups, -1)
    grad_shared = grad_shared.transpose(2, 0, 1, 3)
    grad_shared = lax.all_to_all(grad_shared, "expert", split_axis=0, concat_axis=0, tiled=True)
    grad_shared = grad_shared.transpose(1, 0, 2, 3).astype(jnp.float32)
    grad_shared = grad_shared.reshape(3, groups * shared_units, -1)
    grad_gains = jnp.concatenate(
        [
            g.reshape(groups, -1)
            for g in (grad_attention_gain, grad_ffn_gain, grad_query_gain, grad_latent_gain)
        ],
        axis=1,
    )
    grad_gains = jnp.pad(grad_gains, ((0, 0), (0, gain_room - grad_gains.shape[1])))
    (
        grad_query_up,
        grad_latent_up,
        grad_out_proj,
        grad_query_down,
        grad_latent_down,
        grad_router,
        grad_gains,
    ) = sum_experts(
        calls,
        groups,
        [
            (grad_query_up, 0),
            (grad_latent_up, 0),
            (grad_out_proj, 1),
            (grad_query_down, 0),
            (grad_latent_down, 1),
            (grad_router, 1),
            (grad_gains.reshape(-1, LANES), 0),
        ],
    )
    input_grad, grad_query_down, grad_latent_down, grad_router, grad_gains = gather_tensor(
        calls,
        parts,
        (
            (middle_grad + dresidual).astype(jnp.bfloat16),
            grad_query_down.astype(jnp.bfloat16),
            grad_latent_down.astype(jnp.bfloat16),
            grad_router,
            grad_gains,
        ),
        (0, 1, 0, 0, 0),
    )
    grad_router = jnp.sum(grad_router.reshape(parts, experts, -1), axis=0)
    grad_gains = jnp.sum(grad_gains.reshape(parts, gain_room), axis=0)
    grad_attention_gain, grad_ffn_gain, grad_query_gain, grad_latent_gain = (
        grad_gains[end - size : end] for size, end in zip(gain_sizes, ends)
    )

    return (
        block_out,
        input_grad,
        grad_attention_gain,
        grad_query_down.astype(jnp.float32),
        grad_query_gain,
        grad_query_up,
        grad_latent_down.astype(jnp.float32).T,
        grad_latent_gain,
        grad_latent_up,
        grad_out_proj,
        grad_ffn_gain,
        grad_router.T,
        grad_shared[0].T,
        grad_shared[1].T,
        grad_shared[2],
        grad_gate.transpose(0, 2, 1),
        grad_up.transpose(0, 2, 1),
        grad_down,
    )


def solution(mesh):
    placed = (
        P("expert", None),
        P("expert"),
        P("expert", None),
        P("expert"),
        P("expert", "tensor"),
        P("expert", None),
        P("expert"),
        P("expert", "tensor"),
        P("tensor", "expert"),
        P("expert"),
        P("expert", None),
        P("expert", "tensor"),
        P("expert", "tensor"),
        P("tensor", "expert"),
        P("expert", None, "tensor"),
        P("expert", None, "tensor"),
        P("expert", "tensor", None),
        P("expert", None),
        P("expert", None),
        P("expert", None),
    )
    return jax.shard_map(
        functools.partial(body, Calls()),
        mesh=mesh,
        in_specs=placed,
        out_specs=(
            P("expert", None),
            P("expert", None),
            P("expert"),
            P("expert", None),
            P("expert"),
            P("expert", "tensor"),
            P("expert", None),
            P("expert"),
            P("expert", "tensor"),
            P("tensor", "expert"),
            P("expert"),
            P("expert", None),
            P("expert", "tensor"),
            P("expert", "tensor"),
            P("tensor", "expert"),
            P("expert", None, "tensor"),
            P("expert", None, "tensor"),
            P("expert", "tensor", None),
        ),
        check_vma=False,
    )
```

time: 2250 us -> 799 us (0.36)
  waiting for transfers between devices: 1430 us -> 1.23 us
  Pallas kernels: 0 us -> 609 us
  blocking collectives: 288 us -> 0 us
  matrix products: 230 us -> 65.3 us
  local copies, waits for them, and re-layouts: 163 us -> 35.9 us
  other arithmetic: 95 us -> 42.5 us
    pallas_call x0 -> x12, Pallas kernels: none -> 609 us  [the longest x1 170 us: gather_expert(): pl.pallas_call(functools.partial(gather_expert_kernel, deep, tuple(axes),...]
    reduce_scatter x9 -> x0, waiting for transfers between devices: 524 us -> none  [the longest x1 121 us: body(): lax.psum_scatter(summed[2].astype(jnp.bfloat16), 'expert', scatter_dimens...]
    all_gather x8 -> x1, waiting for transfers between devices: 478 us -> 0.01 us  [gather(): return lax.all_gather(values, axes, axis=dimension, tiled=True)]
    all_to_all x4, waiting for transfers between devices: 322 us -> 1.21 us  [the longest x1 1.2 us: body(): lax.all_to_all(dquery_lat.astype(jnp.bfloat16), 'tensor', split_axis=1, c...]
    all_gather x3 -> x0, blocking collectives: 211 us -> none  [the longest x1 177 us: body(): lax.all_gather(router, 'expert', axis=0, tiled=True)]
    dot_general x99 -> x10, matrix products: 220 us -> 18.9 us  [matmul(): return jnp.dot(left, right, preferred_element_type=jnp.float32)]
    psum x3 -> x0, waiting for transfers between devices: 96.4 us -> none  [the longest x1 69.5 us: body(): lax.psum(mixed_part.astype(jnp.bfloat16), 'tensor').astype(jnp.float32)]
    unnamed x2 -> x0, blocking collectives: 59 us -> none
  transfers between devices with their start and end apart: 24 -> 5, of which waited for: 20 -> 1; matrix products, arithmetic and copies ran while one was open for 14% -> 9% of each run, Pallas kernels for 0% -> 48%
where the time goes in v1:
time: 799 us; the launch traced here: 791 us
  Pallas kernels  609 us (76%)
  matrix products  65.3 us (8%)
  other arithmetic  42.5 us (5%)
  local copies, waits for them, and re-layouts  35.9 us (4%)
  starting transfers between devices  20.8 us (3%)
  between operations  15.8 us (2%)
    pallas_call x1, Pallas kernels, gather_expert(): pl.pallas_call(functools.partial(gather_expert_kernel, deep, tuple(axes),...  170 us
    pallas_call x1, Pallas kernels, sum_expert(): pl.pallas_call(functools.partial(sum_expert_kernel, deep, tuple(axes)), i...  102 us
    pallas_call x1, Pallas kernels, sum_all(): pl.pallas_call(functools.partial(sum_all_kernel, deep, tuple(local), coun...  102 us
    pallas_call x1, Pallas kernels, gather_all(): pl.pallas_call(functools.partial(gather_all_kernel, deep, tuple(streams),...  60.6 us
    pallas_call x1, Pallas kernels, expert_stage(): pl.pallas_call(expert_kernel, grid=(local, blocks // step), in_specs=[row...  54.3 us
    pallas_call x1, Pallas kernels, combine_stage(): pl.pallas_call(combine_kernel, grid=(blocks,), in_specs=[pl.BlockSpec((1,...  43.4 us
    pallas_call x3, Pallas kernels, gather_tensor(): pl.pallas_call(functools.partial(gather_tensor_kernel, tuple(axes)), in_s...  42.6 us
    pallas_call x3, Pallas kernels, sum_tensor(): pl.pallas_call(sum_tensor_kernel, in_specs=[ANY], out_specs=IN_VMEM, out_...  34.6 us
  transfers between devices with their start and end apart: 5, of which 1 were waited for; matrix products, arithmetic and copies ran while one was open for 9% of the time, Pallas kernels for 48%

profile of v1, /device:TPU:0, one launch (start us, length us, event | category | flops | bytes accessed | tf_op | source)
XLA Modules:
  0.0 790.8 jit_solution(16196644881215150386)
XLA Ops:
  7.2 1.7 constant_dynamic-slice_fusion.2
  9.0 2.3 maximum_bitcast_fusion
  11.3 7.4 all-to-all-start
  20.0 169.7 %gather_expert.1 = (f32[128,128]{1,0:T(8,128)}, bf16[2048,384]{1,0:T(8,128)(2,1)}, bf16[144,2048]{1,0:T(8,128)(2,1)}, bf16[1536,768]{1,0:T(8,128)(2,1)}, bf16[51...) custom-call(f32[16,128]{1,0:T(8,128)} %fusion.58.refs_0_, ...), custom_call_target="tpu_custom_call" | custom-call | tf_op jit(solution)/shard_map/gather_expert/pallas_call | solution.py:433
  192.5 1.5 convert_element_type.186
  194.4 1.2 convolution_convert_fusion.16.refs_1_
  195.6 1.4 convolution_convert_fusion.15.refs_0_
  197.0 10.4 %gather_tensor.3 = (bf16[256,1536]{1,0:T(8,128)(2,1)}, bf16[576,256]{1,0:T(8,128)(2,1)}) custom-call(bf16[256,384]{1,0:T(8,128)(2,1)} %convolution_convert_fusion.15.refs_0_, bf16[144,256]{1,0:T(8,128)(2,1)} %convolution_convert_fusion.16.refs_1_), custom_call_target="tpu_custom_call" | custom-call | tf_op jit(solution)/shard_map/gather_tensor/pallas_call | solution.py:487
  210.9 2.8 fusion.28
  217.2 1.7 convolution_convert_fusion.6
  218.9 11.7 %sum_tensor.3 = f32[64,2048]{1,0:T(8,128)} custom-call(bf16[2,2,64,2048]{3,2,1,0:T(8,128)(2,1)} %bitcast.168), custom_call_target="tpu_custom_call" | custom-call | tf_op jit(solution)/shard_map/sum_tensor/pallas_call | solution.py:540
  230.9 1.4 multiply_reduce_fusion.7
  233.8 60.6 %gather_all.1 = (bf16[2048,2048]{1,0:T(8,128)(2,1)}, f32[2048,128]{1,0:T(8,128)}) custom-call(bf16[64,2048]{1,0:T(8,128)(2,1)} %copy-done.6, f32[64,128]{1,0:T(8,128)} %pad.24.refs_1_), custom_call_target="tpu_custom_call" | custom-call | tf_op jit(solution)/shard_map/gather_all/pallas_call | solution.py:654
  294.5 1.6 constant_dynamic-slice_fusion
  296.7 1.3 convert_element_type.194
  300.5 1.4 copy.147.w_ref
  302.0 1.5 fusion.2
  304.2 9.0 %convolution_convert_fusion.1 = bf16[8,256,2048]{2,1,0:T(8,128)(2,1)} fusion(pred[8,256,256]{2,1,0:T(32,128)(4,1)S(1)} %get-tuple-element.117, bf16[8,256,2048]{2,1,0:T(8,128)(2,1)} %bitcast.152), kind=kOutput, calls=%fused_computation.2 | convolution fusion | flops 2151677952 | bytes 17301504 | tf_op jit(solution)/shard_map/bst,btd->bsd/dot_general | solution.py:28
  313.3 2.4 copy.175
  315.6 9.0 %convolution_convert_fusion = bf16[8,256,2048]{2,1,0:T(8,128)(2,1)} fusion(pred[8,256,256]{2,1,0:T(32,128)(4,1)S(1)} %get-tuple-element.117, bf16[8,256,2048]{2,1,0:T(8,128)(2,1)} %bitcast.150), kind=kOutput, calls=%fused_computation.1 | convolution fusion | flops 2151677952 | bytes 17301504 | tf_op jit(solution)/shard_map/bst,btd->bsd/dot_general | solution.py:28
  324.6 54.3 %experts.1 = (bf16[8,8,32,2048]{3,2,1,0:T(8,128)(2,1)}, bf16[8,8,32,2048]{3,2,1,0:T(8,128)(2,1)}, f32[8,8,32,1]{3,2,1,0:T(8,128)}, f32[8,352,2048]{2,1,0:T(8,128...) custom-call(bf16[8,8,32,2048]{3,2,1,0:T(8,128)(2,1)} %bitcast.154, bf16[8,8,32,2048]{3,2,1,0:T(8,128)(2,1)} %bitcast.155, ...), custom_call_target="tpu_custom_call" | custom-call | flops 26575110144 | bytes 137363456 | tf_op jit(solution)/shard_map/experts/pallas_call | solution.py:224
  378.9 1.6 reduce
  381.7 43.4 %combine.1 = (bf16[8,256,2048]{2,1,0:T(8,128)(2,1)}, bf16[8,256,2176]{2,1,0:T(8,128)(2,1)}, f32[3,88,2048]{2,1,0:T(8,128)}) custom-call(bf16[8,256,256]{2,1,0:T(8,128)(2,1)} %get-tuple-element.118.p_ref, bf16[8,256,2048]{2,1,0:T(8,128)(2,1)} %bitcast.217, bf16[8,256,2048]{2,1,0:T(8,128)(2,1)} %bitcast.218, bf16[8,256,128]{2,1,0:T(8,128)(2,1)} %select_convert_fusion.dw_ref, ...), custom_call_target="tpu_custom_call" | custom-call | flops 10938744832 | bytes 50331648 | tf_op jit(solution)/shard_map/combine/pallas_call | solution.py:284
  425.1 101.6 %sum_all.1 = (f32[64,2176]{1,0:T(8,128)}, f32[64,2048]{1,0:T(8,128)}) custom-call(bf16[16,2,64,2176]{3,2,1,0:T(8,128)(2,1)} %bitcast.160, bf16[16,2,64,2048]{3,2,1,0:T(8,128)(2,1)} %bitcast.161), custom_call_target="tpu_custom_call" | custom-call | tf_op jit(solution)/shard_map/sum_all/pallas_call | solution.py:833
  527.7 2.0 multiply_reduce_fusion.3
  529.7 2.1 add_convert_fusion.1
  531.8 15.1 %gather_tensor.4 = (bf16[256,2048]{1,0:T(8,128)(2,1)}, bf16[256,2048]{1,0:T(8,128)(2,1)}) custom-call(bf16[64,2048]{1,0:T(8,128)(2,1)} %get-tuple-element.114.refs_0_, bf16[64,2048]{1,0:T(8,128)(2,1)} %get-tuple-element.113.refs_1_), custom_call_target="tpu_custom_call" | custom-call | tf_op jit(solution)/shard_map/gather_tensor/pallas_call | solution.py:487
  546.9 2.7 convolution_convert_fusion.13
  549.8 2.3 fusion.25
  552.0 1.6 fusion.7
  553.7 3.9 convolution_bitcast_fusion
  557.5 1.8 slice.214
  560.3 4.0 convolution_bitcast_fusion.1
  565.3 1.7 convolution_convert_fusion.11
  567.0 1.6 convolution_convert_fusion.9.refs_1_
  568.8 1.3 fusion.42
  572.3 3.4 convolution_convert_fusion.5
  575.6 2.3 convolution_convert_fusion.2.refs_0_
  578.0 2.1 convolution_convert_fusion.3.refs_2_
  580.1 2.3 concatenate.44
  582.3 1.2 pad.25
  583.6 12.0 %sum_tensor.4 = f32[64,2176]{1,0:T(8,128)} custom-call(bf16[2,2,64,2176]{3,2,1,0:T(8,128)(2,1)} %bitcast.164), custom_call_target="tpu_custom_call" | custom-call | tf_op jit(solution)/shard_map/sum_tensor/pallas_call | solution.py:540
  596.4 1.4 multiply_reduce_fusion.9
  597.8 1.3 multiply_convert_fusion.4
  602.0 3.3 all-to-all-start.2
  605.4 1.8 convolution_convert_fusion.8.refs_5_
  608.1 1.8 convert_element_type.232
  611.0 3.5 all-to-all-start.1
  614.5 1.5 fusion.80
  616.0 2.6 convolution_convert_fusion.7.refs_4_
  618.5 1.2 all-to-all-done.1
  619.7 6.5 all-to-all-start.3
  626.3 3.1 fusion.1
  629.4 10.8 %sum_tensor.5 = f32[64,2048]{1,0:T(8,128)} custom-call(bf16[2,2,64,2048]{3,2,1,0:T(8,128)(2,1)} %bitcast.167), custom_call_target="tpu_custom_call" | custom-call | tf_op jit(solution)/shard_map/sum_tensor/pallas_call | solution.py:540
  640.2 1.5 multiply_reduce_fusion.4
  642.4 2.0 convolution_convert_fusion.4.refs_3_
  644.4 102.4 %sum_expert.1 = (f32[192,768]{1,0:T(8,128)}, f32[64,1024]{1,0:T(8,128)}, f32[512,256]{1,0:T(8,128)}, f32[256,384]{1,0:T(8,128)}, f32[144,256]{1,0:T(8,128)}, /*index=5*/f32[64,256]{1,0:T(8,128)}, f32[16,128]{1,0:T(8,128)}) custom-call(bf16[1536,768]{1,0:T(8,128)(2,1)} %convolution_convert_fusion.2.refs_0_, ...), custom_call_target="tpu_custom_call" | custom-call | tf_op jit(solution)/shard_map/sum_expert/pallas_call | solution.py:948
  746.9 1.7 convert_element_type.229.refs_1_
  748.5 1.6 convert_element_type.230.refs_2_
  750.1 2.2 add_convert_fusion.refs_0_
  752.3 17.1 %gather_tensor.5 = (bf16[256,2048]{1,0:T(8,128)(2,1)}, bf16[256,1536]{1,0:T(8,128)(2,1)}, bf16[576,256]{1,0:T(8,128)(2,1)}, f32[256,256]{1,0:T(8,128)}, f32[64,128]{1,0:T(8,128)}) custom-call(bf16[64,2048]{1,0:T(8,128)(2,1)} %add_convert_fusion.refs_0_, bf16[256,384]{1,0:T(8,128)(2,1)} %convert_element_type.229.refs_1_, ...), custom_call_target="tpu_custom_call" | custom-call | tf_op jit(solution)/shard_map/gather_tensor/pallas_call | solution.py:487
  771.5 2.5 convert_element_type.231
  776.0 1.4 convert_bitcast_fusion
  777.4 1.4 fusion.75
  (277 shorter events, 38.5 us)
Async XLA Ops:
  7.2 308.4 %all-gather.2.cloned.1.call-start = ((), (), s32[]{:S(2)}) async-start(), calls=%async_computation.4 | async-start | bytes 8650752 | tf_op jit(solution)/shard_map/all_gather | solution.py:963
  8.9 9.8 %copy-start.44 = (s32[256,6]{0,1:T(8,128)S(1)}, s32[256,6]{0,1:T(8,128)}, u32[]{:S(2)}) copy-start(s32[256,6]{0,1:T(8,128)} %param.38) | copy-start | bytes 18436
  8.9 10.4 %copy-start.78 = (bf16[64]{0:T(256)(128)(2,1)S(1)}, bf16[64]{0:T(256)(128)(2,1)}, u32[]{:S(2)}) copy-start(bf16[64]{0:T(256)(128)(2,1)} %param.26) | copy-start | bytes 388
  9.0 10.4 %copy-start.79 = (bf16[192]{0:T(256)(128)(2,1)S(1)}, bf16[192]{0:T(256)(128)(2,1)}, u32[]{:S(2)}) copy-start(bf16[192]{0:T(256)(128)(2,1)} %param.23) | copy-start | bytes 1156
  9.0 10.4 %copy-start.80 = (bf16[256]{0:T(256)(128)(2,1)S(1)}, bf16[256]{0:T(256)(128)(2,1)}, u32[]{:S(2)}) copy-start(bf16[256]{0:T(256)(128)(2,1)} %param.29) | copy-start | bytes 1540
  9.0 10.4 %copy-start.81 = (bf16[256]{0:T(256)(128)(2,1)S(1)}, bf16[256]{0:T(256)(128)(2,1)}, u32[]{:S(2)}) copy-start(bf16[256]{0:T(256)(128)(2,1)} %param.21) | copy-start | bytes 1540
  11.3 180.1 %copy-start.82 = (s32[1,3]{1,0:T(1,128)S(1)}, s32[1,3]{1,0:T(1,128)}, u32[]{:S(2)}) copy-start(s32[1,3]{1,0:T(1,128)} %param.37) | copy-start | bytes 40
  11.3 181.1 %copy-start.2 = (bf16[256,2048]{1,0:T(8,128)(2,1)S(1)}, bf16[256,2048]{1,0:T(8,128)(2,1)}, u32[]{:S(2)}) copy-start(bf16[256,2048]{1,0:T(8,128)(2,1)} %param.20) | copy-start | bytes 3145732
  11.3 301.9 %all-to-all-start = ((bf16[8,3,88,256]{3,2,1,0:T(8,128)(2,1)}), bf16[8,3,88,256]{3,2,1,0:T(8,128)(2,1)}, u32[]{:S(2)}, u32[]{:S(2)}) async-start(bf16[8,3,88,256]{3,2,1,0:T(8,128)(2,1)} %maximum_bitcast_fusion), calls=%async_computation | async-start | bytes 2162688 | tf_op jit(solution)/shard_map/all_to_all | solution.py:1081
  191.3 4.2 copy-start.30
  191.6 22.1 %copy-start.60 = (f32[32]{0:T(128)}, f32[32]{0:T(128)S(1)}, u32[]{:S(2)}) copy-start(f32[32]{0:T(128)S(1)} %multiply_exponential_fusion) | copy-start | bytes 388
  191.8 22.0 %copy-start.46 = (f32[256]{0:T(256)}, f32[256]{0:T(256)S(1)}, u32[]{:S(2)}) copy-start(f32[256]{0:T(256)S(1)} %subtract_convert_fusion.2) | copy-start | bytes 3076
  197.0 12.5 %copy-start.4 = (bf16[512,1024]{1,0:T(8,128)(2,1)S(1)}, bf16[512,1024]{1,0:T(8,128)(2,1)}, u32[]{:S(2)}) copy-start(bf16[512,1024]{1,0:T(8,128)(2,1)} %get-tuple-element.59) | copy-start | bytes 3145732
  210.2 5.3 copy-start.8
  210.3 4.5 copy-start.22
  210.9 2.8 copy-start.65
  210.9 3.7 copy-start.56
  216.2 14.4 %copy-start.15 = (bf16[4,128,256]{2,1,0:T(8,128)(2,1)}, bf16[4,128,256]{2,1,0:T(8,128)(2,1)S(1)}, u32[]{:S(2)}) copy-start(bf16[4,128,256]{2,1,0:T(8,128)(2,1)S(1)} %convolution_convert_fusion.14) | copy-start | bytes 786436
  217.2 13.5 %copy-start.43 = (f32[1,2,8,128]{3,2,1,0:T(8,128)S(1)}, f32[1,2,8,128]{3,2,1,0:T(8,128)}, u32[]{:S(2)}) copy-start(f32[1,2,8,128]{3,2,1,0:T(8,128)} %get-tuple-element.121) | copy-start | bytes 24580
  217.2 13.5 %copy-start.45 = (s32[256,6]{0,1:T(8,128)S(1)}, s32[256,6]{0,1:T(8,128)}, u32[]{:S(2)}) copy-start(s32[256,6]{0,1:T(8,128)} %param.38) | copy-start | bytes 18436
  218.9 13.9 %copy-start.27 = (bf16[64,2048]{1,0:T(8,128)(2,1)S(1)}, bf16[64,2048]{1,0:T(8,128)(2,1)}, u32[]{:S(2)}) copy-start(bf16[64,2048]{1,0:T(8,128)(2,1)} %get-tuple-element.64) | copy-start | bytes 786436
  230.9 3.0 copy-start.32
  232.2 63.8 %copy-start.66 = (f32[256]{0:T(256)S(1)}, f32[256]{0:T(256)}, u32[]{:S(2)}) copy-start(f32[256]{0:T(256)} %copy-done.65) | copy-start | bytes 3076
  233.1 65.0 %copy-start.71 = (f32[64]{0:T(128)}, f32[64]{0:T(128)S(1)}, u32[]{:S(2)}) copy-start(f32[64]{0:T(128)S(1)} %get-tuple-element.132) | copy-start | bytes 772
  294.5 3.6 copy-start.53
  294.5 4.2 copy-start.76
  296.1 3.5 copy-start.39
  299.3 4.3 copy-start.48
  299.3 4.3 copy-start.50
  425.1 102.5 %copy-start.72 = (f32[64]{0:T(128)S(1)}, f32[64]{0:T(128)}, u32[]{:S(2)}) copy-start(f32[64]{0:T(128)} %copy-done.71) | copy-start | bytes 772
  425.1 102.6 %copy-start.28 = (bf16[64,2048]{1,0:T(8,128)(2,1)S(1)}, bf16[64,2048]{1,0:T(8,128)(2,1)}, u32[]{:S(2)}) copy-start(bf16[64,2048]{1,0:T(8,128)(2,1)} %get-tuple-element.64) | copy-start | bytes 786436
  425.1 102.6 %copy-start.33 = (pred[64,64]{1,0:T(8,128)(4,1)S(1)}, pred[64,64]{1,0:T(8,128)(4,1)}, u32[]{:S(2)}) copy-start(pred[64,64]{1,0:T(8,128)(4,1)} %copy-done.32) | copy-start | bytes 12292
  425.1 102.6 %copy-start.58 = (f32[64]{0:T(128)S(1)}, f32[64]{0:T(128)}, u32[]{:S(2)}) copy-start(f32[64]{0:T(128)} %copy-done.57) | copy-start | bytes 772
  527.7 19.2 %copy-start.61 = (f32[64]{0:T(128)}, f32[64]{0:T(128)S(1)}, u32[]{:S(2)}) copy-start(f32[64]{0:T(128)S(1)} %get-tuple-element.128) | copy-start | bytes 772
  527.7 19.2 %copy-start.63 = (f32[64]{0:T(128)}, f32[64]{0:T(128)S(1)}, u32[]{:S(2)}) copy-start(f32[64]{0:T(128)S(1)} %get-tuple-element.129) | copy-start | bytes 772
  529.7 17.2 %copy-start.69 = (f32[64]{0:T(128)}, f32[64]{0:T(128)S(1)}, u32[]{:S(2)}) copy-start(f32[64]{0:T(128)S(1)} %broadcast_multiply_fusion.3) | copy-start | bytes 772
  549.6 4.0 copy-start.25
  549.6 4.0 copy-start.36
  549.6 4.0 copy-start.38
  553.6 6.6 copy-start.23
  564.3 2.7 copy-start.41
  564.3 2.7 copy-start.54
  572.2 3.4 copy-start.67
  582.3 14.0 %copy-start.74 = (f32[64]{0:T(128)S(1)}, f32[64]{0:T(128)}, u32[]{:S(2)}) copy-start(f32[64]{0:T(128)} %dynamic-slice.10) | copy-start | bytes 772
  583.5 15.5 %copy-start.11 = (f32[256,512]{1,0:T(8,128)S(1)}, f32[256,512]{1,0:T(8,128)}, u32[]{:S(2)}) copy-start(f32[256,512]{1,0:T(8,128)} %get-tuple-element.111) | copy-start | bytes 1572868
  583.5 15.5 %copy-start.42 = (f32[512]{0:T(512)S(1)}, f32[512]{0:T(512)}, u32[]{:S(2)}) copy-start(f32[512]{0:T(512)} %copy-done.40) | copy-start | bytes 6148
  583.5 15.5 %copy-start.73 = (f32[64]{0:T(128)S(1)}, f32[64]{0:T(128)}, u32[]{:S(2)}) copy-start(f32[64]{0:T(128)} %dynamic-slice.11) | copy-start | bytes 772
  583.5 21.8 %copy-start.7 = (bf16[64,2048]{1,0:T(8,128)(2,1)S(1)}, bf16[64,2048]{1,0:T(8,128)(2,1)}, u32[]{:S(2)}) copy-start(bf16[64,2048]{1,0:T(8,128)(2,1)} %copy-done.6) | copy-start | bytes 786436
  583.5 21.8 %copy-start.34 = (pred[64,64]{1,0:T(8,128)(4,1)S(1)}, pred[64,64]{1,0:T(8,128)(4,1)}, u32[]{:S(2)}) copy-start(pred[64,64]{1,0:T(8,128)(4,1)} %copy-done.32) | copy-start | bytes 12292
  583.5 21.8 %copy-start.62 = (f32[64]{0:T(128)S(1)}, f32[64]{0:T(128)}, u32[]{:S(2)}) copy-start(f32[64]{0:T(128)} %copy-done.61) | copy-start | bytes 772
  583.5 21.8 %copy-start.64 = (f32[64]{0:T(128)S(1)}, f32[64]{0:T(128)}, u32[]{:S(2)}) copy-start(f32[64]{0:T(128)} %copy-done.63) | copy-start | bytes 772
  596.4 11.7 %copy-start.51 = (bf16[2048]{0:T(1024)(128)(2,1)S(1)}, bf16[2048]{0:T(1024)(128)(2,1)}, u32[]{:S(2)}) copy-start(bf16[2048]{0:T(1024)(128)(2,1)} %get-tuple-element.98) | copy-start | bytes 12292
  602.0 9.0 %all-to-all-start.2 = ((bf16[64,4,144]{2,0,1:T(8,128)(2,1)}), bf16[64,4,144]{2,0,1:T(8,128)(2,1)S(1)}, u32[]{:S(2)}, u32[]{:S(2)}) async-start(bf16[64,4,144]{2,0,1:T(8,128)(2,1)} %copy.159), calls=%async_computation.2 | async-start | bytes 262144 | tf_op jit(solution)/shard_map/all_to_all | solution.py:1229
  611.0 5.0 copy-start.31
  611.0 5.0 copy-start.77
  611.0 8.8 %all-to-all-start.1 = ((bf16[64,4,384]{2,0,1:T(8,128)(2,1)}), bf16[64,4,384]{2,0,1:T(8,128)(2,1)S(1)}, u32[]{:S(2)}, u32[]{:S(2)}) async-start(bf16[64,4,384]{2,0,1:T(8,128)(2,1)} %bitcast.147), calls=%async_computation.1 | async-start | bytes 393216 | tf_op jit(solution)/shard_map/all_to_all | solution.py:1226
  619.7 156.3 %all-to-all-start.3 = ((bf16[8,3,88,256]{3,2,1,0:T(8,128)(2,1)}), bf16[8,3,88,256]{3,2,1,0:T(8,128)(2,1)}, u32[]{:S(2)}, u32[]{:S(2)}) async-start(bf16[8,3,88,256]{3,2,1,0:T(8,128)(2,1)} %bitcast.166), calls=%async_computation.3 | async-start | bytes 2162688 | tf_op jit(solution)/shard_map/all_to_all | solution.py:1242
  626.3 13.9 %copy-start.68 = (f32[64]{0:T(128)S(1)}, f32[64]{0:T(128)}, u32[]{:S(2)}) copy-start(f32[64]{0:T(128)} %dynamic-slice.9) | copy-start | bytes 772
  629.4 13.0 %copy-start.3 = (bf16[256,2048]{1,0:T(8,128)(2,1)S(1)}, bf16[256,2048]{1,0:T(8,128)(2,1)}, u32[]{:S(2)}) copy-start(bf16[256,2048]{1,0:T(8,128)(2,1)} %param.20) | copy-start | bytes 3145732
  644.4 105.7 %copy-start.1 = (f32[64,2048]{1,0:T(8,128)S(1)}, f32[64,2048]{1,0:T(8,128)}, u32[]{:S(2)}) copy-start(f32[64,2048]{1,0:T(8,128)} %sum_tensor.5) | copy-start | bytes 1572868
  644.4 105.7 %copy-start.59 = (f32[64]{0:T(128)S(1)}, f32[64]{0:T(128)}, u32[]{:S(2)}) copy-start(f32[64]{0:T(128)} %copy-done.57) | copy-start | bytes 772
  644.4 105.7 %copy-start.70 = (f32[64]{0:T(128)S(1)}, f32[64]{0:T(128)}, u32[]{:S(2)}) copy-start(f32[64]{0:T(128)} %copy-done.69) | copy-start | bytes 772
  769.4 4.5 copy-start.21
  769.4 5.7 copy-start.20
  (24 other events, 36.9 us)
Sparse Core Ops, SparseCore 0:
  11.4 135.6 all-gather.1

commit v2 on v1

v2 whole, which is shorter than its diff:
```python
import functools
import math

import jax
import jax.numpy as jnp
from jax import lax
from jax.experimental import pallas as pl
from jax.experimental.pallas import tpu as pltpu
from jax.sharding import PartitionSpec as P

NOPE = 128
ROPE = 64
VD = 128
CAP = 32
LANES = 128
VMEM_BYTES = 60 * 2**20

EPSILON = 1e-06
ROPE_BASE = 50000.0
ROUTE_SCALE = 2.446

ATTENDED = "attended"
EXPERT = "expert"
FIRST = "first"
GAINS = "gains"
I_PARTIAL = "i_partial"
KEYS = "keys"
LATENT_DOWN = "latent_down"
LATENT_N = "latent_n"
LATENT_T = "latent_t"
LATENT_UP = "latent_up"
OUT_GRAD = "out_grad"
OUT_PROJ = "out_proj"
OWN_SHARED = "own_shared"
QUERIES = "queries"
QUERY_DOWN = "query_down"
QUERY_LAT = "query_lat"
QUERY_N = "query_n"
QUERY_UP = "query_up"
READY = "ready"
ROUTER = "router"
ROUTES = "routes"
SHARED = "shared"
SHUFFLE = "shuffle"
TENSOR = "tensor"
TOKENS = "tokens"
VALUES = "values"
VMEM_ = "vmem"
WEIGHTS = "weights"
ZXYC = "zxyc"


def matmul(left, right):
    return jnp.dot(left, right, preferred_element_type=jnp.float32)


def contract(form, left, right):
    return jnp.einsum(form, left, right, preferred_element_type=jnp.float32)


def matmul_nt(left, right):
    return lax.dot_general(left, right, (((1,), (1,)), ((), ())), preferred_element_type=jnp.float32)


def matmul_tn(left, right):
    return lax.dot_general(left, right, (((0,), (0,)), ((), ())), preferred_element_type=jnp.float32)


def layout(lengths, row_count):
    doc_count = lengths.shape[0]
    doc_ends = jnp.cumsum(lengths)
    starts = doc_ends - lengths
    row_index = jnp.arange(row_count, dtype=jnp.int32)
    doc_ids = jnp.sum((row_index[:, None] >= doc_ends[None, :]).astype(jnp.int32), axis=1)
    owners = doc_ids[:, None] == jnp.arange(doc_count, dtype=jnp.int32)[None, :]
    first_row = jnp.sum(jnp.where(owners, starts[None, :], 0), axis=1)
    positions = (row_index - first_row).astype(jnp.float32)
    allowed = (doc_ids[:, None] == doc_ids[None, :]) & (row_index[None, :] <= row_index[:, None])
    frequency = jnp.exp(
        -math.log(ROPE_BASE) * 2.0 * jnp.arange(ROPE // 2, dtype=jnp.float32) / ROPE
    )
    angles = positions[:, None] * frequency[None, :]
    return (allowed, jnp.cos(angles), jnp.sin(angles))


def swiglu(gate_pre, up_pre):
    sigmoid_gate = jax.nn.sigmoid(gate_pre)
    return (sigmoid_gate, (gate_pre * sigmoid_gate * up_pre).astype(jnp.bfloat16))


def swiglu_back(dhidden, gate_pre, up_pre, sigmoid_gate):
    gate_grad = dhidden * up_pre * sigmoid_gate * (1.0 + gate_pre * (1.0 - sigmoid_gate))
    up_grad = dhidden * gate_pre * sigmoid_gate
    return (gate_grad.astype(jnp.bfloat16), up_grad.astype(jnp.bfloat16))


def expert_kernel(
    x_ref, g_ref, w_ref, gate_ref, up_ref, down_ref, y_ref, dr_ref, dw_ref, gg_ref, gu_ref, gd_ref
):
    blocks, _, cap, width = x_ref.shape
    rows = blocks * cap
    row_inputs = x_ref[...].reshape(rows, width)
    gradient = g_ref[...].reshape(rows, width).astype(jnp.float32)
    weight = w_ref[...].reshape(rows, 1)
    gate, up, down = gate_ref[0], up_ref[0], down_ref[0]
    gate_pre = matmul_nt(row_inputs, gate)
    up_pre = matmul_nt(row_inputs, up)
    sigmoid_gate, hidden = swiglu(gate_pre, up_pre)
    produced = matmul(hidden, down)
    dw_ref[...] = jnp.sum(gradient * produced, axis=1, keepdims=True).reshape(dw_ref.shape)
    y_ref[...] = (weight * produced).astype(jnp.bfloat16).reshape(y_ref.shape)
    cotangent = (weight * gradient).astype(jnp.bfloat16)
    dhidden = matmul_nt(cotangent, down)
    gate_grad, up_grad = swiglu_back(dhidden, gate_pre, up_pre, sigmoid_gate)
    back = matmul(gate_grad, gate) + matmul(up_grad, up)
    dr_ref[...] = back.astype(jnp.bfloat16).reshape(dr_ref.shape)
    first = pl.program_id(1) == 0

    def accumulate(ref, left, right):
        part = matmul_tn(left, right)

        @pl.when(first)
        def _():
            ref[0] = part

        @pl.when(jnp.logical_not(first))
        def _():
            ref[0] += part

    accumulate(gg_ref, gate_grad, row_inputs)
    accumulate(gu_ref, up_grad, row_inputs)
    accumulate(gd_ref, hidden, cotangent)


def expert_stage(row_inputs, gradients, weights, gate_t, up_t, down):
    blocks, local, cap, width = row_inputs.shape
    units = gate_t.shape[1]
    step = min(blocks, 256 // cap)
    rows_spec = pl.BlockSpec((step, 1, cap, width), lambda j, r: (r, j, 0, 0))
    slot_spec = pl.BlockSpec((step, 1, cap, 1), lambda j, r: (r, j, 0, 0))
    unit_spec = pl.BlockSpec((1, units, width), lambda j, r: (j, 0, 0))
    rows_shape = jax.ShapeDtypeStruct(row_inputs.shape, jnp.bfloat16)
    unit_shape = jax.ShapeDtypeStruct((local, units, width), jnp.float32)
    flops = 18 * blocks * local * cap * width * units
    moved = 8 * blocks * local * cap * width + 18 * local * units * width
    return pl.pallas_call(
        expert_kernel,
        grid=(local, blocks // step),
        in_specs=[rows_spec, rows_spec, slot_spec, unit_spec, unit_spec, unit_spec],
        out_specs=[rows_spec, rows_spec, slot_spec, unit_spec, unit_spec, unit_spec],
        out_shape=[
            rows_shape,
            rows_shape,
            jax.ShapeDtypeStruct((blocks, local, cap, 1), jnp.float32),
            unit_shape,
            unit_shape,
            unit_shape,
        ],
        compiler_params=pltpu.CompilerParams(vmem_limit_bytes=VMEM_BYTES),
        cost_estimate=pl.CostEstimate(flops=flops, bytes_accessed=moved, transcendentals=0),
        name="experts",
    )(row_inputs, gradients, weights, gate_t, up_t, down)


def combine_kernel(
    p_ref, y_ref, dr_ref, dw_ref, x_ref, g_ref, shared_ref, out_ref, ds_ref, grad_ref
):
    picks = p_ref[0]
    row_inputs, cotangent = x_ref[0], g_ref[0]
    gate, up, down = shared_ref[0], shared_ref[1], shared_ref[2]
    gate_pre = matmul_nt(row_inputs, gate)
    up_pre = matmul_nt(row_inputs, up)
    sigmoid_gate, hidden = swiglu(gate_pre, up_pre)
    out_ref[0] = (matmul_tn(picks, y_ref[0]) + matmul(hidden, down)).astype(jnp.bfloat16)
    dhidden = matmul_nt(cotangent, down)
    gate_grad, up_grad = swiglu_back(dhidden, gate_pre, up_pre, sigmoid_gate)
    back = matmul_tn(picks, dr_ref[0]) + matmul(gate_grad, gate) + matmul(up_grad, up)
    width = back.shape[1]
    ds_ref[0, :, :width] = back.astype(jnp.bfloat16)
    ds_ref[0, :, width:] = matmul_tn(picks, dw_ref[0]).astype(jnp.bfloat16)
    first = pl.program_id(0) == 0
    for index, (left, right) in enumerate(
        ((gate_grad, row_inputs), (up_grad, row_inputs), (hidden, cotangent))
    ):
        part = matmul_tn(left, right)

        @pl.when(first)
        def _(index=index, part=part):
            grad_ref[index] = part

        @pl.when(jnp.logical_not(first))
        def _(index=index, part=part):
            grad_ref[index] += part


def combine_stage(picks, produced, back, spread, tokens, gradients, shared):
    blocks, slots, rows = picks.shape
    width = tokens.shape[-1]
    slot_spec = pl.BlockSpec((1, slots, width), lambda b: (b, 0, 0))
    rows_spec = pl.BlockSpec((1, rows, width), lambda b: (b, 0, 0))
    whole = pl.BlockSpec(shared.shape, lambda b: (0, 0, 0))
    lanes = spread.shape[-1]
    units = shared.shape[1]
    flops = 4 * blocks * slots * rows * width + 18 * blocks * rows * width * units
    moved = 4 * blocks * slots * width + 8 * blocks * rows * width
    return pl.pallas_call(
        combine_kernel,
        grid=(blocks,),
        in_specs=[
            pl.BlockSpec((1, slots, rows), lambda b: (b, 0, 0)),
            slot_spec,
            slot_spec,
            pl.BlockSpec((1, slots, lanes), lambda b: (b, 0, 0)),
            rows_spec,
            rows_spec,
            whole,
        ],
        out_specs=[
            rows_spec,
            pl.BlockSpec((1, rows, width + lanes), lambda b: (b, 0, 0)),
            whole,
        ],
        out_shape=[
            jax.ShapeDtypeStruct((blocks, rows, width), jnp.bfloat16),
            jax.ShapeDtypeStruct((blocks, rows, width + lanes), jnp.bfloat16),
            jax.ShapeDtypeStruct(shared.shape, jnp.float32),
        ],
        compiler_params=pltpu.CompilerParams(vmem_limit_bytes=VMEM_BYTES),
        cost_estimate=pl.CostEstimate(flops=flops, bytes_accessed=moved, transcendentals=0),
        name="combine",
    )(picks, produced, back, spread, tokens, gradients, shared)


MESH = pl.DeviceIdType.MESH
PAIR = 2
ANY = pl.BlockSpec(memory_space=pl.ANY)
IN_VMEM = pl.BlockSpec(memory_space=pltpu.VMEM)
DMA = pltpu.SemaphoreType.DMA


def place():
    me, part = lax.axis_index(EXPERT), lax.axis_index(TENSOR)
    return (me // PAIR, me % PAIR, part // PAIR, part % PAIR)


def device(z, x, y, c):
    return {EXPERT: z * PAIR + x, TENSOR: y * PAIR + c}


def greet(peers):
    barrier = pltpu.get_barrier_semaphore()
    for peer in peers:
        pl.semaphore_signal(barrier, inc=1, device_id=peer, device_id_type=MESH)
    pl.semaphore_wait(barrier, len(peers))


def push(source, target, send, arrive, peer):
    copy = pltpu.make_async_remote_copy(
        src_ref=source,
        dst_ref=target,
        send_sem=send,
        recv_sem=arrive,
        device_id=peer,
        device_id_type=MESH,
    )
    copy.start()
    return copy


def bring(source, target, done):
    copy = pltpu.make_async_copy(source, target, done)
    copy.start()
    return copy


def arrived(target, done):
    pltpu.make_async_copy(target, target, done).wait()


def slot(ref, axis, index, size):
    start = pl.multiple_of(index * size, size)
    if axis == 0:
        return ref.at[pl.ds(start, size), :]
    return ref.at[:, pl.ds(start, size)]


class Bag(dict):
    __getattr__ = dict.__getitem__
    __setattr__ = dict.__setitem__


class Calls:
    def __init__(self):
        self.count = 0

    def params(self):
        self.count += 1
        return pltpu.CompilerParams(
            collective_id=self.count, has_side_effects=True, vmem_limit_bytes=VMEM_BYTES
        )


def choose(table, index):
    value = table[0]
    for i, entry in enumerate(table[1:], 1):
        if any(entry != other for other in table):
            value = jnp.where(index == i, entry, value)
    return value


class Link:
    def __init__(self, deep):
        me, part = lax.axis_index(EXPERT), lax.axis_index(TENSOR)
        self.deep, self.me, self.part = deep, me, part
        self.z, self.x = me // PAIR, me % PAIR
        self.y, self.c = part // PAIR, part % PAIR
        near = [
            sorted((k for k in range(1, deep)), key=lambda k: abs((z - k) % deep - z))
            for z in range(deep)
        ]
        self.order = [choose([near[z][h] for z in range(deep)], self.z) for h in range(deep - 1)]
        self.drains = []

    def at_z(self, z):
        return device(z, self.x, self.y, self.c)

    def peer(self, axis):
        flip = {name: 1 - getattr(self, name) if name == axis else getattr(self, name) for name in "xyc"}
        return device(self.z, flip["x"], flip["y"], flip["c"])

    def greet(self, groups, axes):
        peers = [{EXPERT: (self.me + j) % groups, TENSOR: self.part} for j in range(1, groups)]
        if "e" not in axes:
            peers = []
        greet(peers + [self.peer(axis) for axis in axes if axis != "e"])

    def emit(self, make, condition=None):
        def start():
            make().start()

        def finish():
            make().wait_send()

        if condition is None:
            start()
            self.drains.append(finish)
        else:
            pl.when(condition)(start)
            self.drains.append(lambda: pl.when(condition)(finish))

    def drain(self):
        for finish in self.drains:
            finish()
        self.drains = []


def spread(link, order, source, at, send, arrive):
    deep, z = link.deep, link.z
    cut = order.find("z")
    before, after = (order[:cut], order[cut + 1 :]) if cut >= 0 else ("", order)
    none = frozenset()

    def piece(k, flips):
        x, y, c = (
            1 - getattr(link, name) if name in flips else getattr(link, name) for name in "xyc"
        )
        return at((z + deep - k) % deep, x, y, c)

    def number(k, flips):
        return k * 8 + sum(1 << "xyc".index(name) for name in flips)

    def forward(k, flips, to_number, peer, condition=None):
        own = isinstance(k, int) and k == 0 and not flips

        def make():
            target = piece(k, flips)
            return pltpu.make_async_remote_copy(
                src_ref=source if own else target,
                dst_ref=target,
                send_sem=send.at[to_number],
                recv_sem=arrive.at[to_number],
                device_id=peer,
                device_id_type=MESH,
            )

        link.emit(make, condition)

    def hand_on(k, flips, axes, along_z):
        if along_z:
            forward(k, flips, number(1, flips), link.at_z(z + 1), z < deep - 1)
            forward(k, flips, number(deep - 1, flips), link.at_z(z - 1), z > 0)
        for axis in axes:
            forward(k, flips, number(k, flips | {axis}), link.peer(axis))

    def take(k, flips):
        arrived(piece(k, flips), arrive.at[number(k, flips)])

    hand_on(0, none, before + after, cut >= 0)
    got = [none]
    for i, axis in enumerate(before):
        for flips in got:
            yield
            take(0, flips | {axis})
            hand_on(0, flips | {axis}, before[i + 1 :] + after, True)
        got = got + [flips | {axis} for flips in got]
    ks = [0]
    if cut >= 0:
        for k in link.order:
            below = z >= k
            onward = jnp.where(below, k + 1, k - 1)
            more = jnp.where(below, z < deep - 1, z > 0)
            following = link.at_z(jnp.where(below, z + 1, z - 1))
            for flips in got:
                yield
                take(k, flips)
                forward(k, flips, number(onward, flips), following, more)
                hand_on(k, flips, after, False)
        ks = ks + link.order
    for i, axis in enumerate(after):
        for k in ks:
            for flips in got:
                yield
                take(k, flips | {axis})
                hand_on(k, flips | {axis}, after[i + 1 :], False)
        got = got + [flips | {axis} for flips in got]


def shuffle(link, groups, source, at, send, arrive):
    def make(j):
        target = (link.me + j) % groups
        return pltpu.make_async_remote_copy(
            src_ref=source(target),
            dst_ref=at(link.me),
            send_sem=send.at[j],
            recv_sem=arrive.at[j],
            device_id={EXPERT: target, TENSOR: link.part},
            device_id_type=MESH,
        )

    for j in range(1, groups):
        link.emit(functools.partial(make, j))
    for j in range(1, groups):
        yield
        arrived(at((link.me + groups - j) % groups), arrive.at[j])


def run(tasks):
    tasks = list(tasks)
    while tasks:
        tasks = [task for task in tasks if next(task, run) is not run]


def add_rows(count, store):
    lax.fori_loop(0, count, lambda i, carry: (store(i), carry)[1], 0)


def sum_all_kernel(deep, chunks, count, *refs):
    partials, outs = refs[:count], refs[count : 2 * count]
    total = len(chunks)
    rest = refs[2 * count :]
    own_buf, from_core = rest[:total], rest[total : 2 * total]
    from_first, from_second = rest[2 * total : 3 * total], rest[3 * total : 4 * total]
    from_deep = rest[4 * total : 5 * total]
    send, arrive, own = rest[5 * total :]
    z, x, y, c = place()
    others = [device((z + k) % deep, x, y, c) for k in range(1, deep)]
    twin, across, beside = (
        device(z, 1 - x, y, c),
        device(z, x, 1 - y, c),
        device(z, x, y, 1 - c),
    )
    greet(others + [twin, across, beside])
    copies, loads = [], []
    for n, (i, left, wide, order) in enumerate(chunks):
        span = pl.ds(left, wide)
        copies.append(
            push(
                partials[i].at[:, 1 - c, :, span],
                from_core[n],
                send.at[n, 0],
                arrive.at[n, 0],
                beside,
            )
        )
        loads.append(bring(partials[i].at[:, c, :, span], own_buf[n], own.at[n]))

    def index(order, depth, on_first, on_second):
        on_x, on_y = (on_first, on_second) if order == 0 else (on_second, on_first)
        return (depth * PAIR + on_x) * PAIR + on_y

    def stage_core(n):
        _, _, _, order = chunks[n]
        buf, other = own_buf[n], from_core[n]
        loads[n].wait()
        arrived(other, arrive.at[n, 0])

        def add(k):
            buf[k] = (buf[k].astype(jnp.float32) + other[k].astype(jnp.float32)).astype(
                jnp.bfloat16
            )

        add_rows(deep * PAIR * PAIR, add)
        mine = x if order == 0 else y
        for depth in range(deep):
            for s in range(PAIR):
                number = 1 + depth * PAIR + s
                copies.append(
                    push(
                        buf.at[index(order, depth, 1 - mine, s)],
                        from_first[n].at[depth * PAIR + s],
                        send.at[n, number],
                        arrive.at[n, number],
                        twin if order == 0 else across,
                    )
                )

    def stage_first(n):
        _, _, _, order = chunks[n]
        buf, other = own_buf[n], from_first[n]
        mine, following = (x, y) if order == 0 else (y, x)
        for number in range(1, 1 + PAIR * deep):
            arrived(other.at[number - 1], arrive.at[n, number])

        def add(k):
            at = index(order, k // PAIR, mine, k % PAIR)
            buf[at] = (buf[at].astype(jnp.float32) + other[k].astype(jnp.float32)).astype(
                jnp.bfloat16
            )

        add_rows(deep * PAIR, add)
        for depth in range(deep):
            number = 1 + PAIR * deep + depth
            copies.append(
                push(
                    buf.at[index(order, depth, mine, 1 - following)],
                    from_second[n].at[depth],
                    send.at[n, number],
                    arrive.at[n, number],
                    across if order == 0 else twin,
                )
            )

    def stage_second(n):
        _, _, _, order = chunks[n]
        buf, other = own_buf[n], from_second[n]
        mine, following = (x, y) if order == 0 else (y, x)
        base = 1 + PAIR * deep
        for depth in range(deep):
            arrived(other.at[depth], arrive.at[n, base + depth])

        def add(k):
            at = index(order, k, mine, following)
            buf[at] = (buf[at].astype(jnp.float32) + other[k].astype(jnp.float32)).astype(
                jnp.bfloat16
            )

        add_rows(deep, add)
        for k in range(1, deep):
            number = base + deep + k - 1
            copies.append(
                push(
                    buf.at[index(order, (z + k) % deep, mine, following)],
                    from_deep[n].at[k - 1],
                    send.at[n, number],
                    arrive.at[n, number],
                    others[k - 1],
                )
            )

    def stage_deep(n):
        i, left, wide, order = chunks[n]
        base = 1 + PAIR * deep + deep
        for k in range(1, deep):
            arrived(from_deep[n].at[k - 1], arrive.at[n, base + k - 1])
        mine, following = (x, y) if order == 0 else (y, x)
        result = own_buf[n][index(order, z, mine, following)].astype(jnp.float32)
        for k in range(deep - 1):
            result = result + from_deep[n][k].astype(jnp.float32)
        outs[i][:, pl.ds(left, wide)] = result

    for step in range(total + 3):
        for lag, stage in enumerate((stage_core, stage_first, stage_second, stage_deep)):
            if 0 <= step - lag < total:
                stage(step - lag)
    for copy in copies:
        copy.wait_send()


def sum_all(calls, groups, parts, arrays):
    deep = groups // PAIR
    rows = arrays[0].shape[0] // (groups * parts)
    budget, calls_of, used = 46 * 2**20, [[]], 0
    number = 0
    for i, array in enumerate(arrays):
        left = 0
        while left < array.shape[1]:
            wide = min(512, array.shape[1] - left)
            if 0 < array.shape[1] - left - wide < 512 // 2:
                wide = array.shape[1] - left
            cost = 2 * rows * wide * (4 * deep * 2 + 2 * deep + deep + deep) + 4 * rows * wide
            if used + cost > budget:
                calls_of.append([])
                used = 0
            used += cost
            calls_of[-1].append((i, left, wide, number % 2))
            number += 1
            left += wide
    views = [a.reshape(groups * parts // PAIR, PAIR, rows, a.shape[1]) for a in arrays]
    pieces = [[] for _ in arrays]
    for chunks in calls_of:
        used_arrays = sorted({c[0] for c in chunks})
        bounds = {
            i: (min(c[1] for c in chunks if c[0] == i), sum(c[2] for c in chunks if c[0] == i))
            for i in used_arrays
        }
        local = [(used_arrays.index(i), left, wide, order) for i, left, wide, order in chunks]
        count = len(used_arrays)
        many = deep * PAIR * PAIR

        def bufs(n):
            return [pltpu.VMEM((n, rows, wide), jnp.bfloat16) for _, _, wide, _ in chunks]

        sems = DMA((len(chunks), 1 + PAIR * deep + deep + deep))
        outs = pl.pallas_call(
            functools.partial(
                sum_all_kernel,
                deep,
                tuple(local),
                count,
            ),
            in_specs=[ANY] * count,
            out_specs=[IN_VMEM] * count,
            out_shape=[
                jax.ShapeDtypeStruct((rows, arrays[i].shape[1]), jnp.float32)
                for i in used_arrays
            ],
            scratch_shapes=bufs(many)
            + bufs(many)
            + bufs(PAIR * deep)
            + bufs(deep)
            + bufs(deep - 1)
            + [sems, sems, DMA((len(chunks),))],
            compiler_params=calls.params(),
            name="sum_all",
        )(*[views[i] for i in used_arrays])
        for i, out in zip(used_arrays, outs):
            pieces[i].append(out[:, bounds[i][0] : bounds[i][0] + bounds[i][1]])
    return [p[0] if len(p) == 1 else jnp.concatenate(p, axis=1) for p in pieces]


def swap_halves(values, half):
    lane = lax.broadcasted_iota(jnp.int32, values.shape, 1)
    wide = values.shape[1]
    return jnp.where(
        lane < half, pltpu.roll(values, wide - half, 1), pltpu.roll(values, half, 1)
    )


def turn(values, cosine, sinusoid):
    return values * cosine + swap_halves(values, ROPE // 2) * sinusoid


def full_gain(gains, row, size, groups):
    total = size * groups
    wide = gains.shape[1]
    result = jnp.zeros((8, total), jnp.float32)
    for e in range(groups):
        share = jnp.broadcast_to(gains[e * 8 + row : e * 8 + row + 1, :], (8, wide))
        if total > wide:
            share = jnp.concatenate([share, jnp.zeros((8, total - wide), jnp.float32)], axis=1)
        result = result + (pltpu.roll(share, e * size, 1) if e else share)
    return result[:1]


def rows_loop(count, step, work):
    def one(i, carry):
        work(pl.ds(pl.multiple_of(i * step, step), step))
        return carry

    lax.fori_loop(0, count // step, one, 0)


def front_kernel(groups, sizes, plan, names, *refs):
    ref = Bag(zip(names, refs))
    deep = groups // PAIR
    link = Link(deep)
    z, x, y, c, part = link.z, link.x, link.y, link.c, link.part
    send, arrive, own, leave = ref.send, ref.arrive, ref.own, ref.leave
    link.greet(groups, "eyc")
    loads, numbers, landing = {}, {}, Bag()
    row_of = {}
    for n, (name, axis, cut, over, orders, home) in enumerate(plan):
        numbers[name] = n
        landing[name] = ref["b_" + name] if home == VMEM_ else ref["o_" + name]

    stream_row = [0]

    def tasks_of(name):
        n = numbers[name]
        _, axis, cut, over, orders, home = plan[n]
        source, target = ref["i_" + name], landing[name]
        if cut is not None:
            source = slot(source, cut[0], part, cut[1])
        if over == READY:
            loads[name] = bring(source, target, own.at[n])
            return []
        if over == SHUFFLE:
            size = source.shape[2]
            keep = ref["k_" + name]
            loads[name] = bring(source.at[link.me], keep, own.at[n])
            row = stream_row[0]
            stream_row[0] += 1
            return [
                shuffle(
                    link,
                    groups,
                    lambda e: source.at[e],
                    lambda e: slot(target, axis, e, size),
                    send.at[row],
                    arrive.at[row],
                )
            ]
        size = cut[1] if cut is not None and cut[0] == axis else source.shape[axis]

        def home_of(sz, sx, sy, sc):
            index = sz * PAIR + sx
            if over == "all":
                index = (index * PAIR + sy) * PAIR + sc
            return slot(target, axis, index, size)

        mine = home_of(z, x, y, c)
        if home == VMEM_:
            loads[name] = bring(source, mine, own.at[n])
        else:
            loads[name] = bring(source, ref["k_" + name], own.at[n])
        return [stream for stream in streams_of(source, home_of, orders)]

    def streams_of(source, home_of, orders):
        result = []
        for i, order in enumerate(orders):
            row = stream_row[0]
            stream_row[0] += 1
            if len(orders) == 1:
                at, part_source = home_of, source
            else:
                wide = source.shape[1] // len(orders)
                span = pl.ds(i * wide, wide)

                def at(*where, span=span):
                    return home_of(*where).at[:, span]

                part_source = source.at[:, span]
            result.append(spread(link, order, part_source, at, send.at[row], arrive.at[row]))
        return result

    def begin(*which):
        found = [task for name in which for task in tasks_of(name)]
        return [task for task in found if next(task, run) is not run]

    gain_tasks = begin(GAINS)
    stem_tasks = begin(QUERY_DOWN, LATENT_DOWN)
    late_tasks = begin(OUT_GRAD)

    def complete(name):
        n = numbers[name]
        loads.pop(name).wait()
        _, axis, cut, over, _, home = plan[n]
        if home == "hbm":
            keep, target = ref["k_" + name], landing[name]
            index = link.me
            if over == "all":
                index = link.me * PAIR * PAIR + part
            move = pltpu.make_async_copy(
                keep, slot(target, axis, index, keep.shape[axis]), own.at[n]
            )
            move.start()
            stores.append(move)

    stores = []

    def keep_out(name, source=None):
        moves = len(stores)
        move = bring(source if source is not None else landing[name], ref["o_" + name], leave.at[len(kept)])
        kept.append(move)

    kept = []
    block_ref = ref.i_block
    first_ref, middle_ref = ref.b_first, ref.b_middle
    width = block_ref.shape[1]
    row_count = block_ref.shape[0]
    sub = row_count // (PAIR * PAIR)

    complete(GAINS)
    run(gain_tasks)
    gains = landing.gains
    attention_gain = full_gain(gains, 0, sizes[0], groups)

    def first_norm(span):
        values = block_ref[span, :].astype(jnp.float32)
        inverse = lax.rsqrt(jnp.mean(values * values, axis=-1, keepdims=True) + EPSILON)
        first_ref[span, :] = (values * inverse * attention_gain).astype(jnp.bfloat16)

    rows_loop(row_count, 32, first_norm)
    for _ in range(deep - 1):
        advance(stem_tasks, 1)
        advance(late_tasks, 1)
    up_tasks = begin(QUERY_UP, LATENT_UP)
    for name in (QUERY_DOWN, LATENT_DOWN):
        complete(name)
    run(stem_tasks)
    ref.b_query_cut[...] = matmul(first_ref[...], landing.query_down[...]).astype(
        jnp.bfloat16
    )
    ref.b_latent_cut[...] = matmul_nt(landing.latent_down[...], first_ref[...]).astype(
        jnp.bfloat16
    )
    query_lat, latent_t = ref.b_query_lat, ref.b_latent_t
    query_cut, latent_cut = ref.b_query_cut, ref.b_latent_cut
    stem_numbers = len(plan)
    stem_tasks = streams_of(
        query_cut, lambda sz, sx, sy, sc: slot(query_lat, 1, sy * PAIR + sc, query_cut.shape[1]), ("yc",)
    ) + streams_of(
        latent_cut, lambda sz, sx, sy, sc: slot(latent_t, 0, sy * PAIR + sc, latent_cut.shape[0]), ("yc",)
    )
    stem_tasks = [task for task in stem_tasks if next(task, run) is not run]
    query_lat[:, pl.ds(pl.multiple_of(part * query_cut.shape[1], LANES), query_cut.shape[1])] = (
        query_cut[...]
    )
    latent_t[pl.ds(pl.multiple_of(part * latent_cut.shape[0], 16), latent_cut.shape[0]), :] = (
        latent_cut[...]
    )
    query_gain = full_gain(gains, 2, sizes[2], groups)
    latent_gain = full_gain(gains, 3, sizes[3], groups)
    cosine, sinusoid = ref.i_cosine, ref.i_sinusoid
    advance(up_tasks, 1)
    run(stem_tasks)
    advance(late_tasks, 2)

    query_n, latent_n, keys = ref.b_query_n, ref.b_latent_n, ref.b_keys

    def query_norm(span):
        values = query_lat[span, :].astype(jnp.float32)
        inverse = lax.rsqrt(jnp.mean(values * values, axis=-1, keepdims=True) + EPSILON)
        query_n[span, :] = (values * inverse * query_gain).astype(jnp.bfloat16)

    rows_loop(row_count, 32, query_norm)
    for _ in range(deep - 2):
        advance(up_tasks, 1)
        advance(late_tasks, 2)
    out_tasks = begin(OUT_PROJ, ROUTER, ROUTES)
    shared_tasks = begin(SHARED)
    latent_rank = latent_n.shape[1]
    latent = latent_t[:latent_rank, :].astype(jnp.float32).T
    inverse = lax.rsqrt(jnp.mean(latent * latent, axis=-1, keepdims=True) + EPSILON)
    latent_n[...] = (latent * inverse * latent_gain).astype(jnp.bfloat16)
    rope_rows = latent_t[latent_rank:, :].astype(jnp.float32).T
    rope_rows = jnp.concatenate(
        [rope_rows, jnp.zeros((row_count, LANES - ROPE), jnp.float32)], axis=1
    )
    key_rope = turn(rope_rows, cosine[...], sinusoid[...])[:, :ROPE].astype(jnp.bfloat16)

    complete(QUERY_UP)
    complete(LATENT_UP)
    run(up_tasks)
    queries, values_ref, attended = ref.b_queries, ref.b_values, ref.b_attended
    heads = queries.shape[0]
    head_width = NOPE + ROPE
    projected = matmul(query_n[...], landing.query_up[...])
    shifted = pltpu.roll(projected, projected.shape[1] - ROPE, 1)
    keyval = matmul(latent_n[...], landing.latent_up[...])
    for h in range(heads):
        start = h * head_width
        base, start = (projected, start) if start % LANES == 0 else (shifted, start - ROPE)
        queries[h, :, :NOPE] = base[:, start : start + NOPE].astype(jnp.bfloat16)
        tail = base[:, start + NOPE : start + NOPE + LANES]
        if tail.shape[1] < LANES:
            tail = jnp.concatenate(
                [tail, jnp.zeros((row_count, LANES - tail.shape[1]), jnp.float32)], axis=1
            )
        queries[h, :, NOPE:] = turn(tail, cosine[...], sinusoid[...])[:, :ROPE].astype(
            jnp.bfloat16
        )
        left = h * (NOPE + VD)
        keys[h, :, :NOPE] = keyval[:, left : left + NOPE].astype(jnp.bfloat16)
        keys[h, :, NOPE:] = key_rope
        values_ref[h] = keyval[:, left + NOPE : left + NOPE + VD].astype(jnp.bfloat16)
        scores = matmul_nt(queries[h], keys[h]) * head_width ** (-0.5)
        scores = jnp.where(ref.i_allowed[...] > 0, scores, -1e30)
        powers = jnp.exp(scores - jnp.max(scores, axis=-1, keepdims=True))
        probs = (powers / jnp.sum(powers, axis=-1, keepdims=True)).astype(jnp.bfloat16)
        attended[:, h * VD : (h + 1) * VD] = matmul(probs, values_ref[h]).astype(jnp.bfloat16)
        if h < deep - 1:
            advance(out_tasks, 1)
        advance(late_tasks, 2)
    advance(out_tasks, max(0, deep - 1 - heads))
    for name in (OUT_PROJ, ROUTER, ROUTES):
        complete(name)
    run(out_tasks)
    for name in (QUERY_DOWN, LATENT_DOWN, QUERY_UP, LATENT_UP, OUT_PROJ, GAINS, ROUTER):
        keep_out(name)
    for name in (FIRST, QUERY_LAT, LATENT_T, QUERY_N, LATENT_N, QUERIES, KEYS, VALUES, ATTENDED):
        keep_out(name, ref["b_" + name])

    partial, from_beside = ref.b_partial, ref.b_from_beside
    give, from_across = ref.b_give, ref.b_from_across
    swap_send, swap_arrive = ref.swap_send, ref.swap_arrive
    for quarter in range(PAIR * PAIR):
        partial[quarter // PAIR, quarter % PAIR] = matmul(
            attended[quarter * sub : (quarter + 1) * sub, :], landing.out_proj[...]
        ).astype(jnp.bfloat16)

    def beside_copy():
        return pltpu.make_async_remote_copy(
            src_ref=partial.at[:, 1 - c],
            dst_ref=from_beside,
            send_sem=swap_send.at[0],
            recv_sem=swap_arrive.at[0],
            device_id=link.peer("c"),
            device_id_type=MESH,
        )

    def across_copy():
        return pltpu.make_async_remote_copy(
            src_ref=give,
            dst_ref=from_across,
            send_sem=swap_send.at[1],
            recv_sem=swap_arrive.at[1],
            device_id=link.peer("y"),
            device_id_type=MESH,
        )

    link.emit(beside_copy)
    advance(late_tasks, 1)
    arrived(from_beside, swap_arrive.at[0])
    give[...] = partial[1 - y, c] + from_beside[1 - y]
    link.emit(across_copy)
    complete(OUT_GRAD)
    complete(SHARED)
    residual = block_ref[pl.ds(pl.multiple_of(part * sub, sub), sub), :].astype(jnp.float32)
    middle_ref[...] = (
        residual + partial[y, c].astype(jnp.float32) + from_beside[y].astype(jnp.float32)
    )
    advance(late_tasks, 1)
    arrived(from_across, swap_arrive.at[1])
    middle = middle_ref[...] + from_across[...].astype(jnp.float32)
    middle_ref[...] = middle
    ffn_gain = full_gain(gains, 1, sizes[1], groups)
    norms = ref.b_norms
    norms[...] = jnp.zeros(norms.shape, jnp.float32)
    for i, gain in enumerate((attention_gain, ffn_gain, query_gain, latent_gain)):
        norms[i : i + 1, : gain.shape[1]] = gain
    keep_out("norms", norms)
    inverse = lax.rsqrt(jnp.mean(middle * middle, axis=-1, keepdims=True) + EPSILON)
    second_ref, weights_ref, chosen_ref = ref.b_second, ref.b_weights, ref.b_chosen
    second_ref[...] = (middle * inverse * ffn_gain).astype(jnp.bfloat16)
    logits = matmul_nt(second_ref[...], landing.router[...])
    experts = logits.shape[1]
    advance(late_tasks, 1)
    routes_rows = ref.i_route_rows[pl.ds(pl.multiple_of(part * sub, sub), sub), :]
    ids = lax.broadcasted_iota(jnp.int32, (sub, experts), 1)
    chosen = jnp.zeros((sub, experts), jnp.float32)
    picked = jax.nn.sigmoid(logits)
    for k in range(routes_rows.shape[1]):
        chosen = jnp.where(routes_rows[:, k : k + 1] == ids, picked, chosen)
    totals = jnp.sum(chosen, axis=-1, keepdims=True)
    weights_ref[...] = jnp.zeros(weights_ref.shape, jnp.float32)
    weights_ref[:, :experts] = ROUTE_SCALE * chosen / totals
    chosen_ref[...] = jnp.zeros(chosen_ref.shape, jnp.float32)
    chosen_ref[:, :experts] = chosen

    def row_home(name):
        def home_of(sz, sx, sy, sc):
            index = ((sz * PAIR + sx) * PAIR + sy) * PAIR + sc
            return slot(ref["o_" + name], 0, index, sub)

        return home_of

    all_tasks = streams_of(weights_ref, row_home(WEIGHTS), (ZXYC,))
    all_tasks += streams_of(second_ref, row_home(TOKENS), (ZXYC, "zyxc") * 2)
    all_tasks = [task for task in all_tasks if next(task, run) is not run]
    mine = link.me * PAIR * PAIR + part
    kept.append(bring(second_ref, slot(ref.o_tokens, 0, mine, sub), leave.at[len(kept)]))
    kept.append(bring(weights_ref, slot(ref.o_weights, 0, mine, sub), leave.at[len(kept)]))
    keep_out("middle", middle_ref)
    keep_out("chosen", chosen_ref)
    run(late_tasks + all_tasks + shared_tasks)
    link.drain()
    for move in stores + kept:
        move.wait()


def front_stage(calls, groups, parts, sizes, items, block, route_rows, allowed, cosine, sinusoid):
    deep = groups // PAIR
    rows, width = block.shape
    sub = rows // parts
    bf16, f32 = jnp.bfloat16, jnp.float32
    names, inputs, in_specs = [], [], []
    out_names, out_shape, plan, scratch = [], [], [], Bag()
    streams = 0
    for name, array, axis, cut, over, orders, home in items:
        names.append("i_" + name)
        inputs.append(array)
        in_specs.append(ANY)
        shape = list(array.shape)
        if over == SHUFFLE:
            shape = shape[1:]
        if cut is not None:
            shape[cut[0]] = cut[1]
        if home == "hbm":
            scratch["k_" + name] = pltpu.VMEM(tuple(shape), array.dtype)
        if over != READY:
            shape[axis] *= groups * parts if over == "all" else groups
            streams += max(1, len(orders))
        if home == VMEM_:
            scratch["b_" + name] = pltpu.VMEM(tuple(shape), array.dtype)
        out_names.append(name)
        out_shape.append(jax.ShapeDtypeStruct(tuple(shape), array.dtype))
        plan.append((name, axis, cut, over, orders, home))
    for name, array in (
        ("block", block),
        ("route_rows", route_rows),
        ("allowed", allowed),
        ("cosine", cosine),
        ("sinusoid", sinusoid),
    ):
        names.append("i_" + name)
        inputs.append(array)
        in_specs.append(IN_VMEM)
    shape_of = Bag((name, shape.shape) for name, shape in zip(out_names, out_shape))
    query_cut, latent_cut = shape_of.query_down[1], shape_of.latent_down[0]
    query_rank, latent_rank = shape_of.query_up[0], shape_of.latent_up[0]
    heads = shape_of.latent_up[1] // (NOPE + VD)
    experts = shape_of.router[0]
    lanes = experts + -experts % LANES
    half = parts // PAIR
    buffers = Bag(
        first=((rows, width), bf16),
        query_lat=((rows, query_cut * parts), bf16),
        latent_t=((latent_cut * parts, rows), bf16),
        query_n=((rows, query_rank), bf16),
        latent_n=((rows, latent_rank), bf16),
        queries=((heads, rows, NOPE + ROPE), bf16),
        keys=((heads, rows, NOPE + ROPE), bf16),
        values=((heads, rows, VD), bf16),
        attended=((rows, heads * VD), bf16),
        middle=((sub, width), f32),
        chosen=((sub, lanes), f32),
        norms=((8, width), f32),
    )
    for name, (shape, dtype) in buffers.items():
        out_names.append(name)
        out_shape.append(jax.ShapeDtypeStruct(shape, dtype))
    inner = Bag(
        query_cut=((rows, query_cut), bf16),
        latent_cut=((latent_cut, rows), bf16),
        partial=((half, PAIR, sub, width), bf16),
        from_beside=((half, sub, width), bf16),
        give=((sub, width), bf16),
        from_across=((sub, width), bf16),
        second=((sub, width), bf16),
        weights=((sub, lanes), f32),
    )
    for name, (shape, dtype) in (buffers | inner).items():
        scratch["b_" + name] = pltpu.VMEM(shape, dtype)
    out_names += [TOKENS, WEIGHTS]
    out_shape += [
        jax.ShapeDtypeStruct((sub * groups * parts, width), bf16),
        jax.ShapeDtypeStruct((sub * groups * parts, lanes), f32),
    ]
    streams += 2 + 1 + 4
    scratch.send = scratch.arrive = DMA((streams, 8 * deep))
    scratch.own = DMA((len(items),))
    scratch.leave = DMA((len(out_names),))
    scratch.swap_send = scratch.swap_arrive = DMA((2,))
    names += ["o_" + name for name in out_names] + list(scratch)
    results = pl.pallas_call(
        functools.partial(front_kernel, groups, tuple(sizes), tuple(plan), tuple(names)),
        in_specs=in_specs,
        out_specs=[ANY] * len(out_names),
        out_shape=out_shape,
        scratch_shapes=list(scratch.values()),
        compiler_params=calls.params(),
        name="front",
    )(*inputs)
    return Bag(zip(out_names, results))


def device_total(link, order, own, give, bufs, result, send, arrive):
    deep, z, x, y = link.deep, link.z, link.x, link.y
    from_core, from_first, from_second, from_deep = bufs
    mine, following = (x, y) if order == 0 else (y, x)
    near, far = (link.peer("x"), link.peer("y")) if order == 0 else (link.peer("y"), link.peer("x"))

    def at(depth, on_first, on_second):
        on_x, on_y = (on_first, on_second) if order == 0 else (on_second, on_first)
        return (depth * PAIR + on_x) * PAIR + on_y

    def hop(number, source, target, peer):
        def make():
            return pltpu.make_async_remote_copy(
                src_ref=source(),
                dst_ref=target,
                send_sem=send.at[number],
                recv_sem=arrive.at[number],
                device_id=peer,
                device_id_type=MESH,
            )

        link.emit(make)

    hop(0, lambda: give, from_core, link.peer("c"))
    yield
    arrived(from_core, arrive.at[0])

    def add_core(k):
        own[k] = own[k] + from_core[k]

    add_rows(deep * PAIR * PAIR, add_core)
    for depth in range(deep):
        for s in range(PAIR):
            n = depth * PAIR + s
            hop(1 + n, lambda d=depth, s=s: own.at[at(d, 1 - mine, s)], from_first.at[n], near)
    yield
    for n in range(PAIR * deep):
        arrived(from_first.at[n], arrive.at[1 + n])

    def add_first(k):
        here = at(k // PAIR, mine, k % PAIR)
        own[here] = own[here] + from_first[k]

    add_rows(deep * PAIR, add_first)
    base = 1 + PAIR * deep
    for depth in range(deep):
        hop(
            base + depth,
            lambda d=depth: own.at[at(d, mine, 1 - following)],
            from_second.at[depth],
            far,
        )
    yield
    for depth in range(deep):
        arrived(from_second.at[depth], arrive.at[base + depth])

    def add_second(k):
        here = at(k, mine, following)
        own[here] = own[here] + from_second[k]

    add_rows(deep, add_second)
    base = base + deep - 1
    for k in range(1, deep):
        hop(
            base + k,
            lambda k=k: own.at[at((z + k) % deep, mine, following)],
            from_deep.at[k - 1],
            link.at_z((z + k) % deep),
        )
    total = own[at(z, mine, following)].astype(jnp.float32)
    yield
    for k in range(1, deep):
        arrived(from_deep.at[k - 1], arrive.at[base + k])
        total = total + from_deep[k - 1].astype(jnp.float32)
    result[...] = total


def total_buffers(deep, rows, wide):
    shapes = (deep * PAIR * PAIR, PAIR * deep, deep, deep - 1)
    return [pltpu.VMEM((n, rows, wide), jnp.bfloat16) for n in shapes]


def total_hops(deep):
    return PAIR * deep + 2 * deep


def route_kernel(ids_ref, routes_ref, x_ref, g_ref, weights_ref, xr_ref, gr_ref, p_ref, w_ref):
    local = ids_ref.shape[0]
    rows = x_ref.shape[0]
    f32, bf16 = jnp.float32, jnp.bfloat16
    ids = ids_ref[...]
    named = jnp.zeros((local, rows), f32)
    for k in range(routes_ref.shape[0]):
        named = jnp.where(routes_ref[k : k + 1, :] == ids, 1.0, named)
    before = lax.broadcasted_iota(jnp.int32, (rows, rows), 0)
    after = lax.broadcasted_iota(jnp.int32, (rows, rows), 1)
    rank = matmul(named.astype(bf16), jnp.where(before < after, 1.0, 0.0).astype(bf16))
    lanes = weights_ref.shape[1]
    mine = jnp.where(lax.broadcasted_iota(jnp.int32, (local, lanes), 1) == ids, 1.0, 0.0)
    weights = lax.dot_general(
        mine,
        weights_ref[...],
        (((1,), (1,)), ((), ())),
        precision=lax.Precision.HIGHEST,
        preferred_element_type=f32,
    )
    slots = lax.broadcasted_iota(jnp.int32, (CAP, rows), 0).astype(f32)
    picks = []
    for j in range(local):
        pick = jnp.where(slots == rank[j : j + 1, :], named[j : j + 1, :], 0.0)
        w_ref[0, j * CAP : (j + 1) * CAP, :] = jnp.sum(
            pick * weights[j : j + 1, :], axis=1, keepdims=True
        )
        picks.append(pick.astype(bf16))
    picks = jnp.concatenate(picks, axis=0)
    p_ref[0] = picks
    xr_ref[0] = matmul(picks, x_ref[...]).astype(bf16)
    gr_ref[0] = matmul(picks, g_ref[...]).astype(bf16)


def route_stage(groups, own_ids, routes_t, tokens, gradients, weights):
    local = own_ids.shape[0]
    rows, width = tokens.shape[0] // groups, tokens.shape[1]
    slots = local * CAP
    row_spec = pl.BlockSpec((rows, width), lambda b: (b, 0))
    slot_spec = pl.BlockSpec((1, slots, width), lambda b: (b, 0, 0))
    slot_shape = jax.ShapeDtypeStruct((groups, slots, width), jnp.bfloat16)
    lanes = weights.shape[1]
    return pl.pallas_call(
        route_kernel,
        grid=(groups,),
        in_specs=[
            pl.BlockSpec((local, 1), lambda b: (0, 0)),
            pl.BlockSpec((routes_t.shape[0], rows), lambda b: (0, b)),
            row_spec,
            row_spec,
            pl.BlockSpec((rows, lanes), lambda b: (b, 0)),
        ],
        out_specs=[
            slot_spec,
            slot_spec,
            pl.BlockSpec((1, slots, rows), lambda b: (b, 0, 0)),
            pl.BlockSpec((1, slots, 1), lambda b: (b, 0, 0)),
        ],
        out_shape=[
            slot_shape,
            slot_shape,
            jax.ShapeDtypeStruct((groups, slots, rows), jnp.bfloat16),
            jax.ShapeDtypeStruct((groups, slots, 1), jnp.float32),
        ],
        compiler_params=pltpu.CompilerParams(vmem_limit_bytes=VMEM_BYTES),
        name="route",
    )(own_ids[:, None], routes_t, tokens, gradients, weights)


def mix_kernel(groups, chunks, names, *refs):
    ref = Bag(zip(names, refs))
    deep = groups // PAIR
    bf16, f32 = jnp.bfloat16, jnp.float32
    link = Link(deep)
    link.greet(groups, "eyc")
    blocks, slots, rows = ref.b_picks.shape
    sub = ref.o_dsecond.shape[0]
    width = ref.i_tokens.shape[1]
    units = ref.i_shared.shape[0] // 3
    loads = [bring(ref.i_picks, ref.b_picks, ref.load.at[0])]
    loads.append(bring(ref.i_shared, ref.b_shared, ref.load.at[1]))

    def fetch(b, at):
        span = pl.ds(pl.multiple_of(b * rows, rows), rows)
        return (
            pltpu.make_async_copy(ref.i_tokens.at[span, :], ref.b_x.at[at], ref.fetch.at[at, 0]),
            pltpu.make_async_copy(ref.i_gradients.at[span, :], ref.b_g.at[at], ref.fetch.at[at, 1]),
        )

    for copy in fetch(0, 0):
        copy.start()
    many = len(chunks)
    work = [(True, *chunk) for chunk in chunks] + [(False, *chunk) for chunk in chunks[:-1]]

    def source_of(n):
        back, left, wide = work[n]
        source = ref.i_back if back else ref.i_produced
        return pltpu.make_async_copy(
            source.at[:, :, pl.ds(left, wide)],
            ref.b_source.at[turn_of[n], :, :, pl.ds(0, wide)],
            ref.pull.at[turn_of[n]],
        )

    has_source = [n != many - 1 for n in range(len(work))]
    order = [many - 1] + [n for n in range(len(work)) if has_source[n]]
    turn_of = {n: i % 2 for i, n in enumerate(order)}
    for load in loads:
        load.wait()
    ref.b_acc[...] = jnp.zeros(ref.b_acc.shape, f32)

    def block(b, carry):
        at = b % 2

        @pl.when(b + 1 < blocks)
        def _():
            for copy in fetch(b + 1, 1 - at):
                copy.start()

        for copy in fetch(b, at):
            copy.wait()
        row_inputs, cotangent = ref.b_x[at], ref.b_g[at]
        pre = matmul_nt(row_inputs, ref.b_shared[: 2 * units, :])
        gate_pre, up_pre = pre[:, :units], pre[:, units:]
        sigmoid_gate, hidden = swiglu(gate_pre, up_pre)
        dhidden = matmul_nt(cotangent, ref.b_shared[2 * units :, :])
        gate_grad, up_grad = swiglu_back(dhidden, gate_pre, up_pre, sigmoid_gate)
        both = jnp.concatenate([gate_grad, up_grad], axis=1)
        ref.b_hidden[b] = hidden
        ref.b_both[b] = both
        ref.b_acc[: 2 * units, :] += matmul_tn(both, row_inputs)
        ref.b_acc[2 * units :, :] += matmul_tn(hidden, cotangent)
        return carry

    source_of(order[1]).start()
    lax.fori_loop(0, blocks, block, 0)
    ref.b_grad[...] = ref.b_acc[...].astype(bf16)
    grad_out = bring(ref.b_grad, ref.o_shared, ref.load.at[0])
    dw_lane = lax.broadcasted_iota(jnp.int32, (slots, chunks[-1][1]), 1)
    tasks, outs = [], []
    pending = [n for n in order if has_source[n]]
    for n in order:
        back, left, wide = work[n]
        if has_source[n]:
            pending.pop(0)
            if pending:
                source_of(pending[0]).start()
            source_of(n).wait()
        staged = None if back else ref.b_stage.at[n % 2]
        if not back and len(outs) >= 2:
            outs[-2].wait()
            outs[-2] = None

        def one(b, carry, n=n, back=back, left=left, wide=wide, staged=staged):
            picks = ref.b_picks[b]
            if not has_source[n]:
                values = matmul_tn(
                    picks, jnp.where(dw_lane == ref.i_lanes[...], ref.i_dweights[b], 0.0).astype(bf16)
                )
            else:
                span = slice(left, left + wide)
                values = matmul_tn(picks, ref.b_source[turn_of[n], b, :, :wide])
                if back:
                    values += matmul(ref.b_both[b], ref.b_shared[: 2 * units, span])
                else:
                    values += matmul(ref.b_hidden[b], ref.b_shared[2 * units :, span])
            values = values.astype(bf16)
            for y in range(PAIR):
                for c in range(PAIR):
                    q = y * PAIR + c
                    piece = values[q * sub : (q + 1) * sub, :]
                    if back:
                        ref["p%d" % n][c, b * PAIR + y] = piece
                    else:
                        staged[b * PAIR + y, c] = piece
            return carry

        lax.fori_loop(0, blocks, one, 0)
        if back:
            task = device_total(
                link,
                n % 2,
                ref["p%d" % n].at[link.c],
                ref["p%d" % n].at[1 - link.c],
                [ref["f%d_%d" % (n, k)] for k in range(4)],
                ref.o_dsecond.at[:, pl.ds(left, wide)],
                ref.send.at[n],
                ref.arrive.at[n],
            )
            advance(tasks)
            tasks += begun([task])
        else:
            outs.append(
                bring(staged, ref.o_mixed.at[:, :, :, pl.ds(left, wide)], ref.push.at[n % 2])
            )
            advance(tasks)
    run(tasks)
    link.drain()
    for copy in outs:
        if copy is not None:
            copy.wait()
    grad_out.wait()


def mix_bytes(groups, rows, slots, width):
    total = groups * rows * width * 2
    return 2 * total + 4 * rows * width * 2 * 2 + 2 * groups * max(rows, slots) * 512 * 2 * 2


def mix_stage(calls, groups, parts, picks, produced, back, dweights, lanes, tokens, gradients, shared):
    deep = groups // PAIR
    blocks, slots, rows = picks.shape
    width = tokens.shape[1]
    sub = rows // parts
    bf16, f32 = jnp.bfloat16, jnp.float32
    experts_wide = lanes[1]
    wide = min(512, width)
    chunks = [(left, wide) for left in range(0, width, wide)] + [(width, experts_wide)]
    inputs = Bag(
        i_picks=picks,
        i_produced=produced,
        i_back=back,
        i_dweights=dweights,
        i_lanes=lanes[0],
        i_tokens=tokens,
        i_gradients=gradients,
        i_shared=shared,
    )
    specs = [IN_VMEM if key in ("i_dweights", "i_lanes") else ANY for key in inputs]
    third = shared.shape[0] // 3
    scratch = Bag(
        b_picks=pltpu.VMEM(picks.shape, bf16),
        b_shared=pltpu.VMEM(shared.shape, bf16),
        b_x=pltpu.VMEM((2, rows, width), bf16),
        b_g=pltpu.VMEM((2, rows, width), bf16),
        b_acc=pltpu.VMEM(shared.shape, f32),
        b_grad=pltpu.VMEM(shared.shape, bf16),
        b_hidden=pltpu.VMEM((blocks, rows, third), bf16),
        b_both=pltpu.VMEM((blocks, rows, 2 * third), bf16),
        b_source=pltpu.VMEM((2, blocks, slots, wide), bf16),
        b_stage=pltpu.VMEM((2, blocks * PAIR, PAIR, sub, wide), bf16),
        load=DMA((2,)),
        fetch=DMA((2, 2)),
        pull=DMA((2,)),
        push=DMA((2,)),
        send=DMA((len(chunks), total_hops(deep))),
        arrive=DMA((len(chunks), total_hops(deep))),
    )
    for n, (_, columns) in enumerate(chunks):
        scratch["p%d" % n] = pltpu.VMEM((PAIR, blocks * PAIR, sub, columns), bf16)
        for k, buffer in enumerate(total_buffers(deep, sub, columns)):
            scratch["f%d_%d" % (n, k)] = buffer
    names = list(inputs) + ["o_dsecond", "o_mixed", "o_shared"] + list(scratch)
    return pl.pallas_call(
        functools.partial(mix_kernel, groups, tuple(chunks), tuple(names)),
        in_specs=specs,
        out_specs=[IN_VMEM, ANY, ANY],
        out_shape=[
            jax.ShapeDtypeStruct((sub, width + experts_wide), f32),
            jax.ShapeDtypeStruct((blocks * PAIR, PAIR, sub, width), bf16),
            jax.ShapeDtypeStruct(shared.shape, bf16),
        ],
        scratch_shapes=list(scratch.values()),
        compiler_params=calls.params(),
        name="mix",
    )(*inputs.values())


def advance(tasks, count=1):
    for _ in range(count):
        for task in tasks:
            next(task, None)


def begun(tasks):
    return [task for task in tasks if next(task, run) is not run]


def tensor_total(link, partial, from_beside, give, from_across, result, send, arrive):
    y, c = link.y, link.c

    def beside():
        return pltpu.make_async_remote_copy(
            src_ref=partial.at[:, 1 - c],
            dst_ref=from_beside,
            send_sem=send.at[0],
            recv_sem=arrive.at[0],
            device_id=link.peer("c"),
            device_id_type=MESH,
        )

    def across():
        return pltpu.make_async_remote_copy(
            src_ref=give,
            dst_ref=from_across,
            send_sem=send.at[1],
            recv_sem=arrive.at[1],
            device_id=link.peer("y"),
            device_id_type=MESH,
        )

    link.emit(beside)
    yield
    arrived(from_beside, arrive.at[0])
    give[...] = partial[1 - y, c] + from_beside[1 - y]
    link.emit(across)
    result[...] = partial[y, c].astype(jnp.float32) + from_beside[y].astype(jnp.float32)
    yield
    arrived(from_across, arrive.at[1])
    result[...] = result[...] + from_across[...].astype(jnp.float32)


def expert_total(link, axis, grad, from_twin, from_deep, result, send, arrive):
    deep, z, x = link.deep, link.z, link.x
    size = result.shape[axis]

    def target(k):
        return (z + k) % deep

    def to_twin(k):
        return pltpu.make_async_remote_copy(
            src_ref=slot(grad, axis, target(k) * PAIR + 1 - x, size),
            dst_ref=from_twin.at[k],
            send_sem=send.at[k],
            recv_sem=arrive.at[k],
            device_id=link.peer("x"),
            device_id_type=MESH,
        )

    def to_deep(k):
        return pltpu.make_async_remote_copy(
            src_ref=from_twin.at[k],
            dst_ref=from_deep.at[k - 1],
            send_sem=send.at[deep + k],
            recv_sem=arrive.at[deep + k],
            device_id=link.at_z(target(k)),
            device_id_type=MESH,
        )

    ks = list(range(1, deep)) + [0]
    for k in ks:
        link.emit(functools.partial(to_twin, k))
    for k in ks[:-1]:
        yield
        arrived(from_twin.at[k], arrive.at[k])
        mine = slot(grad, axis, target(k) * PAIR + x, size)
        from_twin[k] = from_twin[k] + mine[...]
        link.emit(functools.partial(to_deep, k))
    yield
    arrived(from_twin.at[0], arrive.at[0])
    total = slot(grad, axis, z * PAIR + x, size)[...].astype(jnp.float32)
    result[...] = total + from_twin[0].astype(jnp.float32)
    for k in range(1, deep):
        yield
        arrived(from_deep.at[k - 1], arrive.at[deep + k])
        result[...] = result[...] + from_deep[k - 1].astype(jnp.float32)


def back_kernel(groups, sizes, reduced, names, *refs):
    ref = Bag(zip(names, refs))
    deep = groups // PAIR
    parts = PAIR * PAIR
    link = Link(deep)
    part = link.part
    bf16, f32 = jnp.bfloat16, jnp.float32
    link.greet(groups, "eyc")
    loading = {}
    for n, name in enumerate(n[2:] for n in names if n[:2] == "h_"):
        loading[name] = bring(ref["h_" + name], ref["l_" + name], ref.load.at[n])
    left = []

    def leave(name, source=None):
        source = ref["b_" + name] if source is None else source
        left.append(bring(source, ref["o_" + name], ref.leave.at[len(left)]))

    def ready(*which):
        for name in which:
            if name in loading:
                loading.pop(name).wait()
        return [ref["l_" + name] for name in which]

    rows_send, rows_arrive = ref.rows_send, ref.rows_arrive
    used = [0]

    def over_tensor(source, target, axis, size):
        row = used[0]
        used[0] += 1

        def home_of(sz, sx, sy, sc):
            return slot(target, axis, sy * PAIR + sc, size)

        n = len(placed)
        placed.append(bring(source, home_of(link.z, link.x, link.y, link.c), ref.place.at[n]))
        return spread(link, "yc", source, home_of, rows_send.at[row], rows_arrive.at[row])

    placed = []
    totals = {name: i for i, (name, _) in enumerate(reduced)}
    axis_of = dict(reduced)

    def over_expert(name):
        if name not in totals:
            leave(name)
            return []
        i = totals[name]
        return begun(
            [
                expert_total(
                    link,
                    axis_of[name],
                    ref["b_" + name],
                    ref["t_" + name],
                    ref["d_" + name],
                    ref["r_" + name],
                    ref.send.at[i],
                    ref.arrive.at[i],
                )
            ]
        )

    shared_tasks = []
    if SHARED in axis_of:
        wide = ref.o_shared.shape[2]
        source = ref.i_shared
        shared_tasks = begun(
            [
                shuffle(
                    link,
                    groups,
                    lambda e: source.at[:, pl.ds(pl.multiple_of(e * wide, LANES), wide)],
                    lambda e: ref.o_shared.at[e],
                    ref.shared_send,
                    ref.shared_arrive,
                )
            ]
        )
        loading[OWN_SHARED] = bring(
            source.at[:, pl.ds(pl.multiple_of(link.me * wide, LANES), wide)],
            ref.k_shared,
            ref.place.at[len(placed)],
        )
        placed.append(None)

    mixed_parts = len([name for name in names if name[:1] == "m" and name[1:].isdigit()])
    mixed_loads = []
    for n in range(mixed_parts):
        wide = ref.i_block.shape[1] // mixed_parts
        mixed_loads.append(
            bring(
                ref.i_partial.at[:, link.c, :, pl.ds(n * wide, wide)],
                ref["m%d" % n],
                ref.mixed_load.at[n],
            )
        )

    sub, width = ref.i_middle.shape
    experts = ref.i_router.shape[0]
    middle = ref.i_middle[...]
    norms = [ref.i_norms[i : i + 1, : size * groups] for i, size in enumerate(sizes)]
    ffn_gain = norms[1]
    inverse = lax.rsqrt(jnp.mean(middle * middle, axis=-1, keepdims=True) + EPSILON)
    normed = middle * inverse
    chosen = ref.i_chosen[:, :experts]
    dweights = ref.i_dsecond[:, width : width + experts]
    total = jnp.sum(chosen, axis=-1, keepdims=True)
    dchosen = (
        ROUTE_SCALE
        / total
        * (dweights - jnp.sum(dweights * chosen, axis=-1, keepdims=True) / total)
    )
    dlogits = (dchosen * chosen * (1.0 - chosen)).astype(bf16)
    dsecond = ref.i_dsecond[:, :width] + matmul(dlogits, ref.i_router[...])
    scaled = dsecond * ffn_gain
    start = pl.multiple_of(part * sub, sub)
    gradient = ref.i_out_grad[pl.ds(start, sub), :].astype(f32)
    middle_grad = gradient + inverse * (
        scaled - normed * jnp.mean(scaled * normed, axis=-1, keepdims=True)
    )
    ref.b_middle_grad[...] = middle_grad
    ref.b_grad_rows[...] = middle_grad.astype(bf16)
    tensor_tasks = begun([over_tensor(ref.b_grad_rows, ref.b_attention_grad, 0, sub)])
    ref.b_router[...] = matmul_tn(dlogits, (normed * ffn_gain).astype(bf16)).astype(bf16)
    expert_tasks = over_expert(ROUTER)
    gain_sums = {1: jnp.sum(dsecond * normed, axis=0, keepdims=True)}

    run(tensor_tasks)
    placed[1 if SHARED in axis_of else 0].wait()
    placed[1 if SHARED in axis_of else 0] = None

    attended, out_proj = ready(ATTENDED, OUT_PROJ)
    attention_grad = ref.b_attention_grad
    for at in range(0, attended.shape[1], 256):
        ref.b_out_proj[at : at + 256, :] = matmul_tn(
            attended[:, at : at + 256], attention_grad[...]
        ).astype(bf16)
    expert_tasks += over_expert(OUT_PROJ)
    mixed_tasks = []
    if I_PARTIAL in ref:
        partial = ref.i_partial
        for load in mixed_loads:
            load.wait()
        for n in range(mixed_parts):
            wide = width // mixed_parts
            span = pl.ds(n * wide, wide)
            mixed_tasks.append(
                device_total(
                    link,
                    1,
                    ref["m%d" % n],
                    partial.at[:, 1 - link.c, :, span],
                    [ref["m%d_%d" % (n, k)] for k in range(4)],
                    ref.b_mixed.at[:, span],
                    ref.mixed_send.at[n],
                    ref.mixed_arrive.at[n],
                )
            )
        mixed_tasks = begun(mixed_tasks)
    ref.b_attended_grad[...] = matmul_nt(attention_grad[...], out_proj[...]).astype(bf16)

    queries, keys, values = ready(QUERIES, KEYS, VALUES)
    heads, row_count, head_width = queries.shape
    cosine, sinusoid = ref.i_cosine[...], ref.i_sinusoid[...]
    dkey_rope = jnp.zeros((row_count, LANES), f32)
    scale = head_width ** (-0.5)
    filler = jnp.zeros((row_count, LANES - ROPE), f32)
    for h in range(heads):
        scores = matmul_nt(queries[h], keys[h]) * scale
        scores = jnp.where(ref.i_allowed[...] > 0, scores, -1e30)
        powers = jnp.exp(scores - jnp.max(scores, axis=-1, keepdims=True))
        probs = powers / jnp.sum(powers, axis=-1, keepdims=True)
        attended_grad = ref.b_attended_grad[:, h * VD : (h + 1) * VD]
        dvalues = matmul_tn(probs.astype(bf16), attended_grad)
        dprobs = matmul_nt(attended_grad, values[h])
        delta = jnp.sum(probs * dprobs, axis=-1, keepdims=True)
        dscores = (probs * (dprobs - delta) * scale).astype(bf16)
        dquery = matmul(dscores, keys[h])
        dkeys = matmul_tn(dscores, queries[h])
        rope = turn(jnp.concatenate([dquery[:, NOPE:], filler], axis=1), cosine, -sinusoid)
        pair = jnp.concatenate(
            [dquery[:, :NOPE], rope, jnp.zeros((row_count, LANES), f32)], axis=1
        )
        if h % 2 == 0:
            held = pair
        else:
            held = held + pltpu.roll(pair, head_width, 1)
            ref.b_dquery[:, (h - 1) * head_width : (h + 1) * head_width] = held.astype(bf16)
        dkey_rope = dkey_rope + jnp.concatenate([dkeys[:, NOPE:], filler], axis=1)
        base = h * (NOPE + VD)
        ref.b_dkeyval[:, base : base + NOPE] = dkeys[:, :NOPE].astype(bf16)
        ref.b_dkeyval[:, base + NOPE : base + NOPE + VD] = dvalues.astype(bf16)
        advance(expert_tasks)
        advance(mixed_tasks[h % max(1, len(mixed_tasks)) :][:1])
    dkey_rope = turn(dkey_rope, cosine, -sinusoid)

    query_n, latent_n, query_up, latent_up = ready(QUERY_N, LATENT_N, QUERY_UP, LATENT_UP)
    query_rank, latent_rank = query_n.shape[1], latent_n.shape[1]
    for at in range(0, query_rank, 256):
        ref.b_query_up[at : at + 256, :] = matmul_tn(
            query_n[:, at : at + 256], ref.b_dquery[...]
        ).astype(bf16)
    expert_tasks += over_expert(QUERY_UP)
    for at in range(0, latent_rank, 256):
        ref.b_latent_up[at : at + 256, :] = matmul_tn(
            latent_n[:, at : at + 256], ref.b_dkeyval[...]
        ).astype(bf16)
    expert_tasks += over_expert(LATENT_UP)
    partial = ref.b_heads_partial
    lead = query_rank + latent_rank
    for quarter in range(parts):
        span = slice(quarter * sub, (quarter + 1) * sub)
        at = (quarter // PAIR, quarter % PAIR)
        partial[(*at, slice(None), slice(0, query_rank))] = matmul_nt(
            ref.b_dquery[span, :], query_up[...]
        ).astype(bf16)
        partial[(*at, slice(None), slice(query_rank, lead))] = matmul_nt(
            ref.b_dkeyval[span, :], latent_up[...]
        ).astype(bf16)
        partial[(*at, slice(None), slice(lead, lead + LANES))] = dkey_rope[span, :].astype(bf16)
    sum_tasks = begun(
        [
            tensor_total(
                link,
                partial,
                ref.b_heads_beside,
                ref.b_heads_give,
                ref.b_heads_across,
                ref.b_heads_rows,
                ref.sum_send.at[0],
                ref.sum_arrive.at[0],
            )
        ]
    )
    advance(expert_tasks)
    advance(mixed_tasks)
    run(sum_tasks)

    heads_rows = ref.b_heads_rows
    (query_lat, latent_t) = ready(QUERY_LAT, LATENT_T)

    def norm_back(values, gain, cotangent):
        inverse = lax.rsqrt(jnp.mean(values * values, axis=-1, keepdims=True) + EPSILON)
        normed = values * inverse
        scaled = cotangent * gain
        back = inverse * (scaled - normed * jnp.mean(scaled * normed, axis=-1, keepdims=True))
        return (back, jnp.sum(cotangent * normed, axis=0, keepdims=True))

    query_rows = query_lat[pl.ds(start, sub), :].astype(f32)
    back, gain_sums[2] = norm_back(query_rows, norms[2], heads_rows[:, :query_rank])
    ref.b_query_rows[...] = back.astype(bf16)
    ref.b_latent_block[...] = latent_t[:latent_rank, :].astype(f32).T
    latent_rows = ref.b_latent_block[pl.ds(start, sub), :]
    back, gain_sums[3] = norm_back(
        latent_rows, norms[3], heads_rows[:, query_rank:lead]
    )
    ref.b_latent_rows[:, :latent_rank] = back.astype(bf16)
    ref.b_latent_rows[:, latent_rank:] = heads_rows[:, lead:].astype(bf16)
    own = len(placed)
    tensor_tasks = begun(
        [
            over_tensor(ref.b_query_rows, ref.b_dquery_lat, 0, sub),
            over_tensor(ref.b_latent_rows, ref.b_dlatent_all, 0, sub),
        ]
    )
    advance(expert_tasks)
    advance(mixed_tasks)
    run(tensor_tasks)
    for n in (own, own + 1):
        placed[n].wait()
        placed[n] = None

    first, query_down, latent_down = ready(FIRST, QUERY_DOWN, LATENT_DOWN)
    query_cut, latent_cut = query_down.shape[1], latent_down.shape[0]
    dquery_lat = ref.b_dquery_lat[
        :, pl.ds(pl.multiple_of(part * query_cut, LANES), query_cut)
    ]
    ref.b_dlatent_t[...] = ref.b_dlatent_all[...].astype(f32).T
    dlatent_t = ref.b_dlatent_t[
        pl.ds(pl.multiple_of(part * latent_cut, 8), latent_cut), :
    ].astype(bf16)
    for at in range(0, width, 256):
        ref.b_query_down[at : at + 256, :] = matmul_tn(
            first[:, at : at + 256], dquery_lat
        ).astype(bf16)
    expert_tasks += over_expert(QUERY_DOWN)
    for at in range(0, width, 512):
        ref.b_latent_down[:, at : at + 512] = matmul(dlatent_t, first[:, at : at + 512]).astype(
            bf16
        )
    expert_tasks += over_expert(LATENT_DOWN)
    advance(expert_tasks)
    partial = ref.b_first_partial
    for quarter in range(parts):
        span = slice(quarter * sub, (quarter + 1) * sub)
        partial[quarter // PAIR, quarter % PAIR] = (
            matmul_nt(dquery_lat[span], query_down[...])
            + matmul_tn(dlatent_t[:, span], latent_down[...])
        ).astype(bf16)
    sum_tasks = begun(
        [
            tensor_total(
                link,
                partial,
                ref.b_first_beside,
                ref.b_first_give,
                ref.b_first_across,
                ref.b_first_rows,
                ref.sum_send.at[1],
                ref.sum_arrive.at[1],
            )
        ]
    )
    advance(expert_tasks)
    run(sum_tasks)
    residual = ref.i_block[pl.ds(start, sub), :].astype(f32)
    back, gain_sums[0] = norm_back(
        residual, norms[0], ref.b_first_rows[...]
    )
    ref.b_input_rows[...] = (ref.b_middle_grad[...] + back).astype(bf16)
    input_tasks = begun([over_tensor(ref.b_input_rows, ref.o_input_grad, 0, sub)])
    wide = ref.b_gains.shape[1]
    for i, size in enumerate(sizes):
        sums = jnp.broadcast_to(gain_sums[i], (8, gain_sums[i].shape[1]))
        span = sums.shape[1]
        if span < wide:
            sums = jnp.concatenate([sums, jnp.zeros((8, wide - span), f32)], axis=1)
            span = wide
        for e in range(groups):
            moved = pltpu.roll(sums, span - e * size, 1) if e else sums
            ref.b_gains[e * 8 + i : e * 8 + i + 1, :] = moved[:1, :wide]
    for e in range(groups):
        ref.b_gains[e * 8 + len(sizes) : e * 8 + 8, :] = jnp.zeros((8 - len(sizes), wide), f32)
    expert_tasks += over_expert(GAINS)
    advance(expert_tasks)
    run(mixed_tasks)
    mixed = ref.b_mixed if I_PARTIAL in ref else ref.i_mixed
    ref.b_block_rows[...] = (middle + mixed[...]).astype(bf16)
    block_tasks = begun([over_tensor(ref.b_block_rows, ref.o_block_out, 0, sub)])
    run(expert_tasks)

    finished = ("o_query_down", "o_latent_down")
    finals = []
    for name, axis in ((QUERY_DOWN, 1), (LATENT_DOWN, 0), (ROUTER, 0), (GAINS, 0)):
        if name not in totals:
            continue
        share = ref["s_" + name]
        whole = ref["o_" + name] if "o_" + name in finished else ref["g_" + name]
        share[...] = ref["r_" + name][...].astype(share.dtype)
        finals.append(over_tensor(share, whole, axis, share.shape[axis]))
    finals = begun(finals)
    for name in (OUT_PROJ, QUERY_UP, LATENT_UP):
        if name in totals:
            leave(name, ref["r_" + name])
    if SHARED in axis_of:
        loading.pop(OWN_SHARED).wait()
        left.append(
            bring(ref.k_shared, ref.o_shared.at[link.me], ref.leave.at[len(left)])
        )
    run(finals)
    for move in placed:
        if move is not None:
            move.wait()
    for name in (ROUTER, GAINS):
        if name in totals:
            size = ref["s_" + name].shape[0]
            total = ref["g_" + name][:size, :]
            for t in range(1, parts):
                total = total + ref["g_" + name][t * size : (t + 1) * size, :]
            ref["f_" + name][...] = total
            leave(name, ref["f_" + name])
    run(block_tasks + input_tasks + shared_tasks)
    link.drain()
    for move in left:
        move.wait()


def back_stage(calls, groups, parts, sizes, held, small, grad_shared, partial):
    deep = groups // PAIR
    bf16, f32 = jnp.bfloat16, jnp.float32
    rows, width = small.block.shape
    sub = rows // parts
    query_rank, latent_rank = held.query_n.shape[1], held.latent_n.shape[1]
    heads, _, head_width = held.queries.shape
    query_cut, latent_cut = held.query_down.shape[1], held.latent_down.shape[0]
    experts = small.router.shape[0]
    gain_wide = -(-max(sizes) // LANES) * LANES
    lead = query_rank + latent_rank + LANES
    half = parts // PAIR
    full = Bag(
        out_proj=(held.out_proj.shape, 1, bf16),
        query_up=(held.query_up.shape, 0, bf16),
        latent_up=(held.latent_up.shape, 0, bf16),
        query_down=((width, query_cut), 0, bf16),
        latent_down=((latent_cut, width), 1, bf16),
        router=((experts, width), 1, bf16),
        gains=((groups * 8, gain_wide), 0, f32),
    )
    reduced, pieces = [], {}
    for name, (shape, axis, dtype) in full.items():
        piece = list(shape)
        piece[axis] //= groups
        if aligned(piece[axis], 1) or axis == 0:
            reduced.append((name, axis))
            pieces[name] = tuple(piece)
    buffers = Bag(
        middle_grad=((sub, width), f32),
        grad_rows=((sub, width), bf16),
        block_rows=((sub, width), bf16),
        attention_grad=((rows, width), bf16),
        attended_grad=(held.attended.shape, bf16),
        dquery=((rows, heads * head_width), bf16),
        dkeyval=((rows, heads * (NOPE + VD)), bf16),
        heads_partial=((half, PAIR, sub, lead), bf16),
        heads_beside=((half, sub, lead), bf16),
        heads_give=((sub, lead), bf16),
        heads_across=((sub, lead), bf16),
        heads_rows=((sub, lead), f32),
        query_rows=((sub, query_rank), bf16),
        latent_rows=((sub, latent_rank + LANES), bf16),
        latent_block=((rows, latent_rank), f32),
        dquery_lat=((rows, query_rank), bf16),
        dlatent_all=((rows, latent_rank + LANES), bf16),
        dlatent_t=((latent_rank + LANES, rows), f32),
        first_partial=((half, PAIR, sub, width), bf16),
        first_beside=((half, sub, width), bf16),
        first_give=((sub, width), bf16),
        first_across=((sub, width), bf16),
        first_rows=((sub, width), f32),
        input_rows=((sub, width), bf16),
    )
    for name, (shape, _, dtype) in full.items():
        buffers[name] = (shape, dtype)
    scratch = Bag(("b_" + name, pltpu.VMEM(*spec)) for name, spec in buffers.items())
    for name, array in held.items():
        scratch["l_" + name] = pltpu.VMEM(array.shape, array.dtype)
    outs = Bag(block_out=((rows, width), bf16), input_grad=((rows, width), bf16))
    for name, (shape, axis, dtype) in full.items():
        if name not in pieces:
            outs[name] = (shape, dtype)
            continue
        piece = pieces[name]
        scratch["t_" + name] = pltpu.VMEM((deep, *piece), dtype)
        scratch["d_" + name] = pltpu.VMEM((deep - 1, *piece), dtype)
        scratch["r_" + name] = pltpu.VMEM(piece, f32)
        outs[name] = (piece, f32)
        if name in (QUERY_DOWN, LATENT_DOWN, ROUTER, GAINS):
            kind = bf16 if name in (QUERY_DOWN, LATENT_DOWN) else f32
            along = 1 if name == QUERY_DOWN else 0
            whole = list(piece)
            whole[along] *= parts
            scratch["s_" + name] = pltpu.VMEM(piece, kind)
            if name in (QUERY_DOWN, LATENT_DOWN):
                outs[name] = (tuple(whole), bf16)
            else:
                scratch["g_" + name] = pltpu.VMEM(tuple(whole), kind)
                scratch["f_" + name] = pltpu.VMEM(piece, f32)
    share = grad_shared.shape[1] // groups
    inputs = {"i_" + name: array for name, array in small.items()}
    specs = [IN_VMEM] * len(small)
    if aligned(share, 1):
        reduced.append((SHARED, 1))
        inputs["i_shared"] = grad_shared
        specs.append(ANY)
        outs.shared = ((groups, grad_shared.shape[0], share), bf16)
        scratch.k_shared = pltpu.VMEM((grad_shared.shape[0], share), bf16)
        scratch.shared_send = scratch.shared_arrive = DMA((groups,))
    inputs |= {"h_" + name: array for name, array in held.items()}
    specs += [ANY] * len(held)
    if partial is not None:
        inputs[I_PARTIAL] = partial
        specs.append(ANY)
        mixed_parts = max(1, width // 512)
        wide = width // mixed_parts
        for n in range(mixed_parts):
            scratch["m%d" % n] = pltpu.VMEM((groups * half, sub, wide), bf16)
            for k, buffer in enumerate(total_buffers(deep, sub, wide)):
                scratch["m%d_%d" % (n, k)] = buffer
        scratch.b_mixed = pltpu.VMEM((sub, width), f32)
        scratch.mixed_load = DMA((mixed_parts,))
        scratch.mixed_send = scratch.mixed_arrive = DMA((mixed_parts, total_hops(deep)))
    scratch.load = DMA((len(held),))
    scratch.leave = DMA((len(outs) + 1,))
    scratch.place = DMA((12,))
    scratch.rows_send = scratch.rows_arrive = DMA((12, 8))
    scratch.send = scratch.arrive = DMA((len(full), 2 * deep))
    scratch.sum_send = scratch.sum_arrive = DMA((2, 2))
    names = list(inputs) + ["o_" + name for name in outs] + list(scratch)
    reduced = [entry for entry in reduced]
    results = pl.pallas_call(
        functools.partial(back_kernel, groups, tuple(sizes), tuple(reduced), tuple(names)),
        in_specs=specs,
        out_specs=[ANY] * len(outs),
        out_shape=[jax.ShapeDtypeStruct(*spec) for spec in outs.values()],
        scratch_shapes=list(scratch.values()),
        compiler_params=calls.params(),
        name="back",
    )(*inputs.values())
    results = Bag(zip(outs, results))
    for name, (shape, axis, dtype) in full.items():
        if name not in pieces:
            results[name] = scatter_sum(results[name], EXPERT, axis)
            if name == LATENT_DOWN:
                results[name] = gather(results[name].astype(bf16), TENSOR, 0).astype(f32)
            if name == ROUTER:
                results[name] = lax.psum(results[name].astype(bf16), TENSOR).astype(f32)
    if SHARED not in results:
        split = grad_shared.reshape(grad_shared.shape[0], groups, share).transpose(1, 0, 2)
        results.shared = lax.all_to_all(
            split, EXPERT, split_axis=0, concat_axis=0, tiled=True
        )
    return results


ALL = (EXPERT, TENSOR)


def gather(values, axes, dimension):
    return lax.all_gather(values, axes, axis=dimension, tiled=True)


def scatter_sum(values, axes, dimension):
    return lax.psum_scatter(
        values.astype(jnp.bfloat16), axes, scatter_dimension=dimension, tiled=True
    ).astype(jnp.float32)


def aligned(size, axis):
    return size % LANES == 0 if axis else size % 16 == 0


def ready_items(items, part):
    result = []
    for name, array, axis, cut, over, orders, home in items:
        if axis == 1 and array.shape[-1] % LANES:
            if over == SHUFFLE:
                array = lax.all_to_all(array, EXPERT, split_axis=0, concat_axis=0, tiled=True)
                array = array.transpose(1, 0, 2).reshape(array.shape[1], -1)
            else:
                if cut is not None:
                    array = lax.dynamic_slice_in_dim(array, part * cut[1], cut[1], axis=cut[0])
                array = gather(array, EXPERT, axis)
            cut, over, orders, home = None, READY, (), VMEM_
        result.append((name, array, axis, cut, over, orders, home))
    return result


def body(
    calls,
    block_in,
    attention_gain,
    query_down,
    query_gain,
    query_up,
    latent_down,
    latent_gain,
    latent_up,
    out_proj,
    ffn_gain,
    router,
    shared_gate,
    shared_up,
    shared_down,
    expert_gate,
    expert_up,
    expert_down,
    doc_lengths,
    routes,
    out_grad,
):
    groups = lax.axis_size(EXPERT)
    parts = lax.axis_size(TENSOR)
    me = lax.axis_index(EXPERT)
    part = lax.axis_index(TENSOR)
    row_count, width = block_in.shape
    top = routes.shape[1]
    local = expert_gate.shape[0]
    experts = local * groups

    all_gains = (attention_gain, ffn_gain, query_gain, latent_gain)
    gain_sizes = [g.shape[0] for g in all_gains]
    gain_wide = -(-max(gain_sizes) // LANES) * LANES
    gains = jnp.stack(
        [jnp.pad(g.astype(jnp.float32), (0, gain_wide - g.shape[0])) for g in all_gains]
    )
    gains = jnp.pad(gains, ((0, 8 - len(all_gains)), (0, 0)))
    routes_pad = jnp.pad(routes.T, ((0, -top % 8), (0, 0)), constant_values=-1)
    shared = jnp.stack([shared_gate.T, shared_up.T, shared_down])
    shared_units = shared.shape[1] // groups
    shared = shared.reshape(3, groups, shared_units, -1).transpose(1, 0, 2, 3)
    shared = shared.reshape(groups, 3 * shared_units, -1)
    query_cut = query_down.shape[1] // parts
    latent_cut = latent_down.shape[1] // parts
    allowed, cosine, sinusoid = layout(doc_lengths[0], row_count)
    allowed = allowed.astype(jnp.float32)
    tables = [
        jnp.pad(jnp.concatenate(pair, axis=1), ((0, 0), (0, LANES - ROPE)))
        for pair in ((cosine, cosine), (-sinusoid, sinusoid))
    ]
    items = [
        (GAINS, gains, 0, None, EXPERT, ("zx",), VMEM_),
        (QUERY_DOWN, query_down, 0, (1, query_cut), EXPERT, ("zx",), VMEM_),
        (LATENT_DOWN, latent_down.T, 1, (0, latent_cut), EXPERT, ("zx",), VMEM_),
        (QUERY_UP, query_up, 0, None, EXPERT, ("zx",), VMEM_),
        (LATENT_UP, latent_up, 0, None, EXPERT, ("zx",), VMEM_),
        (OUT_PROJ, out_proj, 1, None, EXPERT, ("zx",), VMEM_),
        (ROUTER, router.T, 1, None, EXPERT, ("zx",), VMEM_),
        (ROUTES, routes_pad, 1, None, EXPERT, ("zx",), "hbm"),
        (SHARED, shared, 1, None, SHUFFLE, (), "hbm"),
        (OUT_GRAD, out_grad, 0, (0, row_count // parts), "all", (ZXYC, "xzyc"), "hbm"),
    ]
    front = front_stage(
        calls,
        groups,
        parts,
        gain_sizes,
        ready_items(items, part),
        block_in,
        routes,
        allowed,
        *tables,
    )
    router_t = front.router
    shared = front.shared
    tokens, gradients = front.tokens, front.out_grad
    lane_pad = -experts % LANES
    own_ids = me * local + jnp.arange(local, dtype=jnp.int32)
    expert_rows, expert_grads, picks, slot_weights = route_stage(
        groups, own_ids, front.routes, tokens, gradients, front.weights
    )
    slot_shape = (groups, local, CAP)
    produced, back_rows, slot_dweights, grad_gate, grad_up, grad_down = expert_stage(
        expert_rows.reshape(*slot_shape, width),
        expert_grads.reshape(*slot_shape, width),
        slot_weights.reshape(*slot_shape, 1),
        expert_gate.transpose(0, 2, 1),
        expert_up.transpose(0, 2, 1),
        expert_down,
    )
    slots = local * CAP
    produced = produced.reshape(groups, slots, width)
    back_rows = back_rows.reshape(groups, slots, width)
    slot_dweights = slot_dweights.reshape(groups, slots, 1)
    slot_lanes = jnp.repeat(own_ids, CAP)[:, None]
    if mix_bytes(groups, row_count, slots, width) < 40 * 2**20:
        mixed = None
        dsecond, partial, grad_shared = mix_stage(
            calls,
            groups,
            parts,
            picks,
            produced,
            back_rows,
            slot_dweights,
            (slot_lanes, experts + lane_pad),
            tokens,
            gradients,
            shared,
        )
    else:
        partial = None
        lane_ids = jnp.arange(experts + lane_pad, dtype=jnp.int32)
        spread_out = jnp.where(slot_lanes == lane_ids[None, :], slot_dweights, 0.0)
        mixed_part, dsecond_part, grad_shared = combine_stage(
            picks,
            produced,
            back_rows,
            spread_out.astype(jnp.bfloat16),
            tokens.reshape(groups, row_count, width),
            gradients.reshape(groups, row_count, width),
            shared.reshape(3, shared_units, width),
        )
        grad_shared = grad_shared.astype(jnp.bfloat16).reshape(3 * shared_units, width)
        dsecond, mixed = sum_all(
            calls,
            groups,
            parts,
            (
                dsecond_part.reshape(-1, width + experts + lane_pad),
                mixed_part.reshape(-1, width),
            ),
        )
    held = Bag(
        (name, front[name])
        for name in (
            ATTENDED,
            OUT_PROJ,
            QUERIES,
            KEYS,
            VALUES,
            QUERY_N,
            LATENT_N,
            QUERY_UP,
            LATENT_UP,
            QUERY_LAT,
            LATENT_T,
            FIRST,
            QUERY_DOWN,
            LATENT_DOWN,
        )
    )
    small = Bag(
        dsecond=dsecond,
        middle=front.middle,
        chosen=front.chosen,
        router=router_t,
        out_grad=out_grad,
        block=block_in,
        allowed=allowed,
        cosine=tables[0],
        sinusoid=tables[1],
        norms=front.norms,
    )
    if partial is None:
        small.mixed = mixed
    back = back_stage(calls, groups, parts, gain_sizes, held, small, grad_shared, partial)
    grad_shared = back.shared.reshape(groups, 3, shared_units, -1).transpose(1, 0, 2, 3)
    grad_shared = grad_shared.astype(jnp.float32).reshape(3, groups * shared_units, -1)
    grad_gains = [back.gains[i, :size] for i, size in enumerate(gain_sizes)]

    return (
        back.block_out,
        back.input_grad,
        grad_gains[0],
        back.query_down.astype(jnp.float32),
        grad_gains[2],
        back.query_up,
        back.latent_down.T.astype(jnp.float32),
        grad_gains[3],
        back.latent_up,
        back.out_proj,
        grad_gains[1],
        back.router.T,
        grad_shared[0].T,
        grad_shared[1].T,
        grad_shared[2],
        grad_gate.transpose(0, 2, 1),
        grad_up.transpose(0, 2, 1),
        grad_down,
    )


def solution(mesh):
    placed = (
        P(EXPERT, None),
        P(EXPERT),
        P(EXPERT, None),
        P(EXPERT),
        P(EXPERT, TENSOR),
        P(EXPERT, None),
        P(EXPERT),
        P(EXPERT, TENSOR),
        P(TENSOR, EXPERT),
        P(EXPERT),
        P(EXPERT, None),
        P(EXPERT, TENSOR),
        P(EXPERT, TENSOR),
        P(TENSOR, EXPERT),
        P(EXPERT, None, TENSOR),
        P(EXPERT, None, TENSOR),
        P(EXPERT, TENSOR, None),
        P(EXPERT, None),
        P(EXPERT, None),
        P(EXPERT, None),
    )
    return jax.shard_map(
        functools.partial(body, Calls()),
        mesh=mesh,
        in_specs=placed,
        out_specs=(
            P(EXPERT, None),
            P(EXPERT, None),
            P(EXPERT),
            P(EXPERT, None),
            P(EXPERT),
            P(EXPERT, TENSOR),
            P(EXPERT, None),
            P(EXPERT),
            P(EXPERT, TENSOR),
            P(TENSOR, EXPERT),
            P(EXPERT),
            P(EXPERT, None),
            P(EXPERT, TENSOR),
            P(EXPERT, TENSOR),
            P(TENSOR, EXPERT),
            P(EXPERT, None, TENSOR),
            P(EXPERT, None, TENSOR),
            P(EXPERT, TENSOR, None),
        ),
        check_vma=False,
    )
```

time: 799 us -> 592 us (0.74)
  matrix products: 65.3 us -> 0 us
  Pallas kernels: 609 us -> 555 us
  other arithmetic: 42.5 us -> 9.54 us
  starting transfers between devices: 20.8 us -> 0 us
  local copies, waits for them, and re-layouts: 35.9 us -> 16.1 us
  between operations: 15.8 us -> 1.21 us
    dot_general x27 -> x0, matrix products: 65.3 us -> none  [the longest x9 30.7 us: contract(): return jnp.einsum(form, left, right, preferred_element_type=jnp.float32)]
    pallas_call x11 -> x4, Pallas kernels: 555 us -> 501 us  [the longest x1 203 us: front_stage(): pl.pallas_call(functools.partial(front_kernel, groups, tuple(sizes), tupl...]
    all_to_all x4 -> x0, starting transfers between devices: 20.8 us -> none  [the longest x1 7.41 us: body(): lax.all_to_all(shared, 'expert', split_axis=0, concat_axis=0, tiled=True)]
    convert_element_type x13 -> x4, other arithmetic: 18.5 us -> 4.28 us  [the longest x1 2.46 us: body(): back.query_down.astype(jnp.float32)]
    reduce_sum x12 -> x0, other arithmetic: 9.13 us -> none  [the longest x3 3.96 us: gain_gradient(): return jnp.sum(cotangent * (values * inverse), axis=0)]
  transfers between devices with their start and end apart: 5 -> 0, of which waited for: 1 -> 0; matrix products, arithmetic and copies ran while one was open for 9% -> 0% of each run, Pallas kernels for 48% -> 0%
where the time goes in v2:
time: 592 us; the launch traced here: 582 us
  Pallas kernels  555 us (94%)
  local copies, waits for them, and re-layouts  16.1 us (3%)
  other arithmetic  9.54 us (2%)
    pallas_call x1, Pallas kernels, front_stage(): pl.pallas_call(functools.partial(front_kernel, groups, tuple(sizes), tupl...  203 us
    pallas_call x1, Pallas kernels, back_stage(): pl.pallas_call(functools.partial(back_kernel, groups, tuple(sizes), tuple...  175 us
    pallas_call x1, Pallas kernels, mix_stage(): pl.pallas_call(functools.partial(mix_kernel, groups, tuple(chunks), tuple...  106 us
    pallas_call x1, Pallas kernels, expert_stage(): pl.pallas_call(expert_kernel, grid=(local, blocks // step), in_specs=[row...  54.1 us
    pallas_call x1, Pallas kernels, route_stage(): pl.pallas_call(route_kernel, grid=(groups,), in_specs=[pl.BlockSpec((loca...  17 us

profile of v2, /device:TPU:0, one launch (start us, length us, event | category | flops | bytes accessed | tf_op | source)
XLA Modules:
  0.0 581.9 jit_solution(6421780800355381075)
XLA Ops:
  0.7 0.0 copy-start.8
  0.7 0.0 copy-start.9
  0.7 0.6 iota_add_fusion.ids_ref
  1.3 0.7 pad.28
  1.9 0.7 pad.27
  2.6 0.7 stack.33
  3.3 0.7 stack.32
  3.9 0.6 fusion.10.refs_0_
  4.5 1.3 pad.31.refs_7_
  5.8 2.3 pad_maximum_fusion
  8.1 0.0 copy-done.8
  8.1 0.8 copy.56.refs_11_
  8.9 0.0 copy-done.9
  8.9 0.2 reduce-window.4
  9.1 0.1 convert_reduce_fusion
  9.2 0.8 fusion.1.refs_12_.refs_6_
  10.0 0.1 select_reduce_fusion
  10.1 0.5 fusion.2
  10.7 0.8 select_maximum_fusion
  11.5 202.9 %front.1 = (f32[64,256]{1,0:T(8,128)}, bf16[2048,384]{1,0:T(8,128)(2,1)}, bf16[144,2048]{1,0:T(8,128)(2,1)}, bf16[1536,768]{1,0:T(8,128)(2,1)}, bf16[512,1024]{1...) custom-call(f32[8,256]{1,0:T(8,128)} %fusion.10.refs_0_, ...), custom_call_target="tpu_custom_call" | custom-call | tf_op jit(solution)/shard_map/front/pallas_call | solution.py:1076
  214.5 17.0 %route.1 = (bf16[8,256,2048]{2,1,0:T(8,128)(2,1)}, bf16[8,256,2048]{2,1,0:T(8,128)(2,1)}, bf16[8,256,256]{2,1,0:T(8,128)(2,1)}, f32[8,256,1]{2,1,0:T(8,128)}) custom-call(s32[8,1]{1,0:T(8,128)} %iota_add_fusion.ids_ref, s32[8,2048]{1,0:T(8,128)} %get-tuple-element.64.routes_ref, bf16[2048,2048]{1,0:T(8,128)(2,1)} %get-tuple-element.65.x_ref.refs_5_, ...), custom_call_target="tpu_custom_call" | custom-call | tf_op jit(solution)/shard_map/route/pallas_call | solution.py:1216
  231.5 54.1 %experts.1 = (bf16[8,8,32,2048]{3,2,1,0:T(8,128)(2,1)}, bf16[8,8,32,2048]{3,2,1,0:T(8,128)(2,1)}, f32[8,8,32,1]{3,2,1,0:T(8,128)}, f32[8,352,2048]{2,1,0:T(8,128...) custom-call(bf16[8,8,32,2048]{3,2,1,0:T(8,128)(2,1)} %bitcast.76, bf16[8,8,32,2048]{3,2,1,0:T(8,128)(2,1)} %bitcast.77, ...), custom_call_target="tpu_custom_call" | custom-call | flops 26575110144 | bytes 137363456 | tf_op jit(solution)/shard_map/experts/pallas_call | solution.py:146
  285.6 0.1 broadcast_in_dim.19
  285.7 0.8 broadcast_in_dim_reshape.4.refs_4_
  286.4 105.8 %mix.1 = (f32[64,2176]{1,0:T(8,128)}, bf16[16,2,64,2048]{3,2,1,0:T(8,128)(2,1)}, bf16[264,2048]{1,0:T(8,128)(2,1)}) custom-call(bf16[8,256,256]{2,1,0:T(8,128)(2,1)} %get-tuple-element.68.refs_0_, bf16[8,256,2048]{2,1,0:T(8,128)(2,1)} %bitcast.56, bf16[8,256,2048]{2,1,0:T(8,128)(2,1)} %bitcast.57, f32[8,256,1]{2,1,0:T(8,128)} %bitcast.60, ...), custom_call_target="tpu_custom_call" | custom-call | tf_op jit(solution)/shard_map/mix/pallas_call | solution.py:1426
  392.2 175.1 %back.1 = (bf16[256,2048]{1,0:T(8,128)(2,1)}, bf16[256,2048]{1,0:T(8,128)(2,1)}, f32[512,256]{1,0:T(8,128)}, f32[192,768]{1,0:T(8,128)}, f32[64,1024]{1,0:T(8,12...) custom-call(f32[64,2176]{1,0:T(8,128)} %get-tuple-element.76.refs_0_, ...), custom_call_target="tpu_custom_call" | custom-call | tf_op jit(solution)/shard_map/back/pallas_call | solution.py:2019
  567.4 0.0 copy-start.5
  567.4 0.0 copy-start
  567.4 1.4 fusion.13
  568.8 2.5 convert_element_type.47
  571.3 1.3 slice.25
  572.5 0.0 copy-done.5
  572.5 0.9 convert_bitcast_fusion.1
  573.4 1.2 slice_bitcast_fusion
  574.6 0.0 copy-done
  574.6 0.2 convert_bitcast_fusion
  574.7 0.0 copy-start.2
  574.7 0.0 copy-start.1
  574.8 1.4 fusion.12
  576.1 0.0 copy-start.3
  576.1 0.4 copy-done.2
  576.5 0.0 copy-start.6
  576.5 1.0 copy.64
  577.5 0.0 copy-done.1
  577.5 0.0 copy-start.4
  577.5 0.0 copy-start.7
  577.5 1.0 copy.65
  578.5 0.0 copy-done.3
  578.5 0.8 copy.66
  579.3 0.0 copy-done.6
  579.3 0.7 copy.67
  580.0 0.0 copy-done.4
  580.0 0.8 copy.68
  580.8 0.0 copy-done.7
  580.8 0.6 copy.69
  (6 shorter events, 0.0 us)
Async XLA Ops:
  0.7 7.5 %copy-start.8 = (s32[256,6]{0,1:T(8,128)S(1)}, s32[256,6]{0,1:T(8,128)}, u32[]{:S(2)}) copy-start(s32[256,6]{0,1:T(8,128)} %param.38) | copy-start | bytes 18436
  0.7 8.3 %copy-start.9 = (s32[1,3]{1,0:T(1,128)S(1)}, s32[1,3]{1,0:T(1,128)}, u32[]{:S(2)}) copy-start(s32[1,3]{1,0:T(1,128)} %param.37) | copy-start | bytes 40
  567.4 5.1 copy-start.5
  567.4 7.2 %copy-start = (bf16[8,264,256]{2,1,0:T(8,128)(2,1)S(1)}, bf16[8,264,256]{2,1,0:T(8,128)(2,1)}, u32[]{:S(2)}) copy-start(bf16[8,264,256]{2,1,0:T(8,128)(2,1)} %get-tuple-element.106) | copy-start | bytes 3244036
  574.7 1.8 copy-start.2
  574.7 2.8 copy-start.1
  576.1 2.3 copy-start.3
  576.5 2.8 copy-start.6
  577.5 2.5 copy-start.4
  577.5 3.3 copy-start.7

commit v3 on v2

--- a/solution.py
+++ b/solution.py
@@ -23,7 +23,6 @@
 EXPERT = "expert"
 FIRST = "first"
 GAINS = "gains"
-I_PARTIAL = "i_partial"
 KEYS = "keys"
 LATENT_DOWN = "latent_down"
 LATENT_N = "latent_n"
@@ -733,7 +732,20 @@
             loads[name] = bring(source, mine, own.at[n])
         else:
             loads[name] = bring(source, ref["k_" + name], own.at[n])
-        return [stream for stream in streams_of(source, home_of, orders)]
+        if orders == ("e",):
+            row = stream_row[0]
+            stream_row[0] += 1
+            return [
+                shuffle(
+                    link,
+                    groups,
+                    lambda e: source,
+                    lambda e: slot(target, axis, e, size),
+                    send.at[row],
+                    arrive.at[row],
+                )
+            ]
+        return streams_of(source, home_of, orders)
 
     def streams_of(source, home_of, orders):
         result = []
@@ -757,7 +769,7 @@
         found = [task for name in which for task in tasks_of(name)]
         return [task for task in found if next(task, run) is not run]
 
-    gain_tasks = begin(GAINS)
+    gain_tasks = begin(GAINS, ROUTES)
     stem_tasks = begin(QUERY_DOWN, LATENT_DOWN)
     late_tasks = begin(OUT_GRAD)
 
@@ -791,6 +803,7 @@
     sub = row_count // (PAIR * PAIR)
 
     complete(GAINS)
+    complete(ROUTES)
     run(gain_tasks)
     gains = landing.gains
     attention_gain = full_gain(gains, 0, sizes[0], groups)
@@ -847,8 +860,7 @@
     for _ in range(deep - 2):
         advance(up_tasks, 1)
         advance(late_tasks, 2)
-    out_tasks = begin(OUT_PROJ, ROUTER, ROUTES)
-    shared_tasks = begin(SHARED)
+    out_tasks = begin(OUT_PROJ, ROUTER)
     latent_rank = latent_n.shape[1]
     latent = latent_t[:latent_rank, :].astype(jnp.float32).T
     inverse = lax.rsqrt(jnp.mean(latent * latent, axis=-1, keepdims=True) + EPSILON)
@@ -893,7 +905,8 @@
             advance(out_tasks, 1)
         advance(late_tasks, 2)
     advance(out_tasks, max(0, deep - 1 - heads))
-    for name in (OUT_PROJ, ROUTER, ROUTES):
+    shared_tasks = begin(SHARED)
+    for name in (OUT_PROJ, ROUTER):
         complete(name)
     run(out_tasks)
     for name in (QUERY_DOWN, LATENT_DOWN, QUERY_UP, LATENT_UP, OUT_PROJ, GAINS, ROUTER):
@@ -1240,6 +1253,9 @@
     )(own_ids[:, None], routes_t, tokens, gradients, weights)
 
 
+MIX_LAGS = (1, 3, 5, 7)
+
+
 def mix_kernel(groups, chunks, names, *refs):
     ref = Bag(zip(names, refs))
     deep = groups // PAIR
@@ -1300,16 +1316,30 @@
         both = jnp.concatenate([gate_grad, up_grad], axis=1)
         ref.b_hidden[b] = hidden
         ref.b_both[b] = both
-        ref.b_acc[: 2 * units, :] += matmul_tn(both, row_inputs)
-        ref.b_acc[2 * units :, :] += matmul_tn(hidden, cotangent)
         return carry
+
+    def shared_gradients(b):
+        at = b % 2
+        if b + 1 < blocks:
+            for copy in fetch(b + 1, 1 - at):
+                copy.start()
+        for copy in fetch(b, at):
+            copy.wait()
+        ref.b_acc[: 2 * units, :] += matmul_tn(ref.b_both[b], ref.b_x[at])
+        ref.b_acc[2 * units :, :] += matmul_tn(ref.b_hidden[b], ref.b_g[at])
 
     source_of(order[1]).start()
     lax.fori_loop(0, blocks, block, 0)
-    ref.b_grad[...] = ref.b_acc[...].astype(bf16)
-    grad_out = bring(ref.b_grad, ref.o_shared, ref.load.at[0])
+    for copy in fetch(0, 0):
+        copy.start()
     dw_lane = lax.broadcasted_iota(jnp.int32, (slots, chunks[-1][1]), 1)
-    tasks, outs = [], []
+    tasks = []
+
+    def step_at(moment):
+        for lag in MIX_LAGS:
+            if 0 <= moment - lag < len(tasks):
+                next(tasks[moment - lag], None)
+
     pending = [n for n in order if has_source[n]]
     for n in order:
         back, left, wide = work[n]
@@ -1318,12 +1348,8 @@
             if pending:
                 source_of(pending[0]).start()
             source_of(n).wait()
-        staged = None if back else ref.b_stage.at[n % 2]
-        if not back and len(outs) >= 2:
-            outs[-2].wait()
-            outs[-2] = None
-
-        def one(b, carry, n=n, back=back, left=left, wide=wide, staged=staged):
+
+        def one(b, carry, n=n, back=back, left=left, wide=wide):
             picks = ref.b_picks[b]
             if not has_source[n]:
                 values = matmul_tn(
@@ -1341,36 +1367,32 @@
                 for c in range(PAIR):
                     q = y * PAIR + c
                     piece = values[q * sub : (q + 1) * sub, :]
-                    if back:
-                        ref["p%d" % n][c, b * PAIR + y] = piece
-                    else:
-                        staged[b * PAIR + y, c] = piece
+                    ref["p%d" % n][c, b * PAIR + y] = piece
             return carry
 
         lax.fori_loop(0, blocks, one, 0)
-        if back:
-            task = device_total(
-                link,
-                n % 2,
-                ref["p%d" % n].at[link.c],
-                ref["p%d" % n].at[1 - link.c],
-                [ref["f%d_%d" % (n, k)] for k in range(4)],
-                ref.o_dsecond.at[:, pl.ds(left, wide)],
-                ref.send.at[n],
-                ref.arrive.at[n],
-            )
-            advance(tasks)
-            tasks += begun([task])
-        else:
-            outs.append(
-                bring(staged, ref.o_mixed.at[:, :, :, pl.ds(left, wide)], ref.push.at[n % 2])
-            )
-            advance(tasks)
-    run(tasks)
+        result = ref.o_dsecond if back else ref.o_mixed
+        task = device_total(
+            link,
+            n % 2,
+            ref["p%d" % n].at[link.c],
+            ref["p%d" % n].at[1 - link.c],
+            [ref["f%d_%d" % (n, k)] for k in range(4)],
+            result.at[:, pl.ds(left, wide)],
+            ref.send.at[n],
+            ref.arrive.at[n],
+        )
+        tasks += begun([task])
+        step_at(len(tasks) - 1)
+    share = -(-blocks // 4)
+    for late in range(MIX_LAGS[-1]):
+        step_at(len(order) + late)
+        for b in range(late * share, min(blocks, (late + 1) * share)):
+            shared_gradients(b)
+        if late == 3:
+            ref.b_grad[...] = ref.b_acc[...].astype(bf16)
+            grad_out = bring(ref.b_grad, ref.o_shared, ref.load.at[0])
     link.drain()
-    for copy in outs:
-        if copy is not None:
-            copy.wait()
     grad_out.wait()
 
 
@@ -1410,15 +1432,13 @@
         b_hidden=pltpu.VMEM((blocks, rows, third), bf16),
         b_both=pltpu.VMEM((blocks, rows, 2 * third), bf16),
         b_source=pltpu.VMEM((2, blocks, slots, wide), bf16),
-        b_stage=pltpu.VMEM((2, blocks * PAIR, PAIR, sub, wide), bf16),
         load=DMA((2,)),
         fetch=DMA((2, 2)),
         pull=DMA((2,)),
-        push=DMA((2,)),
-        send=DMA((len(chunks), total_hops(deep))),
-        arrive=DMA((len(chunks), total_hops(deep))),
-    )
-    for n, (_, columns) in enumerate(chunks):
+        send=DMA((2 * len(chunks), total_hops(deep))),
+        arrive=DMA((2 * len(chunks), total_hops(deep))),
+    )
+    for n, (_, columns) in enumerate(chunks + chunks[:-1]):
         scratch["p%d" % n] = pltpu.VMEM((PAIR, blocks * PAIR, sub, columns), bf16)
         for k, buffer in enumerate(total_buffers(deep, sub, columns)):
             scratch["f%d_%d" % (n, k)] = buffer
@@ -1426,10 +1446,10 @@
     return pl.pallas_call(
         functools.partial(mix_kernel, groups, tuple(chunks), tuple(names)),
         in_specs=specs,
-        out_specs=[IN_VMEM, ANY, ANY],
+        out_specs=[IN_VMEM, IN_VMEM, ANY],
         out_shape=[
             jax.ShapeDtypeStruct((sub, width + experts_wide), f32),
-            jax.ShapeDtypeStruct((blocks * PAIR, PAIR, sub, width), bf16),
+            jax.ShapeDtypeStruct((sub, width), f32),
             jax.ShapeDtypeStruct(shared.shape, bf16),
         ],
         scratch_shapes=list(scratch.values()),
@@ -1572,9 +1592,9 @@
     def over_expert(name):
         if name not in totals:
             leave(name)
-            return []
+            return
         i = totals[name]
-        return begun(
+        tasks = begun(
             [
                 expert_total(
                     link,
@@ -1588,6 +1608,18 @@
                 )
             ]
         )
+        queue.extend([task, deep - 1] for task in tasks)
+
+    queue, finishing = [], []
+
+    def pump(count):
+        while count and queue:
+            entry = queue[0]
+            next(entry[0], None)
+            entry[1] -= 1
+            count -= 1
+            if not entry[1]:
+                finishing.append(queue.pop(0)[0])
 
     shared_tasks = []
     if SHARED in axis_of:
@@ -1612,18 +1644,6 @@
         )
         placed.append(None)
 
-    mixed_parts = len([name for name in names if name[:1] == "m" and name[1:].isdigit()])
-    mixed_loads = []
-    for n in range(mixed_parts):
-        wide = ref.i_block.shape[1] // mixed_parts
-        mixed_loads.append(
-            bring(
-                ref.i_partial.at[:, link.c, :, pl.ds(n * wide, wide)],
-                ref["m%d" % n],
-                ref.mixed_load.at[n],
-            )
-        )
-
     sub, width = ref.i_middle.shape
     experts = ref.i_router.shape[0]
     middle = ref.i_middle[...]
@@ -1650,11 +1670,13 @@
     ref.b_middle_grad[...] = middle_grad
     ref.b_grad_rows[...] = middle_grad.astype(bf16)
     tensor_tasks = begun([over_tensor(ref.b_grad_rows, ref.b_attention_grad, 0, sub)])
+    ref.b_block_rows[...] = (middle + ref.i_mixed[...]).astype(bf16)
     ref.b_router[...] = matmul_tn(dlogits, (normed * ffn_gain).astype(bf16)).astype(bf16)
-    expert_tasks = over_expert(ROUTER)
+    over_expert(ROUTER)
     gain_sums = {1: jnp.sum(dsecond * normed, axis=0, keepdims=True)}
 
     run(tensor_tasks)
+    block_tasks = begun([over_tensor(ref.b_block_rows, ref.o_block_out, 0, sub)])
     placed[1 if SHARED in axis_of else 0].wait()
     placed[1 if SHARED in axis_of else 0] = None
 
@@ -1664,28 +1686,7 @@
         ref.b_out_proj[at : at + 256, :] = matmul_tn(
             attended[:, at : at + 256], attention_grad[...]
         ).astype(bf16)
-    expert_tasks += over_expert(OUT_PROJ)
-    mixed_tasks = []
-    if I_PARTIAL in ref:
-        partial = ref.i_partial
-        for load in mixed_loads:
-            load.wait()
-        for n in range(mixed_parts):
-            wide = width // mixed_parts
-            span = pl.ds(n * wide, wide)
-            mixed_tasks.append(
-                device_total(
-                    link,
-                    1,
-                    ref["m%d" % n],
-                    partial.at[:, 1 - link.c, :, span],
-                    [ref["m%d_%d" % (n, k)] for k in range(4)],
-                    ref.b_mixed.at[:, span],
-                    ref.mixed_send.at[n],
-                    ref.mixed_arrive.at[n],
-                )
-            )
-        mixed_tasks = begun(mixed_tasks)
+    over_expert(OUT_PROJ)
     ref.b_attended_grad[...] = matmul_nt(attention_grad[...], out_proj[...]).astype(bf16)
 
     queries, keys, values = ready(QUERIES, KEYS, VALUES)
@@ -1719,8 +1720,8 @@
         base = h * (NOPE + VD)
         ref.b_dkeyval[:, base : base + NOPE] = dkeys[:, :NOPE].astype(bf16)
         ref.b_dkeyval[:, base + NOPE : base + NOPE + VD] = dvalues.astype(bf16)
-        advance(expert_tasks)
-        advance(mixed_tasks[h % max(1, len(mixed_tasks)) :][:1])
+        if h:
+            pump(1)
     dkey_rope = turn(dkey_rope, cosine, -sinusoid)
 
     query_n, latent_n, query_up, latent_up = ready(QUERY_N, LATENT_N, QUERY_UP, LATENT_UP)
@@ -1729,12 +1730,12 @@
         ref.b_query_up[at : at + 256, :] = matmul_tn(
             query_n[:, at : at + 256], ref.b_dquery[...]
         ).astype(bf16)
-    expert_tasks += over_expert(QUERY_UP)
+    over_expert(QUERY_UP)
     for at in range(0, latent_rank, 256):
         ref.b_latent_up[at : at + 256, :] = matmul_tn(
             latent_n[:, at : at + 256], ref.b_dkeyval[...]
         ).astype(bf16)
-    expert_tasks += over_expert(LATENT_UP)
+    over_expert(LATENT_UP)
     partial = ref.b_heads_partial
     lead = query_rank + latent_rank
     for quarter in range(parts):
@@ -1761,8 +1762,7 @@
             )
         ]
     )
-    advance(expert_tasks)
-    advance(mixed_tasks)
+    pump(1)
     run(sum_tasks)
 
     heads_rows = ref.b_heads_rows
@@ -1792,8 +1792,7 @@
             over_tensor(ref.b_latent_rows, ref.b_dlatent_all, 0, sub),
         ]
     )
-    advance(expert_tasks)
-    advance(mixed_tasks)
+    pump(1)
     run(tensor_tasks)
     for n in (own, own + 1):
         placed[n].wait()
@@ -1812,13 +1811,13 @@
         ref.b_query_down[at : at + 256, :] = matmul_tn(
             first[:, at : at + 256], dquery_lat
         ).astype(bf16)
-    expert_tasks += over_expert(QUERY_DOWN)
+    over_expert(QUERY_DOWN)
     for at in range(0, width, 512):
         ref.b_latent_down[:, at : at + 512] = matmul(dlatent_t, first[:, at : at + 512]).astype(
             bf16
         )
-    expert_tasks += over_expert(LATENT_DOWN)
-    advance(expert_tasks)
+    over_expert(LATENT_DOWN)
+    pump(1)
     partial = ref.b_first_partial
     for quarter in range(parts):
         span = slice(quarter * sub, (quarter + 1) * sub)
@@ -1840,7 +1839,7 @@
             )
         ]
     )
-    advance(expert_tasks)
+    pump(1)
     run(sum_tasks)
     residual = ref.i_block[pl.ds(start, sub), :].astype(f32)
     back, gain_sums[0] = norm_back(
@@ -1860,13 +1859,9 @@
             ref.b_gains[e * 8 + i : e * 8 + i + 1, :] = moved[:1, :wide]
     for e in range(groups):
         ref.b_gains[e * 8 + len(sizes) : e * 8 + 8, :] = jnp.zeros((8 - len(sizes), wide), f32)
-    expert_tasks += over_expert(GAINS)
-    advance(expert_tasks)
-    run(mixed_tasks)
-    mixed = ref.b_mixed if I_PARTIAL in ref else ref.i_mixed
-    ref.b_block_rows[...] = (middle + mixed[...]).astype(bf16)
-    block_tasks = begun([over_tensor(ref.b_block_rows, ref.o_block_out, 0, sub)])
-    run(expert_tasks)
+    over_expert(GAINS)
+    pump(len(queue) * deep)
+    run(finishing)
 
     finished = ("o_query_down", "o_latent_down")
     finals = []
@@ -1904,7 +1899,7 @@
         move.wait()
 
 
-def back_stage(calls, groups, parts, sizes, held, small, grad_shared, partial):
+def back_stage(calls, groups, parts, sizes, held, small, grad_shared):
     deep = groups // PAIR
     bf16, f32 = jnp.bfloat16, jnp.float32
     rows, width = small.block.shape
@@ -1996,18 +1991,6 @@
         scratch.shared_send = scratch.shared_arrive = DMA((groups,))
     inputs |= {"h_" + name: array for name, array in held.items()}
     specs += [ANY] * len(held)
-    if partial is not None:
-        inputs[I_PARTIAL] = partial
-        specs.append(ANY)
-        mixed_parts = max(1, width // 512)
-        wide = width // mixed_parts
-        for n in range(mixed_parts):
-            scratch["m%d" % n] = pltpu.VMEM((groups * half, sub, wide), bf16)
-            for k, buffer in enumerate(total_buffers(deep, sub, wide)):
-                scratch["m%d_%d" % (n, k)] = buffer
-        scratch.b_mixed = pltpu.VMEM((sub, width), f32)
-        scratch.mixed_load = DMA((mixed_parts,))
-        scratch.mixed_send = scratch.mixed_arrive = DMA((mixed_parts, total_hops(deep)))
     scratch.load = DMA((len(held),))
     scratch.leave = DMA((len(outs) + 1,))
     scratch.place = DMA((12,))
@@ -2127,14 +2110,14 @@
         for pair in ((cosine, cosine), (-sinusoid, sinusoid))
     ]
     items = [
-        (GAINS, gains, 0, None, EXPERT, ("zx",), VMEM_),
+        (GAINS, gains, 0, None, EXPERT, ("e",), VMEM_),
         (QUERY_DOWN, query_down, 0, (1, query_cut), EXPERT, ("zx",), VMEM_),
         (LATENT_DOWN, latent_down.T, 1, (0, latent_cut), EXPERT, ("zx",), VMEM_),
         (QUERY_UP, query_up, 0, None, EXPERT, ("zx",), VMEM_),
         (LATENT_UP, latent_up, 0, None, EXPERT, ("zx",), VMEM_),
         (OUT_PROJ, out_proj, 1, None, EXPERT, ("zx",), VMEM_),
         (ROUTER, router.T, 1, None, EXPERT, ("zx",), VMEM_),
-        (ROUTES, routes_pad, 1, None, EXPERT, ("zx",), "hbm"),
+        (ROUTES, routes_pad, 1, None, EXPERT, ("e",), "hbm"),
         (SHARED, shared, 1, None, SHUFFLE, (), "hbm"),
         (OUT_GRAD, out_grad, 0, (0, row_count // parts), "all", (ZXYC, "xzyc"), "hbm"),
     ]
@@ -2172,8 +2155,7 @@
     slot_dweights = slot_dweights.reshape(groups, slots, 1)
     slot_lanes = jnp.repeat(own_ids, CAP)[:, None]
     if mix_bytes(groups, row_count, slots, width) < 40 * 2**20:
-        mixed = None
-        dsecond, partial, grad_shared = mix_stage(
+        dsecond, mixed, grad_shared = mix_stage(
             calls,
             groups,
             parts,
@@ -2187,7 +2169,6 @@
             shared,
         )
     else:
-        partial = None
         lane_ids = jnp.arange(experts + lane_pad, dtype=jnp.int32)
         spread_out = jnp.where(slot_lanes == lane_ids[None, :], slot_dweights, 0.0)
         mixed_part, dsecond_part, grad_shared = combine_stage(
@@ -2230,6 +2211,7 @@
     )
     small = Bag(
         dsecond=dsecond,
+        mixed=mixed,
         middle=front.middle,
         chosen=front.chosen,
         router=router_t,
@@ -2240,9 +2222,7 @@
         sinusoid=tables[1],
         norms=front.norms,
     )
-    if partial is None:
-        small.mixed = mixed
-    back = back_stage(calls, groups, parts, gain_sizes, held, small, grad_shared, partial)
+    back = back_stage(calls, groups, parts, gain_sizes, held, small, grad_shared)
     grad_shared = back.shared.reshape(groups, 3, shared_units, -1).transpose(1, 0, 2, 3)
     grad_shared = grad_shared.astype(jnp.float32).reshape(3, groups * shared_units, -1)
     grad_gains = [back.gains[i, :size] for i, size in enumerate(gain_sizes)]

time: 592 us -> 542 us (0.916)
  Pallas kernels: 555 us -> 505 us
    pallas_call x1, Pallas kernels: 175 us -> 128 us  [back_stage(): pl.pallas_call(functools.partial(back_kernel, groups, tuple(sizes), tuple...]
    pallas_call x1, Pallas kernels: 203 us -> 191 us  [front_stage(): pl.pallas_call(functools.partial(front_kernel, groups, tuple(sizes), tupl...]
    pallas_call x1, Pallas kernels: 106 us -> 115 us  [mix_stage(): pl.pallas_call(functools.partial(mix_kernel, groups, tuple(chunks), tuple...]
where the time goes in v3:
time: 542 us; the launch traced here: 532 us
  Pallas kernels  505 us (93%)
  local copies, waits for them, and re-layouts  16.1 us (3%)
  other arithmetic  9.54 us (2%)
    pallas_call x1, Pallas kernels, front_stage(): pl.pallas_call(functools.partial(front_kernel, groups, tuple(sizes), tupl...  191 us
    pallas_call x1, Pallas kernels, back_stage(): pl.pallas_call(functools.partial(back_kernel, groups, tuple(sizes), tuple...  128 us
    pallas_call x1, Pallas kernels, mix_stage(): pl.pallas_call(functools.partial(mix_kernel, groups, tuple(chunks), tuple...  115 us
    pallas_call x1, Pallas kernels, expert_stage(): pl.pallas_call(expert_kernel, grid=(local, blocks // step), in_specs=[row...  54.1 us
    pallas_call x1, Pallas kernels, route_stage(): pl.pallas_call(route_kernel, grid=(groups,), in_specs=[pl.BlockSpec((loca...  17 us

profile of v3, /device:TPU:0, one launch (start us, length us, event | category | flops | bytes accessed | tf_op | source)
XLA Modules:
  0.0 532.1 jit_solution(12804403337886682316)
XLA Ops:
  0.7 0.0 copy-start.8
  0.7 0.0 copy-start.9
  0.7 0.6 iota_add_fusion.ids_ref
  1.3 0.7 pad.28
  1.9 0.7 pad.27
  2.6 0.7 stack.33
  3.3 0.7 stack.32
  3.9 0.6 fusion.10.refs_0_
  4.5 1.3 pad.31.refs_7_
  5.8 2.3 pad_maximum_fusion
  8.1 0.0 copy-done.8
  8.1 0.8 copy.56.refs_11_
  8.9 0.0 copy-done.9
  8.9 0.2 reduce-window.4
  9.1 0.1 convert_reduce_fusion
  9.2 0.8 fusion.1.refs_12_.refs_7_
  10.0 0.1 select_reduce_fusion
  10.1 0.5 fusion.2
  10.7 0.8 select_maximum_fusion
  11.5 191.3 %front.1 = (f32[64,256]{1,0:T(8,128)}, bf16[2048,384]{1,0:T(8,128)(2,1)}, bf16[144,2048]{1,0:T(8,128)(2,1)}, bf16[1536,768]{1,0:T(8,128)(2,1)}, bf16[512,1024]{1...) custom-call(f32[8,256]{1,0:T(8,128)} %fusion.10.refs_0_, ...), custom_call_target="tpu_custom_call" | custom-call | tf_op jit(solution)/shard_map/front/pallas_call | solution.py:1089
  202.8 17.0 %route.1 = (bf16[8,256,2048]{2,1,0:T(8,128)(2,1)}, bf16[8,256,2048]{2,1,0:T(8,128)(2,1)}, bf16[8,256,256]{2,1,0:T(8,128)(2,1)}, f32[8,256,1]{2,1,0:T(8,128)}) custom-call(s32[8,1]{1,0:T(8,128)} %iota_add_fusion.ids_ref, s32[8,2048]{1,0:T(8,128)} %get-tuple-element.64.routes_ref, bf16[2048,2048]{1,0:T(8,128)(2,1)} %get-tuple-element.65.x_ref.refs_5_, ...), custom_call_target="tpu_custom_call" | custom-call | tf_op jit(solution)/shard_map/route/pallas_call | solution.py:1229
  219.8 54.1 %experts.1 = (bf16[8,8,32,2048]{3,2,1,0:T(8,128)(2,1)}, bf16[8,8,32,2048]{3,2,1,0:T(8,128)(2,1)}, f32[8,8,32,1]{3,2,1,0:T(8,128)}, f32[8,352,2048]{2,1,0:T(8,128...) custom-call(bf16[8,8,32,2048]{3,2,1,0:T(8,128)(2,1)} %bitcast.76, bf16[8,8,32,2048]{3,2,1,0:T(8,128)(2,1)} %bitcast.77, ...), custom_call_target="tpu_custom_call" | custom-call | flops 26575110144 | bytes 137363456 | tf_op jit(solution)/shard_map/experts/pallas_call | solution.py:145
  273.9 0.1 broadcast_in_dim.19
  274.0 0.8 broadcast_in_dim_reshape.4.refs_4_
  274.7 114.7 %mix.1 = (f32[64,2176]{1,0:T(8,128)}, f32[64,2048]{1,0:T(8,128)}, bf16[264,2048]{1,0:T(8,128)(2,1)}) custom-call(bf16[8,256,256]{2,1,0:T(8,128)(2,1)} %get-tuple-element.68.refs_0_, bf16[8,256,2048]{2,1,0:T(8,128)(2,1)} %bitcast.56, bf16[8,256,2048]{2,1,0:T(8,128)(2,1)} %bitcast.57, f32[8,256,1]{2,1,0:T(8,128)} %bitcast.60, ...), custom_call_target="tpu_custom_call" | custom-call | tf_op jit(solution)/shard_map/mix/pallas_call | solution.py:1446
  389.4 128.2 %back.1 = (bf16[256,2048]{1,0:T(8,128)(2,1)}, bf16[256,2048]{1,0:T(8,128)(2,1)}, f32[512,256]{1,0:T(8,128)}, f32[192,768]{1,0:T(8,128)}, f32[64,1024]{1,0:T(8,12...) custom-call(f32[64,2176]{1,0:T(8,128)} %get-tuple-element.76.refs_0_, ...), custom_call_target="tpu_custom_call" | custom-call | tf_op jit(solution)/shard_map/back/pallas_call | solution.py:2002
  517.6 0.0 copy-start.5
  517.6 0.0 copy-start
  517.6 1.4 fusion.13
  519.0 2.5 convert_element_type.47
  521.5 1.3 slice.25
  522.7 0.0 copy-done.5
  522.7 0.9 convert_bitcast_fusion.1
  523.6 1.2 slice_bitcast_fusion
  524.8 0.0 copy-done
  524.8 0.2 convert_bitcast_fusion
  524.9 0.0 copy-start.2
  525.0 0.0 copy-start.1
  525.0 1.4 fusion.12
  526.3 0.0 copy-start.3
  526.3 0.4 copy-done.2
  526.7 0.0 copy-start.6
  526.7 1.0 copy.64
  527.7 0.0 copy-done.1
  527.7 0.0 copy-start.4
  527.7 0.0 copy-start.7
  527.7 1.0 copy.65
  528.7 0.0 copy-done.3
  528.7 0.8 copy.66
  529.5 0.0 copy-done.6
  529.5 0.7 copy.67
  530.2 0.0 copy-done.4
  530.2 0.8 copy.68
  531.0 0.0 copy-done.7
  531.0 0.6 copy.69
  (6 shorter events, 0.0 us)
Async XLA Ops:
  0.7 7.5 %copy-start.8 = (s32[256,6]{0,1:T(8,128)S(1)}, s32[256,6]{0,1:T(8,128)}, u32[]{:S(2)}) copy-start(s32[256,6]{0,1:T(8,128)} %param.38) | copy-start | bytes 18436
  0.7 8.3 %copy-start.9 = (s32[1,3]{1,0:T(1,128)S(1)}, s32[1,3]{1,0:T(1,128)}, u32[]{:S(2)}) copy-start(s32[1,3]{1,0:T(1,128)} %param.37) | copy-start | bytes 40
  517.6 5.1 copy-start.5
  517.6 7.2 %copy-start = (bf16[8,264,256]{2,1,0:T(8,128)(2,1)S(1)}, bf16[8,264,256]{2,1,0:T(8,128)(2,1)}, u32[]{:S(2)}) copy-start(bf16[8,264,256]{2,1,0:T(8,128)(2,1)} %get-tuple-element.106) | copy-start | bytes 3244036
  524.9 1.8 copy-start.2
  525.0 2.8 copy-start.1
  526.3 2.3 copy-start.3
  526.7 2.8 copy-start.6
  527.7 2.5 copy-start.4
  527.7 3.3 copy-start.7

commit v4 on v3

--- a/solution.py
+++ b/solution.py
@@ -662,6 +662,9 @@
 def full_gain(gains, row, size, groups):
     total = size * groups
     wide = gains.shape[1]
+    if size % LANES == 0:
+        shares = [gains[e * 8 + row : e * 8 + row + 1, :size] for e in range(groups)]
+        return jnp.concatenate(shares, axis=1)
     result = jnp.zeros((8, total), jnp.float32)
     for e in range(groups):
         share = jnp.broadcast_to(gains[e * 8 + row : e * 8 + row + 1, :], (8, wide))
@@ -677,6 +680,10 @@
         return carry
 
     lax.fori_loop(0, count // step, one, 0)
+
+
+def by_rows(count, work):
+    rows_loop(count, 16 if count % 16 == 0 else count, work)
 
 
 def front_kernel(groups, sizes, plan, names, *refs):
@@ -922,50 +929,33 @@
             attended[quarter * sub : (quarter + 1) * sub, :], landing.out_proj[...]
         ).astype(jnp.bfloat16)
 
-    def beside_copy():
-        return pltpu.make_async_remote_copy(
-            src_ref=partial.at[:, 1 - c],
-            dst_ref=from_beside,
-            send_sem=swap_send.at[0],
-            recv_sem=swap_arrive.at[0],
-            device_id=link.peer("c"),
-            device_id_type=MESH,
-        )
-
-    def across_copy():
-        return pltpu.make_async_remote_copy(
-            src_ref=give,
-            dst_ref=from_across,
-            send_sem=swap_send.at[1],
-            recv_sem=swap_arrive.at[1],
-            device_id=link.peer("y"),
-            device_id_type=MESH,
-        )
-
-    link.emit(beside_copy)
+    sum_task = tensor_total(
+        link, partial, from_beside, give, from_across, middle_ref, swap_send, swap_arrive
+    )
+    next(sum_task, None)
     advance(late_tasks, 1)
-    arrived(from_beside, swap_arrive.at[0])
-    give[...] = partial[1 - y, c] + from_beside[1 - y]
-    link.emit(across_copy)
+    next(sum_task, None)
     complete(OUT_GRAD)
     complete(SHARED)
-    residual = block_ref[pl.ds(pl.multiple_of(part * sub, sub), sub), :].astype(jnp.float32)
-    middle_ref[...] = (
-        residual + partial[y, c].astype(jnp.float32) + from_beside[y].astype(jnp.float32)
-    )
     advance(late_tasks, 1)
-    arrived(from_across, swap_arrive.at[1])
-    middle = middle_ref[...] + from_across[...].astype(jnp.float32)
-    middle_ref[...] = middle
+    next(sum_task, None)
     ffn_gain = full_gain(gains, 1, sizes[1], groups)
     norms = ref.b_norms
     norms[...] = jnp.zeros(norms.shape, jnp.float32)
     for i, gain in enumerate((attention_gain, ffn_gain, query_gain, latent_gain)):
         norms[i : i + 1, : gain.shape[1]] = gain
     keep_out("norms", norms)
-    inverse = lax.rsqrt(jnp.mean(middle * middle, axis=-1, keepdims=True) + EPSILON)
     second_ref, weights_ref, chosen_ref = ref.b_second, ref.b_weights, ref.b_chosen
-    second_ref[...] = (middle * inverse * ffn_gain).astype(jnp.bfloat16)
+    start = pl.multiple_of(part * sub, sub)
+
+    def middle_norm(span):
+        mine = pl.ds(pl.multiple_of(start + span.start, 16), span.size)
+        middle = middle_ref[span, :] + block_ref[mine, :].astype(jnp.float32)
+        middle_ref[span, :] = middle
+        inverse = lax.rsqrt(jnp.mean(middle * middle, axis=-1, keepdims=True) + EPSILON)
+        second_ref[span, :] = (middle * inverse * ffn_gain).astype(jnp.bfloat16)
+
+    by_rows(sub, middle_norm)
     logits = matmul_nt(second_ref[...], landing.router[...])
     experts = logits.shape[1]
     advance(late_tasks, 1)
@@ -989,7 +979,7 @@
         return home_of
 
     all_tasks = streams_of(weights_ref, row_home(WEIGHTS), (ZXYC,))
-    all_tasks += streams_of(second_ref, row_home(TOKENS), (ZXYC, "zyxc") * 2)
+    all_tasks += streams_of(second_ref, row_home(TOKENS), (ZXYC, "zyxc"))
     all_tasks = [task for task in all_tasks if next(task, run) is not run]
     mine = link.me * PAIR * PAIR + part
     kept.append(bring(second_ref, slot(ref.o_tokens, 0, mine, sub), leave.at[len(kept)]))
@@ -1080,7 +1070,7 @@
         jax.ShapeDtypeStruct((sub * groups * parts, width), bf16),
         jax.ShapeDtypeStruct((sub * groups * parts, lanes), f32),
     ]
-    streams += 2 + 1 + 4
+    streams += 2 + 1 + 2
     scratch.send = scratch.arrive = DMA((streams, 8 * deep))
     scratch.own = DMA((len(items),))
     scratch.leave = DMA((len(out_names),))
@@ -1167,12 +1157,17 @@
             from_deep.at[k - 1],
             link.at_z((z + k) % deep),
         )
-    total = own[at(z, mine, following)].astype(jnp.float32)
     yield
     for k in range(1, deep):
         arrived(from_deep.at[k - 1], arrive.at[base + k])
-        total = total + from_deep[k - 1].astype(jnp.float32)
-    result[...] = total
+
+    def finish(span):
+        total = own[at(z, mine, following), span, :].astype(jnp.float32)
+        for k in range(1, deep):
+            total = total + from_deep[k - 1, span, :].astype(jnp.float32)
+        result[span, :] = total
+
+    by_rows(result.shape[0], finish)
 
 
 def total_buffers(deep, rows, wide):
@@ -1276,8 +1271,6 @@
             pltpu.make_async_copy(ref.i_gradients.at[span, :], ref.b_g.at[at], ref.fetch.at[at, 1]),
         )
 
-    for copy in fetch(0, 0):
-        copy.start()
     many = len(chunks)
     work = [(True, *chunk) for chunk in chunks] + [(False, *chunk) for chunk in chunks[:-1]]
 
@@ -1291,32 +1284,46 @@
         )
 
     has_source = [n != many - 1 for n in range(len(work))]
-    order = [many - 1] + [n for n in range(len(work)) if has_source[n]]
-    turn_of = {n: i % 2 for i, n in enumerate(order)}
+    order = [n for n in range(many, len(work))] + [many - 1] + list(range(many - 1))
+    turn_of = {n: i % 2 for i, n in enumerate(n for n in order if has_source[n])}
     for load in loads:
         load.wait()
     ref.b_acc[...] = jnp.zeros(ref.b_acc.shape, f32)
 
-    def block(b, carry):
-        at = b % 2
-
-        @pl.when(b + 1 < blocks)
-        def _():
-            for copy in fetch(b + 1, 1 - at):
-                copy.start()
-
-        for copy in fetch(b, at):
-            copy.wait()
-        row_inputs, cotangent = ref.b_x[at], ref.b_g[at]
-        pre = matmul_nt(row_inputs, ref.b_shared[: 2 * units, :])
+    def fetch_one(which, b, at):
+        source, target, column = (
+            (ref.i_tokens, ref.b_x, 0) if which == 0 else (ref.i_gradients, ref.b_g, 1)
+        )
+        span = pl.ds(pl.multiple_of(b * rows, rows), rows)
+        return pltpu.make_async_copy(source.at[span, :], target.at[at], ref.fetch.at[at, column])
+
+    def over_blocks(which, work):
+        fetch_one(which, 0, 0).start()
+
+        def one(b, carry):
+            at = b % 2
+
+            @pl.when(b + 1 < blocks)
+            def _():
+                fetch_one(which, b + 1, 1 - at).start()
+
+            fetch_one(which, b, at).wait()
+            work(b, at)
+            return carry
+
+        lax.fori_loop(0, blocks, one, 0)
+
+    def forward_block(b, at):
+        pre = matmul_nt(ref.b_x[at], ref.b_shared[: 2 * units, :])
+        ref.b_pre[b] = pre
+        ref.b_hidden[b] = swiglu(pre[:, :units], pre[:, units:])[1]
+
+    def backward_block(b, at):
+        pre = ref.b_pre[b]
         gate_pre, up_pre = pre[:, :units], pre[:, units:]
-        sigmoid_gate, hidden = swiglu(gate_pre, up_pre)
-        dhidden = matmul_nt(cotangent, ref.b_shared[2 * units :, :])
-        gate_grad, up_grad = swiglu_back(dhidden, gate_pre, up_pre, sigmoid_gate)
-        both = jnp.concatenate([gate_grad, up_grad], axis=1)
-        ref.b_hidden[b] = hidden
-        ref.b_both[b] = both
-        return carry
+        dhidden = matmul_nt(ref.b_g[at], ref.b_shared[2 * units :, :])
+        grads = swiglu_back(dhidden, gate_pre, up_pre, jax.nn.sigmoid(gate_pre))
+        ref.b_both[b] = jnp.concatenate(grads, axis=1)
 
     def shared_gradients(b):
         at = b % 2
@@ -1328,10 +1335,8 @@
         ref.b_acc[: 2 * units, :] += matmul_tn(ref.b_both[b], ref.b_x[at])
         ref.b_acc[2 * units :, :] += matmul_tn(ref.b_hidden[b], ref.b_g[at])
 
-    source_of(order[1]).start()
-    lax.fori_loop(0, blocks, block, 0)
-    for copy in fetch(0, 0):
-        copy.start()
+    source_of(order[0]).start()
+    over_blocks(0, forward_block)
     dw_lane = lax.broadcasted_iota(jnp.int32, (slots, chunks[-1][1]), 1)
     tasks = []
 
@@ -1384,6 +1389,10 @@
         )
         tasks += begun([task])
         step_at(len(tasks) - 1)
+        if n == many + 2:
+            over_blocks(1, backward_block)
+    for copy in fetch(0, 0):
+        copy.start()
     share = -(-blocks // 4)
     for late in range(MIX_LAGS[-1]):
         step_at(len(order) + late)
@@ -1429,6 +1438,7 @@
         b_g=pltpu.VMEM((2, rows, width), bf16),
         b_acc=pltpu.VMEM(shared.shape, f32),
         b_grad=pltpu.VMEM(shared.shape, bf16),
+        b_pre=pltpu.VMEM((blocks, rows, 2 * third), f32),
         b_hidden=pltpu.VMEM((blocks, rows, third), bf16),
         b_both=pltpu.VMEM((blocks, rows, 2 * third), bf16),
         b_source=pltpu.VMEM((2, blocks, slots, wide), bf16),
@@ -1494,12 +1504,24 @@
     link.emit(beside)
     yield
     arrived(from_beside, arrive.at[0])
-    give[...] = partial[1 - y, c] + from_beside[1 - y]
+    rows = result.shape[0]
+
+    def add_given(span):
+        give[span, :] = partial[1 - y, c, span, :] + from_beside[1 - y, span, :]
+
+    def add_kept(span):
+        kept = partial[y, c, span, :].astype(jnp.float32)
+        result[span, :] = kept + from_beside[y, span, :].astype(jnp.float32)
+
+    def add_last(span):
+        result[span, :] = result[span, :] + from_across[span, :].astype(jnp.float32)
+
+    by_rows(rows, add_given)
     link.emit(across)
-    result[...] = partial[y, c].astype(jnp.float32) + from_beside[y].astype(jnp.float32)
+    by_rows(rows, add_kept)
     yield
     arrived(from_across, arrive.at[1])
-    result[...] = result[...] + from_across[...].astype(jnp.float32)
+    by_rows(rows, add_last)
 
 
 def expert_total(link, axis, grad, from_twin, from_deep, result, send, arrive):
@@ -1536,16 +1558,26 @@
         yield
         arrived(from_twin.at[k], arrive.at[k])
         mine = slot(grad, axis, target(k) * PAIR + x, size)
-        from_twin[k] = from_twin[k] + mine[...]
+
+        def add(span, mine=mine, k=k):
+            from_twin[k, span, :] = from_twin[k, span, :] + mine[span, :]
+
+        by_rows(result.shape[0], add)
         link.emit(functools.partial(to_deep, k))
     yield
     arrived(from_twin.at[0], arrive.at[0])
-    total = slot(grad, axis, z * PAIR + x, size)[...].astype(jnp.float32)
-    result[...] = total + from_twin[0].astype(jnp.float32)
+    mine = slot(grad, axis, z * PAIR + x, size)
+
+    def finish(span):
+        total = mine[span, :].astype(jnp.float32) + from_twin[0, span, :].astype(jnp.float32)
+        for k in range(1, deep):
+            total = total + from_deep[k - 1, span, :].astype(jnp.float32)
+        result[span, :] = total
+
     for k in range(1, deep):
         yield
         arrived(from_deep.at[k - 1], arrive.at[deep + k])
-        result[...] = result[...] + from_deep[k - 1].astype(jnp.float32)
+    by_rows(result.shape[0], finish)
 
 
 def back_kernel(groups, sizes, reduced, names, *refs):
@@ -1646,11 +1678,24 @@
 
     sub, width = ref.i_middle.shape
     experts = ref.i_router.shape[0]
-    middle = ref.i_middle[...]
     norms = [ref.i_norms[i : i + 1, : size * groups] for i, size in enumerate(sizes)]
-    ffn_gain = norms[1]
-    inverse = lax.rsqrt(jnp.mean(middle * middle, axis=-1, keepdims=True) + EPSILON)
-    normed = middle * inverse
+    sums = ref.b_sums
+    sums[...] = jnp.zeros(sums.shape, f32)
+    start = pl.multiple_of(part * sub, sub)
+
+    def norm_back(which, values, cotangent):
+        inverse = lax.rsqrt(jnp.mean(values * values, axis=-1, keepdims=True) + EPSILON)
+        normed = values * inverse
+        scaled = cotangent * norms[which]
+        sums[which : which + 1, : values.shape[1]] += jnp.sum(
+            cotangent * normed, axis=0, keepdims=True
+        )
+        back = inverse * (scaled - normed * jnp.mean(scaled * normed, axis=-1, keepdims=True))
+        return (back, normed)
+
+    def own_rows(span):
+        return pl.ds(pl.multiple_of(start + span.start, 16), span.size)
+
     chosen = ref.i_chosen[:, :experts]
     dweights = ref.i_dsecond[:, width : width + experts]
     total = jnp.sum(chosen, axis=-1, keepdims=True)
@@ -1660,21 +1705,22 @@
         * (dweights - jnp.sum(dweights * chosen, axis=-1, keepdims=True) / total)
     )
     dlogits = (dchosen * chosen * (1.0 - chosen)).astype(bf16)
-    dsecond = ref.i_dsecond[:, :width] + matmul(dlogits, ref.i_router[...])
-    scaled = dsecond * ffn_gain
-    start = pl.multiple_of(part * sub, sub)
-    gradient = ref.i_out_grad[pl.ds(start, sub), :].astype(f32)
-    middle_grad = gradient + inverse * (
-        scaled - normed * jnp.mean(scaled * normed, axis=-1, keepdims=True)
-    )
-    ref.b_middle_grad[...] = middle_grad
-    ref.b_grad_rows[...] = middle_grad.astype(bf16)
+    ref.b_first_rows[...] = matmul(dlogits, ref.i_router[...])
+
+    def middle_back(span):
+        middle = ref.i_middle[span, :]
+        dsecond = ref.i_dsecond[span, :width] + ref.b_first_rows[span, :]
+        back, normed = norm_back(1, middle, dsecond)
+        middle_grad = ref.i_out_grad[own_rows(span), :].astype(f32) + back
+        ref.b_middle_grad[span, :] = middle_grad
+        ref.b_grad_rows[span, :] = middle_grad.astype(bf16)
+        ref.b_block_rows[span, :] = (middle + ref.i_mixed[span, :]).astype(bf16)
+        ref.b_input_rows[span, :] = (normed * norms[1]).astype(bf16)
+
+    by_rows(sub, middle_back)
     tensor_tasks = begun([over_tensor(ref.b_grad_rows, ref.b_attention_grad, 0, sub)])
-    ref.b_block_rows[...] = (middle + ref.i_mixed[...]).astype(bf16)
-    ref.b_router[...] = matmul_tn(dlogits, (normed * ffn_gain).astype(bf16)).astype(bf16)
+    ref.b_router[...] = matmul_tn(dlogits, ref.b_input_rows[...]).astype(bf16)
     over_expert(ROUTER)
-    gain_sums = {1: jnp.sum(dsecond * normed, axis=0, keepdims=True)}
-
     run(tensor_tasks)
     block_tasks = begun([over_tensor(ref.b_block_rows, ref.o_block_out, 0, sub)])
     placed[1 if SHARED in axis_of else 0].wait()
@@ -1726,10 +1772,11 @@
 
     query_n, latent_n, query_up, latent_up = ready(QUERY_N, LATENT_N, QUERY_UP, LATENT_UP)
     query_rank, latent_rank = query_n.shape[1], latent_n.shape[1]
-    for at in range(0, query_rank, 256):
-        ref.b_query_up[at : at + 256, :] = matmul_tn(
-            query_n[:, at : at + 256], ref.b_dquery[...]
-        ).astype(bf16)
+
+    def query_up_rows(span):
+        ref.b_query_up[span, :] = matmul_tn(query_n[:, span], ref.b_dquery[...]).astype(bf16)
+
+    rows_loop(query_rank, 256, query_up_rows)
     over_expert(QUERY_UP)
     for at in range(0, latent_rank, 256):
         ref.b_latent_up[at : at + 256, :] = matmul_tn(
@@ -1768,23 +1815,17 @@
     heads_rows = ref.b_heads_rows
     (query_lat, latent_t) = ready(QUERY_LAT, LATENT_T)
 
-    def norm_back(values, gain, cotangent):
-        inverse = lax.rsqrt(jnp.mean(values * values, axis=-1, keepdims=True) + EPSILON)
-        normed = values * inverse
-        scaled = cotangent * gain
-        back = inverse * (scaled - normed * jnp.mean(scaled * normed, axis=-1, keepdims=True))
-        return (back, jnp.sum(cotangent * normed, axis=0, keepdims=True))
-
-    query_rows = query_lat[pl.ds(start, sub), :].astype(f32)
-    back, gain_sums[2] = norm_back(query_rows, norms[2], heads_rows[:, :query_rank])
-    ref.b_query_rows[...] = back.astype(bf16)
     ref.b_latent_block[...] = latent_t[:latent_rank, :].astype(f32).T
-    latent_rows = ref.b_latent_block[pl.ds(start, sub), :]
-    back, gain_sums[3] = norm_back(
-        latent_rows, norms[3], heads_rows[:, query_rank:lead]
-    )
-    ref.b_latent_rows[:, :latent_rank] = back.astype(bf16)
-    ref.b_latent_rows[:, latent_rank:] = heads_rows[:, lead:].astype(bf16)
+
+    def latents_back(span):
+        mine = own_rows(span)
+        back, _ = norm_back(2, query_lat[mine, :].astype(f32), heads_rows[span, :query_rank])
+        ref.b_query_rows[span, :] = back.astype(bf16)
+        back, _ = norm_back(3, ref.b_latent_block[mine, :], heads_rows[span, query_rank:lead])
+        ref.b_latent_rows[span, :latent_rank] = back.astype(bf16)
+        ref.b_latent_rows[span, latent_rank:] = heads_rows[span, lead:].astype(bf16)
+
+    by_rows(sub, latents_back)
     own = len(placed)
     tensor_tasks = begun(
         [
@@ -1807,10 +1848,14 @@
     dlatent_t = ref.b_dlatent_t[
         pl.ds(pl.multiple_of(part * latent_cut, 8), latent_cut), :
     ].astype(bf16)
-    for at in range(0, width, 256):
-        ref.b_query_down[at : at + 256, :] = matmul_tn(
-            first[:, at : at + 256], dquery_lat
-        ).astype(bf16)
+    ref.b_dquery_cut[...] = dquery_lat
+
+    def query_down_rows(span):
+        ref.b_query_down[span, :] = matmul_tn(first[:, span], ref.b_dquery_cut[...]).astype(
+            bf16
+        )
+
+    rows_loop(width, 256, query_down_rows)
     over_expert(QUERY_DOWN)
     for at in range(0, width, 512):
         ref.b_latent_down[:, at : at + 512] = matmul(dlatent_t, first[:, at : at + 512]).astype(
@@ -1841,22 +1886,29 @@
     )
     pump(1)
     run(sum_tasks)
-    residual = ref.i_block[pl.ds(start, sub), :].astype(f32)
-    back, gain_sums[0] = norm_back(
-        residual, norms[0], ref.b_first_rows[...]
-    )
-    ref.b_input_rows[...] = (ref.b_middle_grad[...] + back).astype(bf16)
+
+    def first_back(span):
+        residual = ref.i_block[own_rows(span), :].astype(f32)
+        back, _ = norm_back(0, residual, ref.b_first_rows[span, :])
+        ref.b_input_rows[span, :] = (ref.b_middle_grad[span, :] + back).astype(bf16)
+
+    by_rows(sub, first_back)
     input_tasks = begun([over_tensor(ref.b_input_rows, ref.o_input_grad, 0, sub)])
     wide = ref.b_gains.shape[1]
     for i, size in enumerate(sizes):
-        sums = jnp.broadcast_to(gain_sums[i], (8, gain_sums[i].shape[1]))
-        span = sums.shape[1]
+        span = size * groups
+        total = jnp.broadcast_to(sums[i : i + 1, :span], (8, span))
         if span < wide:
-            sums = jnp.concatenate([sums, jnp.zeros((8, wide - span), f32)], axis=1)
+            total = jnp.concatenate([total, jnp.zeros((8, wide - span), f32)], axis=1)
             span = wide
         for e in range(groups):
-            moved = pltpu.roll(sums, span - e * size, 1) if e else sums
-            ref.b_gains[e * 8 + i : e * 8 + i + 1, :] = moved[:1, :wide]
+            if size % LANES == 0:
+                moved = total[:1, e * size : (e + 1) * size]
+                if size < wide:
+                    moved = jnp.concatenate([moved, jnp.zeros((1, wide - size), f32)], axis=1)
+            else:
+                moved = (pltpu.roll(total, span - e * size, 1) if e else total)[:1, :wide]
+            ref.b_gains[e * 8 + i : e * 8 + i + 1, :] = moved
     for e in range(groups):
         ref.b_gains[e * 8 + len(sizes) : e * 8 + 8, :] = jnp.zeros((8 - len(sizes), wide), f32)
     over_expert(GAINS)
@@ -1929,6 +1981,7 @@
             pieces[name] = tuple(piece)
     buffers = Bag(
         middle_grad=((sub, width), f32),
+        sums=((8, width), f32),
         grad_rows=((sub, width), bf16),
         block_rows=((sub, width), bf16),
         attention_grad=((rows, width), bf16),
@@ -1944,6 +1997,7 @@
         latent_rows=((sub, latent_rank + LANES), bf16),
         latent_block=((rows, latent_rank), f32),
         dquery_lat=((rows, query_rank), bf16),
+        dquery_cut=((rows, query_cut), bf16),
         dlatent_all=((rows, latent_rank + LANES), bf16),
         dlatent_t=((latent_rank + LANES, rows), f32),
         first_partial=((half, PAIR, sub, width), bf16),

time: 542 us -> 533 us (0.983); the launches traced: 532 us -> 532 us
  no operation moved by 1% of the time
where the time goes in v4:
time: 533 us; the launch traced here: 532 us
  Pallas kernels  505 us (95%)
  local copies, waits for them, and re-layouts  16.1 us (3%)
  other arithmetic  9.54 us (2%)
    pallas_call x1, Pallas kernels, front_stage(): pl.pallas_call(functools.partial(front_kernel, groups, tuple(sizes), tupl...  191 us
    pallas_call x1, Pallas kernels, back_stage(): pl.pallas_call(functools.partial(back_kernel, groups, tuple(sizes), tuple...  130 us
    pallas_call x1, Pallas kernels, mix_stage(): pl.pallas_call(functools.partial(mix_kernel, groups, tuple(chunks), tuple...  113 us
    pallas_call x1, Pallas kernels, expert_stage(): pl.pallas_call(expert_kernel, grid=(local, blocks // step), in_specs=[row...  54.3 us
    pallas_call x1, Pallas kernels, route_stage(): pl.pallas_call(route_kernel, grid=(groups,), in_specs=[pl.BlockSpec((loca...  16.9 us

profile of v4, /device:TPU:0, one launch (start us, length us, event | category | flops | bytes accessed | tf_op | source)
XLA Modules:
  0.0 531.8 jit_solution(2626611408988566673)
XLA Ops:
  0.7 0.0 copy-start.8
  0.7 0.0 copy-start.9
  0.7 0.6 iota_add_fusion.ids_ref
  1.3 0.7 pad.28
  1.9 0.7 pad.27
  2.6 0.7 stack.33
  3.3 0.7 stack.32
  3.9 0.6 fusion.10.refs_0_
  4.5 1.3 pad.31.refs_7_
  5.8 2.3 pad_maximum_fusion
  8.1 0.0 copy-done.8
  8.1 0.8 copy.56.refs_11_
  8.9 0.0 copy-done.9
  8.9 0.2 reduce-window.4
  9.1 0.1 convert_reduce_fusion
  9.2 0.8 fusion.1.refs_12_.refs_7_
  10.0 0.1 select_reduce_fusion
  10.1 0.5 fusion.2
  10.7 0.8 select_maximum_fusion
  11.5 190.7 %front.1 = (f32[64,256]{1,0:T(8,128)}, bf16[2048,384]{1,0:T(8,128)(2,1)}, bf16[144,2048]{1,0:T(8,128)(2,1)}, bf16[1536,768]{1,0:T(8,128)(2,1)}, bf16[512,1024]{1...) custom-call(f32[8,256]{1,0:T(8,128)} %fusion.10.refs_0_, ...), custom_call_target="tpu_custom_call" | custom-call | tf_op jit(solution)/shard_map/front/pallas_call | solution.py:1079
  202.3 16.9 %route.1 = (bf16[8,256,2048]{2,1,0:T(8,128)(2,1)}, bf16[8,256,2048]{2,1,0:T(8,128)(2,1)}, bf16[8,256,256]{2,1,0:T(8,128)(2,1)}, f32[8,256,1]{2,1,0:T(8,128)}) custom-call(s32[8,1]{1,0:T(8,128)} %iota_add_fusion.ids_ref, s32[8,2048]{1,0:T(8,128)} %get-tuple-element.64.routes_ref, bf16[2048,2048]{1,0:T(8,128)(2,1)} %get-tuple-element.65.x_ref.refs_5_, ...), custom_call_target="tpu_custom_call" | custom-call | tf_op jit(solution)/shard_map/route/pallas_call | solution.py:1224
  219.1 54.3 %experts.1 = (bf16[8,8,32,2048]{3,2,1,0:T(8,128)(2,1)}, bf16[8,8,32,2048]{3,2,1,0:T(8,128)(2,1)}, f32[8,8,32,1]{3,2,1,0:T(8,128)}, f32[8,352,2048]{2,1,0:T(8,128...) custom-call(bf16[8,8,32,2048]{3,2,1,0:T(8,128)(2,1)} %bitcast.76, bf16[8,8,32,2048]{3,2,1,0:T(8,128)(2,1)} %bitcast.77, ...), custom_call_target="tpu_custom_call" | custom-call | flops 26575110144 | bytes 137363456 | tf_op jit(solution)/shard_map/experts/pallas_call | solution.py:145
  273.4 0.1 broadcast_in_dim.19
  273.5 0.8 broadcast_in_dim_reshape.4.refs_4_
  274.2 113.2 %mix.1 = (f32[64,2176]{1,0:T(8,128)}, f32[64,2048]{1,0:T(8,128)}, bf16[264,2048]{1,0:T(8,128)(2,1)}) custom-call(bf16[8,256,256]{2,1,0:T(8,128)(2,1)} %get-tuple-element.68.refs_0_, bf16[8,256,2048]{2,1,0:T(8,128)(2,1)} %bitcast.56, bf16[8,256,2048]{2,1,0:T(8,128)(2,1)} %bitcast.57, f32[8,256,1]{2,1,0:T(8,128)} %bitcast.60, ...), custom_call_target="tpu_custom_call" | custom-call | tf_op jit(solution)/shard_map/mix/pallas_call | solution.py:1456
  387.5 130.3 %back.1 = (bf16[256,2048]{1,0:T(8,128)(2,1)}, bf16[256,2048]{1,0:T(8,128)(2,1)}, f32[512,256]{1,0:T(8,128)}, f32[192,768]{1,0:T(8,128)}, f32[64,1024]{1,0:T(8,12...) custom-call(f32[64,2176]{1,0:T(8,128)} %get-tuple-element.76.refs_0_, ...), custom_call_target="tpu_custom_call" | custom-call | tf_op jit(solution)/shard_map/back/pallas_call | solution.py:2056
  517.8 0.0 copy-start.5
  517.8 0.0 copy-start
  517.8 1.4 fusion.13
  519.2 2.5 convert_element_type.47
  521.6 1.3 slice.25
  522.9 0.0 copy-done.5
  522.9 0.9 convert_bitcast_fusion.1
  523.8 1.2 slice_bitcast_fusion
  525.0 0.0 copy-done
  525.0 0.2 convert_bitcast_fusion
  525.1 0.0 copy-start.2
  525.1 0.0 copy-start.1
  525.1 1.4 fusion.12
  526.5 0.0 copy-start.3
  526.5 0.4 copy-done.2
  526.9 0.0 copy-start.6
  526.9 1.0 copy.64
  527.9 0.0 copy-done.1
  527.9 0.0 copy-start.4
  527.9 0.0 copy-start.7
  527.9 1.0 copy.65
  528.9 0.0 copy-done.3
  528.9 0.8 copy.66
  529.7 0.0 copy-done.6
  529.7 0.7 copy.67
  530.4 0.0 copy-done.4
  530.4 0.8 copy.68
  531.2 0.0 copy-done.7
  531.2 0.6 copy.69
  (6 shorter events, 0.0 us)
Async XLA Ops:
  0.7 7.5 %copy-start.8 = (s32[256,6]{0,1:T(8,128)S(1)}, s32[256,6]{0,1:T(8,128)}, u32[]{:S(2)}) copy-start(s32[256,6]{0,1:T(8,128)} %param.38) | copy-start | bytes 18436
  0.7 8.3 %copy-start.9 = (s32[1,3]{1,0:T(1,128)S(1)}, s32[1,3]{1,0:T(1,128)}, u32[]{:S(2)}) copy-start(s32[1,3]{1,0:T(1,128)} %param.37) | copy-start | bytes 40
  517.8 5.1 copy-start.5
  517.8 7.2 %copy-start = (bf16[8,264,256]{2,1,0:T(8,128)(2,1)S(1)}, bf16[8,264,256]{2,1,0:T(8,128)(2,1)}, u32[]{:S(2)}) copy-start(bf16[8,264,256]{2,1,0:T(8,128)(2,1)} %get-tuple-element.106) | copy-start | bytes 3244036
  525.1 1.8 copy-start.2
  525.1 2.8 copy-start.1
  526.5 2.3 copy-start.3
  526.9 2.8 copy-start.6
  527.9 2.5 copy-start.4
  527.9 3.3 copy-start.7

commit v5 on v4

--- a/solution.py
+++ b/solution.py
@@ -2146,10 +2146,10 @@
     all_gains = (attention_gain, ffn_gain, query_gain, latent_gain)
     gain_sizes = [g.shape[0] for g in all_gains]
     gain_wide = -(-max(gain_sizes) // LANES) * LANES
-    gains = jnp.stack(
-        [jnp.pad(g.astype(jnp.float32), (0, gain_wide - g.shape[0])) for g in all_gains]
-    )
-    gains = jnp.pad(gains, ((0, 8 - len(all_gains)), (0, 0)))
+    gains = sum(
+        jnp.pad(g.astype(jnp.float32)[None], ((i, 7 - i), (0, gain_wide - g.shape[0])))
+        for i, g in enumerate(all_gains)
+    )
     routes_pad = jnp.pad(routes.T, ((0, -top % 8), (0, 0)), constant_values=-1)
     shared = jnp.stack([shared_gate.T, shared_up.T, shared_down])
     shared_units = shared.shape[1] // groups

time: 533 us -> 533 us (level)
  no operation moved by 1% of the time
where the time goes in v5:
time: 533 us; the launch traced here: 532 us
  Pallas kernels  505 us (95%)
  local copies, waits for them, and re-layouts  15.5 us (3%)
  other arithmetic  10.2 us (2%)
    pallas_call x1, Pallas kernels, front_stage(): pl.pallas_call(functools.partial(front_kernel, groups, tuple(sizes), tupl...  191 us
    pallas_call x1, Pallas kernels, back_stage(): pl.pallas_call(functools.partial(back_kernel, groups, tuple(sizes), tuple...  130 us
    pallas_call x1, Pallas kernels, mix_stage(): pl.pallas_call(functools.partial(mix_kernel, groups, tuple(chunks), tuple...  113 us
    pallas_call x1, Pallas kernels, expert_stage(): pl.pallas_call(expert_kernel, grid=(local, blocks // step), in_specs=[row...  54.3 us
    pallas_call x1, Pallas kernels, route_stage(): pl.pallas_call(route_kernel, grid=(groups,), in_specs=[pl.BlockSpec((loca...  16.9 us

profile of v5, /device:TPU:0, one launch (start us, length us, event | category | flops | bytes accessed | tf_op | source)
XLA Modules:
  0.0 531.8 jit_solution(7881398834455641963)
XLA Ops:
  0.7 0.0 copy-start.8
  0.7 0.0 copy-start.9
  0.7 0.6 iota_add_fusion.ids_ref
  1.3 0.7 broadcast_in_dim.47
  1.9 0.7 broadcast_in_dim.46
  2.6 0.7 broadcast_in_dim.45
  3.3 1.3 convert_add_fusion.refs_0_
  4.5 1.3 pad.47.refs_7_
  5.8 2.3 pad_maximum_fusion
  8.1 0.0 copy-done.8
  8.1 0.8 copy.56.refs_11_
  8.9 0.0 copy-done.9
  8.9 0.2 reduce-window.4
  9.1 0.1 convert_reduce_fusion
  9.2 0.8 fusion.1.refs_12_.refs_7_
  10.0 0.1 select_reduce_fusion
  10.1 0.5 fusion.2
  10.6 0.8 select_maximum_fusion
  11.5 190.7 %front.1 = (f32[64,256]{1,0:T(8,128)}, bf16[2048,384]{1,0:T(8,128)(2,1)}, bf16[144,2048]{1,0:T(8,128)(2,1)}, bf16[1536,768]{1,0:T(8,128)(2,1)}, bf16[512,1024]{1...) custom-call(f32[8,256]{1,0:T(8,128)} %convert_add_fusion.refs_0_, ...), custom_call_target="tpu_custom_call" | custom-call | tf_op jit(solution)/shard_map/front/pallas_call | solution.py:1079
  202.2 16.9 %route.1 = (bf16[8,256,2048]{2,1,0:T(8,128)(2,1)}, bf16[8,256,2048]{2,1,0:T(8,128)(2,1)}, bf16[8,256,256]{2,1,0:T(8,128)(2,1)}, f32[8,256,1]{2,1,0:T(8,128)}) custom-call(s32[8,1]{1,0:T(8,128)} %iota_add_fusion.ids_ref, s32[8,2048]{1,0:T(8,128)} %get-tuple-element.64.routes_ref, bf16[2048,2048]{1,0:T(8,128)(2,1)} %get-tuple-element.65.x_ref.refs_5_, ...), custom_call_target="tpu_custom_call" | custom-call | tf_op jit(solution)/shard_map/route/pallas_call | solution.py:1224
  219.1 54.3 %experts.1 = (bf16[8,8,32,2048]{3,2,1,0:T(8,128)(2,1)}, bf16[8,8,32,2048]{3,2,1,0:T(8,128)(2,1)}, f32[8,8,32,1]{3,2,1,0:T(8,128)}, f32[8,352,2048]{2,1,0:T(8,128...) custom-call(bf16[8,8,32,2048]{3,2,1,0:T(8,128)(2,1)} %bitcast.78, bf16[8,8,32,2048]{3,2,1,0:T(8,128)(2,1)} %bitcast.79, ...), custom_call_target="tpu_custom_call" | custom-call | flops 26575110144 | bytes 137363456 | tf_op jit(solution)/shard_map/experts/pallas_call | solution.py:145
  273.4 0.1 broadcast_in_dim.52
  273.4 0.8 broadcast_in_dim_reshape.4.refs_4_
  274.2 113.2 %mix.1 = (f32[64,2176]{1,0:T(8,128)}, f32[64,2048]{1,0:T(8,128)}, bf16[264,2048]{1,0:T(8,128)(2,1)}) custom-call(bf16[8,256,256]{2,1,0:T(8,128)(2,1)} %get-tuple-element.68.refs_0_, bf16[8,256,2048]{2,1,0:T(8,128)(2,1)} %bitcast.57, bf16[8,256,2048]{2,1,0:T(8,128)(2,1)} %bitcast.58, f32[8,256,1]{2,1,0:T(8,128)} %bitcast.61, ...), custom_call_target="tpu_custom_call" | custom-call | tf_op jit(solution)/shard_map/mix/pallas_call | solution.py:1456
  387.4 130.3 %back.1 = (bf16[256,2048]{1,0:T(8,128)(2,1)}, bf16[256,2048]{1,0:T(8,128)(2,1)}, f32[512,256]{1,0:T(8,128)}, f32[192,768]{1,0:T(8,128)}, f32[64,1024]{1,0:T(8,12...) custom-call(f32[64,2176]{1,0:T(8,128)} %get-tuple-element.76.refs_0_, ...), custom_call_target="tpu_custom_call" | custom-call | tf_op jit(solution)/shard_map/back/pallas_call | solution.py:2056
  517.8 0.0 copy-start.5
  517.8 0.0 copy-start
  517.8 1.4 fusion.5
  519.2 2.5 convert_element_type.49
  521.6 1.3 slice.25
  522.9 0.0 copy-done.5
  522.9 0.9 convert_bitcast_fusion.1
  523.7 1.2 slice_bitcast_fusion
  524.9 0.0 copy-done
  524.9 0.2 convert_bitcast_fusion
  525.1 0.0 copy-start.2
  525.1 0.0 copy-start.1
  525.1 1.4 fusion.4
  526.5 0.0 copy-start.3
  526.5 0.4 copy-done.2
  526.9 0.0 copy-start.6
  526.9 1.0 copy.64
  527.9 0.0 copy-done.1
  527.9 0.0 copy-start.4
  527.9 0.0 copy-start.7
  527.9 1.0 copy.65
  528.8 0.0 copy-done.3
  528.9 0.8 copy.66
  529.7 0.0 copy-done.6
  529.7 0.7 copy.67
  530.4 0.0 copy-done.4
  530.4 0.8 copy.68
  531.2 0.0 copy-done.7
  531.2 0.6 copy.69
  (4 shorter events, 0.0 us)
Async XLA Ops:
  0.7 7.5 %copy-start.8 = (s32[256,6]{0,1:T(8,128)S(1)}, s32[256,6]{0,1:T(8,128)}, u32[]{:S(2)}) copy-start(s32[256,6]{0,1:T(8,128)} %param.38) | copy-start | bytes 18436
  0.7 8.2 %copy-start.9 = (s32[1,3]{1,0:T(1,128)S(1)}, s32[1,3]{1,0:T(1,128)}, u32[]{:S(2)}) copy-start(s32[1,3]{1,0:T(1,128)} %param.37) | copy-start | bytes 40
  517.8 5.1 copy-start.5
  517.8 7.2 %copy-start = (bf16[8,264,256]{2,1,0:T(8,128)(2,1)S(1)}, bf16[8,264,256]{2,1,0:T(8,128)(2,1)}, u32[]{:S(2)}) copy-start(bf16[8,264,256]{2,1,0:T(8,128)(2,1)} %get-tuple-element.106) | copy-start | bytes 3244036
  525.1 1.8 copy-start.2
  525.1 2.8 copy-start.1
  526.5 2.3 copy-start.3
  526.9 2.8 copy-start.6
  527.9 2.5 copy-start.4
  527.9 3.3 copy-start.7
